TPU v7x, 32 devices: a whole 2x2x4 slice. The times are simulated.
32 devices in a mesh: head: 4 (over y, core), blk: 8 (over z, x).
Axes of the slice: x: 2, y: 2, z: 4, core: 2. Of those that a mesh axis runs over, the one named last changes fastest.
Arguments:
- block_input: bfloat16 [4096, 1024], P(('head', 'blk')), may hold values from -6 to 6
- span_order: int32 [32], replicated, may hold values from 0 to 31, each once
- norm1_gain: bfloat16 [1024], P(('head', 'blk')), may hold values from 0.099609375 to 1.8984375
- w_query: bfloat16 [1024, 1024], P(('head', 'blk')), may hold values from -0.1875 to 0.1875
- key_weight: bfloat16 [1024, 512], P(('head', 'blk')), may hold values from -0.1875 to 0.1875
- value_weight: bfloat16 [1024, 512], P(('head', 'blk')), may hold values from -0.1875 to 0.1875
- qk_gain: float32 [2, 64], replicated, may hold values from 0.5 to 3, as said below
- w_out: bfloat16 [1024, 1024], P(('head', 'blk')), may hold values from -6 to 6
- norm2_gain: bfloat16 [1024], P(('head', 'blk')), may hold values from 0.099609375 to 1.8984375
- w_gate: bfloat16 [1024, 4608], P(('head', 'blk')), may hold values from -0.1875 to 0.1875
- w_up: bfloat16 [1024, 4608], P(('head', 'blk')), may hold values from -0.1875 to 0.1875
- w_down: bfloat16 [4608, 1024], P(('head', 'blk')), may hold values from -0.09375 to 0.09375
- out_grad: bfloat16 [4096, 1024], P(('head', 'blk')), may hold values from -6 to 6
Outputs:
- block_output: bfloat16 [4096, 1024], P(('head', 'blk'))
- input_grad: bfloat16 [4096, 1024], P(('head', 'blk'))
- norm1_grad: float32 [1024], P(('head', 'blk'))
- query_grad: float32 [1024, 1024], P(('head', 'blk'))
- key_grad: float32 [1024, 512], P(('head', 'blk'))
- value_grad: float32 [1024, 512], P(('head', 'blk'))
- qk_gain_grad: float32 [2, 64], replicated
- out_proj_grad: float32 [1024, 1024], P(('head', 'blk'))
- norm2_grad: float32 [1024], P(('head', 'blk'))
- gate_grad: float32 [1024, 4608], P(('head', 'blk'))
- up_grad: float32 [1024, 4608], P(('head', 'blk'))
- down_grad: float32 [4608, 1024], P(('head', 'blk'))
Inputs may be any that keep to these rules, and one draw needn't show every extreme that they name: Storage span c of 128 rows holds the sequence positions from span_order[c] * 128 on; every span place occurs once. `qk_gain`: positive gains.
All inputs are finite; a program needn't handle non-finite values.
Results may differ from a plain program's by a relative error of at most 0.02.
The roundings to bfloat16 on the way count: a program that leaves them out, or rounds other values in their place, can miss the bound.
Values may be sent and summed in bfloat16 or wider, within the bound.
A program may use at most 512 MiB of HBM per device.

v0:
```python
import math

import jax
import jax.numpy as jnp
from jax import lax
from jax.sharding import PartitionSpec as P

EPS = 1e-05
THETA = 1000000.0
NEG = -1e30


def rms_norm(values, gain_vec):
    inverse = lax.rsqrt(jnp.mean(values * values, axis=-1, keepdims=True) + EPS)
    return values * inverse * gain_vec


def rotate(field_in, where_at):
    half_size = field_in.shape[-1] // 2
    frequency = jnp.exp(
        jnp.arange(half_size, dtype=jnp.float32)
        * jnp.float32(-2.0 * math.log(THETA) / field_in.shape[-1])
    )
    angles = where_at.astype(jnp.float32)[:, None] * frequency[None, :]
    cosine = jnp.cos(angles)[:, None, :]
    sine_part = jnp.sin(angles)[:, None, :]
    first_half = field_in[..., :half_size]
    second_half = field_in[..., half_size:]
    return jnp.concatenate(
        [
            first_half * cosine - second_half * sine_part,
            second_half * cosine + first_half * sine_part,
        ],
        axis=-1,
    )


def head_map(raw_rows, gain_vec, where_at):
    row_count = raw_rows.shape[0]
    shaped = raw_rows.reshape(row_count, -1, gain_vec.shape[0])
    return rotate(rms_norm(shaped, gain_vec), where_at).reshape(row_count, -1)


def lookup(span_ids, order_table):
    matches = span_ids[:, None] == jnp.arange(order_table.shape[0], dtype=jnp.int32)[None, :]
    return jnp.sum(jnp.where(matches, order_table[None, :], 0), axis=1)


def positions(row_ids, tok_rows, blocks, group_rows, order_table):
    span_ids = row_ids % group_rows // tok_rows * blocks + row_ids // group_rows
    return lookup(span_ids, order_table) * tok_rows + row_ids % tok_rows


def local(
    block_input,
    span_order,
    norm1_gain,
    w_query,
    key_weight,
    value_weight,
    qk_gain,
    w_out,
    norm2_gain,
    w_gate,
    w_up,
    w_down,
    out_grad,
):
    blocks = lax.axis_size("blk")
    groups = lax.axis_size("head")
    tok_rows = block_input.shape[0]
    group_rows = groups * tok_rows
    head_size = qk_gain.shape[1]
    kv_total = key_weight.shape[1] // head_size
    kv_local = kv_total // groups
    share_count = w_query.shape[1] // key_weight.shape[1]
    score_scale = float(head_size) ** (-0.5)
    blk_index = lax.axis_index("blk")
    head_index = lax.axis_index("head")
    own_rows = (
        blk_index * group_rows + head_index * tok_rows + jnp.arange(tok_rows, dtype=jnp.int32)
    )
    tok_where = positions(own_rows, tok_rows, blocks, group_rows, span_order)
    query_where = positions(
        blk_index * group_rows + jnp.arange(group_rows, dtype=jnp.int32),
        tok_rows,
        blocks,
        group_rows,
        span_order,
    )
    gathered = (
        lax.all_gather(norm1_gain, ("head", "blk"), axis=0, tiled=True),
        lax.all_gather(w_query, ("head", "blk"), axis=0, tiled=True),
        lax.all_gather(key_weight, ("head", "blk"), axis=0, tiled=True),
        lax.all_gather(value_weight, ("head", "blk"), axis=0, tiled=True),
        lax.all_gather(w_out, ("head", "blk"), axis=0, tiled=True),
        lax.all_gather(norm2_gain, ("head", "blk"), axis=0, tiled=True),
        lax.all_gather(w_gate, ("head", "blk"), axis=0, tiled=True),
        lax.all_gather(w_up, ("head", "blk"), axis=0, tiled=True),
        lax.all_gather(w_down, ("head", "blk"), axis=0, tiled=True),
    )
    (
        gain_one,
        query_full,
        key_full,
        value_full,
        out_full,
        gain_two,
        gate_full,
        up_full,
        down_full,
    ) = gathered
    gain_one = gain_one.astype(jnp.float32)
    gain_two = gain_two.astype(jnp.float32)
    in_flat = block_input.astype(jnp.float32)
    normed = rms_norm(in_flat, gain_one).astype(jnp.bfloat16)
    q_raw = jnp.dot(normed, query_full, preferred_element_type=jnp.float32)
    k_raw = jnp.dot(normed, key_full, preferred_element_type=jnp.float32)
    v_raw = jnp.dot(normed, value_full, preferred_element_type=jnp.float32)

    def query_map(raw_rows, gain_vec):
        return head_map(raw_rows, gain_vec, tok_where)

    queries = query_map(q_raw, qk_gain[0]).astype(jnp.bfloat16)
    keys = query_map(k_raw, qk_gain[1]).astype(jnp.bfloat16)
    values = v_raw.astype(jnp.bfloat16)
    q_heads, k_heads, v_heads = (
        lax.all_to_all(queries, "head", split_axis=1, concat_axis=0, tiled=True),
        lax.all_to_all(keys, "head", split_axis=1, concat_axis=0, tiled=True),
        lax.all_to_all(values, "head", split_axis=1, concat_axis=0, tiled=True),
    )
    q_four = q_heads.reshape(group_rows, kv_local, share_count, head_size)

    def key_where(row_count):
        return positions(
            jnp.arange(row_count, dtype=jnp.int32), tok_rows, blocks, group_rows, span_order
        )

    start_state = (
        jnp.full((kv_local, share_count, group_rows), NEG, jnp.float32),
        jnp.zeros((kv_local, share_count, group_rows), jnp.float32),
        jnp.zeros((group_rows, kv_local, share_count, head_size), jnp.float32),
    )
    key_piece = lax.all_gather(k_heads, "blk", axis=0, tiled=True)
    value_piece = lax.all_gather(v_heads, "blk", axis=0, tiled=True)
    row_count = key_piece.shape[0]
    key_three = key_piece.reshape(row_count, kv_local, head_size)
    value_three = value_piece.reshape(row_count, kv_local, head_size)
    causal = key_where(row_count)[None, :] <= query_where[:, None]

    def update(held_state):
        row_max, row_sum, accumulated = held_state
        scores = (
            jnp.einsum("qkgd,nkd->kgqn", q_four, key_three, preferred_element_type=jnp.float32)
            * score_scale
        )
        scores = jnp.where(causal, scores, NEG)
        new_max = jnp.maximum(row_max, jnp.max(scores, axis=-1))
        weights = jnp.where(causal, jnp.exp(scores - new_max[..., None]), 0.0)
        row_sum = jnp.sum(weights, axis=-1)
        value_part = jnp.einsum(
            "kgqn,nkd->qkgd",
            weights.astype(jnp.bfloat16),
            value_three,
            preferred_element_type=jnp.float32,
        )
        accumulated = value_part
        return (new_max, row_sum, accumulated)

    row_max, row_sum, accumulated = update(start_state)
    attended_heads = (accumulated / row_sum.transpose(2, 0, 1)[..., None]).astype(jnp.bfloat16)
    log_total = row_max + jnp.log(row_sum)
    attended = lax.all_to_all(
        attended_heads.reshape(group_rows, -1), "head", split_axis=0, concat_axis=1, tiled=True
    )
    middle = in_flat + jnp.dot(attended, out_full, preferred_element_type=jnp.float32)
    normed2 = rms_norm(middle, gain_two).astype(jnp.bfloat16)
    gate_rows = jnp.dot(normed2, gate_full, preferred_element_type=jnp.float32)
    up_rows = jnp.dot(normed2, up_full, preferred_element_type=jnp.float32)
    hidden = (jax.nn.silu(gate_rows) * up_rows).astype(jnp.bfloat16)
    block_output = (middle + jnp.dot(hidden, down_full, preferred_element_type=jnp.float32)).astype(
        jnp.bfloat16
    )
    gathered = (
        lax.all_gather(norm1_gain, ("head", "blk"), axis=0, tiled=True),
        lax.all_gather(w_query, ("head", "blk"), axis=0, tiled=True),
        lax.all_gather(key_weight, ("head", "blk"), axis=0, tiled=True),
        lax.all_gather(value_weight, ("head", "blk"), axis=0, tiled=True),
        lax.all_gather(w_out, ("head", "blk"), axis=0, tiled=True),
        lax.all_gather(norm2_gain, ("head", "blk"), axis=0, tiled=True),
        lax.all_gather(w_gate, ("head", "blk"), axis=0, tiled=True),
        lax.all_gather(w_up, ("head", "blk"), axis=0, tiled=True),
        lax.all_gather(w_down, ("head", "blk"), axis=0, tiled=True),
    )
    (
        gain_one,
        query_full,
        key_full,
        value_full,
        out_full,
        gain_two,
        gate_full,
        up_full,
        down_full,
    ) = gathered
    gain_one = gain_one.astype(jnp.float32)
    gain_two = gain_two.astype(jnp.float32)
    dhidden = jnp.dot(out_grad, down_full.T, preferred_element_type=jnp.float32)
    down_grad = jnp.dot(hidden.T, out_grad, preferred_element_type=jnp.float32)
    _, gate_back = jax.vjp(lambda gate_in, up_in: jax.nn.silu(gate_in) * up_in, gate_rows, up_rows)
    dgate, dup = gate_back(dhidden)
    dgate = dgate.astype(jnp.bfloat16)
    dup = dup.astype(jnp.bfloat16)
    dnormed2 = jnp.dot(dgate, gate_full.T, preferred_element_type=jnp.float32) + jnp.dot(
        dup, up_full.T, preferred_element_type=jnp.float32
    )
    gate_grad = jnp.dot(normed2.T, dgate, preferred_element_type=jnp.float32)
    up_grad = jnp.dot(normed2.T, dup, preferred_element_type=jnp.float32)
    _, norm2_back = jax.vjp(rms_norm, middle, gain_two)
    dmiddle_norm, norm2_grad = norm2_back(dnormed2)
    dmiddle = out_grad.astype(jnp.float32) + dmiddle_norm
    dmiddle_b = dmiddle.astype(jnp.bfloat16)
    out_proj_grad = jnp.dot(attended.T, dmiddle_b, preferred_element_type=jnp.float32)
    dattended = jnp.dot(dmiddle_b, out_full.T, preferred_element_type=jnp.float32).astype(
        jnp.bfloat16
    )
    grad_heads = lax.all_to_all(dattended, "head", split_axis=1, concat_axis=0, tiled=True)
    grad_four = grad_heads.reshape(group_rows, kv_local, share_count, head_size)
    delta_rows = jnp.sum(
        grad_four.astype(jnp.float32) * attended_heads.astype(jnp.float32), axis=-1
    ).transpose(1, 2, 0)
    back_state = (
        jnp.zeros((group_rows, kv_local, share_count, head_size), jnp.float32),
        jnp.zeros((blocks * group_rows, kv_local * head_size), jnp.float32),
        jnp.zeros((blocks * group_rows, kv_local * head_size), jnp.float32),
    )
    key_piece = lax.all_gather(k_heads, "blk", axis=0, tiled=True)
    value_piece = lax.all_gather(v_heads, "blk", axis=0, tiled=True)
    row_count = key_piece.shape[0]
    collect_key_three = key_piece.reshape(row_count, kv_local, head_size)
    collect_value_three = value_piece.reshape(row_count, kv_local, head_size)
    collect_causal = key_where(row_count)[None, :] <= query_where[:, None]

    def update(held_state):
        scores = (
            jnp.einsum(
                "qkgd,nkd->kgqn", q_four, collect_key_three, preferred_element_type=jnp.float32
            )
            * score_scale
        )
        scores = jnp.where(collect_causal, scores, NEG)
        prob_rows = jnp.where(collect_causal, jnp.exp(scores - log_total[..., None]), 0.0)
        value_part = jnp.einsum(
            "kgqn,qkgd->nkd",
            prob_rows.astype(jnp.bfloat16),
            grad_four,
            preferred_element_type=jnp.float32,
        )
        dprob = jnp.einsum(
            "qkgd,nkd->kgqn", grad_four, collect_value_three, preferred_element_type=jnp.float32
        )
        dscore = (prob_rows * (dprob - delta_rows[..., None])).astype(jnp.bfloat16)
        query_acc = (
            jnp.einsum(
                "kgqn,nkd->qkgd", dscore, collect_key_three, preferred_element_type=jnp.float32
            )
            * score_scale
        )
        key_part = (
            jnp.einsum("kgqn,qkgd->nkd", dscore, q_four, preferred_element_type=jnp.float32)
            * score_scale
        )
        key_acc = key_part.reshape(row_count, -1)
        value_acc = value_part.reshape(row_count, -1)
        return (query_acc, key_acc, value_acc)

    query_acc, key_acc, value_acc = update(back_state)
    key_sums, value_sums = (
        lax.psum_scatter(
            key_acc.astype(jnp.bfloat16), "blk", scatter_dimension=0, tiled=True
        ).astype(jnp.float32),
        lax.psum_scatter(
            value_acc.astype(jnp.bfloat16), "blk", scatter_dimension=0, tiled=True
        ).astype(jnp.float32),
    )
    dqueries, dkeys, dvalues = (
        lax.all_to_all(
            query_acc.reshape(group_rows, -1).astype(jnp.bfloat16),
            "head",
            split_axis=0,
            concat_axis=1,
            tiled=True,
        ),
        lax.all_to_all(
            key_sums.astype(jnp.bfloat16), "head", split_axis=0, concat_axis=1, tiled=True
        ),
        lax.all_to_all(
            value_sums.astype(jnp.bfloat16), "head", split_axis=0, concat_axis=1, tiled=True
        ),
    )
    _, query_back = jax.vjp(query_map, q_raw, qk_gain[0])
    dq_raw, qgain_grad = query_back(dqueries.astype(jnp.float32))
    _, key_back = jax.vjp(query_map, k_raw, qk_gain[1])
    dk_raw, kgain_grad = key_back(dkeys.astype(jnp.float32))
    dq_raw = dq_raw.astype(jnp.bfloat16)
    dk_raw = dk_raw.astype(jnp.bfloat16)
    dnormed = jnp.dot(dq_raw, query_full.T, preferred_element_type=jnp.float32)
    dnormed = dnormed + jnp.dot(dk_raw, key_full.T, preferred_element_type=jnp.float32)
    dnormed = dnormed + jnp.dot(dvalues, value_full.T, preferred_element_type=jnp.float32)
    query_grad = jnp.dot(normed.T, dq_raw, preferred_element_type=jnp.float32)
    key_grad = jnp.dot(normed.T, dk_raw, preferred_element_type=jnp.float32)
    value_grad = jnp.dot(normed.T, dvalues, preferred_element_type=jnp.float32)
    _, norm1_back = jax.vjp(rms_norm, in_flat, gain_one)
    dinput_norm, norm1_grad = norm1_back(dnormed)
    input_grad = (dmiddle + dinput_norm).astype(jnp.bfloat16)
    summed = (
        lax.psum_scatter(norm1_grad, ("head", "blk"), scatter_dimension=0, tiled=True),
        lax.psum_scatter(query_grad, ("head", "blk"), scatter_dimension=0, tiled=True),
        lax.psum_scatter(key_grad, ("head", "blk"), scatter_dimension=0, tiled=True),
        lax.psum_scatter(value_grad, ("head", "blk"), scatter_dimension=0, tiled=True),
        lax.psum_scatter(out_proj_grad, ("head", "blk"), scatter_dimension=0, tiled=True),
        lax.psum_scatter(norm2_grad, ("head", "blk"), scatter_dimension=0, tiled=True),
        lax.psum_scatter(gate_grad, ("head", "blk"), scatter_dimension=0, tiled=True),
        lax.psum_scatter(up_grad, ("head", "blk"), scatter_dimension=0, tiled=True),
        lax.psum_scatter(down_grad, ("head", "blk"), scatter_dimension=0, tiled=True),
    )
    qk_gain_grad = lax.psum(jnp.stack([qgain_grad, kgain_grad]), ("head", "blk"))
    return (
        block_output,
        input_grad,
        summed[0],
        summed[1],
        summed[2],
        summed[3],
        qk_gain_grad,
        summed[4],
        summed[5],
        summed[6],
        summed[7],
        summed[8],
    )


def solution(mesh):
    in_specs = (
        P(("head", "blk"), None),
        P(),
        P(("head", "blk")),
        P(("head", "blk"), None),
        P(("head", "blk"), None),
        P(("head", "blk"), None),
        P(),
        P(("head", "blk"), None),
        P(("head", "blk")),
        P(("head", "blk"), None),
        P(("head", "blk"), None),
        P(("head", "blk"), None),
        P(("head", "blk"), None),
    )
    out_specs = (
        P(("head", "blk"), None),
        P(("head", "blk"), None),
        P(("head", "blk")),
        P(("head", "blk"), None),
        P(("head", "blk"), None),
        P(("head", "blk"), None),
        P(),
        P(("head", "blk"), None),
        P(("head", "blk")),
        P(("head", "blk"), None),
        P(("head", "blk"), None),
        P(("head", "blk"), None),
    )
    return jax.shard_map(local, mesh=mesh, in_specs=in_specs, out_specs=out_specs, check_vma=False)
```

profile of v0, /device:TPU:0, one launch (start us, length us, event | category | flops | bytes accessed | tf_op | source)
XLA Modules:
  0.0 1970.0 jit_solution(9084363389160186047)
XLA Ops:
  11.1 42.0 %all-reduce.9 = (bf16[1024]{0:T(1024)(128)(2,1)S(1)}, bf16[1024]{0:T(1024)(128)(2,1)S(1)}) all-reduce(bf16[1024]{0:T(1024)(128)(2,1)S(1)} %dynamic-update-slice, bf16[1024]{0:T(1024)(128)(2,1)S(1)} %dynamic-update-slice.1), channel_id=1, replica_groups=mesh['head'=4,'blk'=8] {'head','blk'}, use_global_device_ids=true, to_apply=%add.4 | all-reduce | flops 2048 | bytes 8192
  54.9 12.6 all-gather.10.cloned.1.call-done
  69.9 3.3 all-to-all-start
  73.3 4.5 all-to-all-done
  79.5 43.9 %all-gather.14.cloned.1.call-done = bf16[1024,512]{1,0:T(8,128)(2,1)} async-done(((bf16[32,512]{1,0:T(8,128)(2,1)}), bf16[1024,512]{1,0:T(8,128)(2,1)}) %all-gather.14.cloned.1.call-update) | async-done | bytes 1048592 | tf_op jit(solution)/shard_map/all_gather | solution.py:94
  126.1 7.1 all_to_all.125
  138.5 43.2 %all-gather.18.cloned.1.call-done = bf16[1024,1024]{1,0:T(8,128)(2,1)} async-done(((bf16[32,1024]{1,0:T(8,128)(2,1)}), bf16[1024,1024]{1,0:T(8,128)(2,1)}) %all-gather.18.cloned.1.call-update) | async-done | bytes 2097168 | tf_op jit(solution)/shard_map/all_gather | solution.py:93
  185.4 3.6 all-to-all-start.2
  191.3 32.1 %all-gather.12.cloned.1.call-done = bf16[4096,128]{1,0:T(8,128)(2,1)} async-done(((bf16[512,128]{1,0:T(8,128)(2,1)}), bf16[4096,128]{1,0:T(8,128)(2,1)}) %all-gather.12.cloned.1.call-update) | async-done | bytes 1048592 | tf_op jit(solution)/shard_map/all_gather | solution.py:145
  225.7 39.3 %all-gather.16.cloned.1.call-done = bf16[4096,128]{1,0:T(8,128)(2,1)} async-done(((bf16[512,128]{1,0:T(8,128)(2,1)}), bf16[4096,128]{1,0:T(8,128)(2,1)}) %all-gather.16.cloned.1.call-update) | async-done | bytes 1048592 | tf_op jit(solution)/shard_map/all_gather | solution.py:144
  266.9 15.1 fusion.5
  282.1 15.2 fusion.2
  297.3 15.4 fusion.34
  313.6 3.6 all-to-all-start.3
  317.2 5.8 all-gather.20.cloned.1.call-done
  325.5 80.8 %all-gather.24.cloned.1.call-done = bf16[1024,4608]{1,0:T(8,128)(2,1)} async-done(((bf16[32,4608]{1,0:T(8,128)(2,1)}), bf16[1024,4608]{1,0:T(8,128)(2,1)}) %all-gather.24.cloned.1.call-update) | async-done | bytes 9437200 | tf_op jit(solution)/shard_map/all_gather | solution.py:99
  406.3 6.5 fusion.101
  412.9 76.5 %all-gather.22.cloned.1.call-done = bf16[1024,4608]{1,0:T(8,128)(2,1)} async-done(((bf16[32,4608]{1,0:T(8,128)(2,1)}), bf16[1024,4608]{1,0:T(8,128)(2,1)}) %all-gather.22.cloned.1.call-update) | async-done | bytes 9437200 | tf_op jit(solution)/shard_map/all_gather | solution.py:98
  489.4 6.5 fusion.100
  495.9 76.5 %all-gather.26.cloned.1.call-done = bf16[4608,1024]{1,0:T(8,128)(2,1)} async-done(((bf16[144,1024]{1,0:T(8,128)(2,1)}), bf16[4608,1024]{1,0:T(8,128)(2,1)}) %all-gather.26.cloned.1.call-update) | async-done | bytes 9437200 | tf_op jit(solution)/shard_map/all_gather | solution.py:100
  572.4 9.0 multiply_convert_fusion
  581.5 3.1 fusion.102
  584.6 7.6 multiply_reduce_fusion
  594.8 3.4 all-to-all-start.4
  600.0 4.2 all-to-all-done.4
  607.9 15.8 fusion.16
  626.1 23.3 %fusion.1 = bf16[2,2,512,4096]{2,3,1,0:T(8,128)(2,1)} fusion(f32[2,4096,512,2]{2,1,3,0:T(8,128)} %get-tuple-element.45, f32[2,2,512]{2,1,0:T(2,128)} %bitcast.199, f32[2,2,512]{2,1,0:T(2,128)} %log_add_fusion, pred[512,4096]{0,1:T(8,128)(4,1)} %broadcast_compare_fusion, bf16[4096,2,64,1]{0,2,3,1:T(8,128)(2,1)} %bitcast.184, ...), kind=kOutput, calls=%fused_computation.2 | convolution fusion | flops 1132462080 | bytes 53755904 | tf_op jit(solution)/shard_map/qkgd,nkd->kgqn/dot_general | solution.py:259
  649.4 12.0 fusion.19
  663.8 25.0 %reduce-scatter.12.cloned.1.call-done = bf16[512,128]{1,0:T(8,128)(2,1)} async-done(((bf16[4096,128]{1,0:T(8,128)(2,1)}), bf16[512,128]{1,0:T(8,128)(2,1)}) %reduce-scatter.12.cloned.1.call-update) | async-done | bytes 131088 | tf_op jit(solution)/shard_map/reduce_scatter | solution.py:282
  688.8 8.6 all_to_all.126
  702.0 53.6 %reduce-scatter.10.cloned.1.call-done = bf16[512,128]{1,0:T(8,128)(2,1)} async-done(((bf16[4096,128]{1,0:T(8,128)(2,1)}), bf16[512,128]{1,0:T(8,128)(2,1)}) %reduce-scatter.10.cloned.1.call-update) | async-done | bytes 131088 | tf_op jit(solution)/shard_map/reduce_scatter | solution.py:279
  755.5 7.9 all_to_all.127
  773.4 3.6 fusion.48
  777.2 9.1 fusion.29
  788.0 8.9 all_to_all.128
  800.4 3.4 fusion.93
  803.9 8.9 fusion.106
  812.8 9.2 fusion.105
  822.1 9.1 fusion.104
  831.3 5.9 fusion.27
  839.3 39.3 %all-reduce.8 = (f32[1024]{0:T(1024)S(1)}, f32[2,64]{1,0:T(2,128)}, f32[1024]{0:T(1024)S(1)}) all-reduce(f32[1024]{0:T(1024)S(1)} %get-tuple-element.14, f32[2,64]{1,0:T(2,128)S(1)} %pad_maximum_fusion.2, f32[1024]{0:T(1024)S(1)} %copy-done.36), channel_id=4, replica_groups=mesh['head'=4,'blk'=8] {'head','blk'}, use_global_device_ids=true, to_apply=%region_17.18.clone | all-reduce | flops 2176 | bytes 17408
  881.2 15.7 reduce-scatter.18.cloned.1.call-done
  896.9 139.0 %reduce-scatter.16.cloned.1.call-done = f32[32,512]{1,0:T(8,128)} async-done(((f32[1024,512]{1,0:T(8,128)}), f32[32,512]{1,0:T(8,128)}) %reduce-scatter.16.cloned.1.call-update) | async-done | bytes 65552 | tf_op jit(solution)/shard_map/reduce_scatter | solution.py:319
  1035.9 145.1 %reduce-scatter.20.cloned.1.call-done = f32[32,1024]{1,0:T(8,128)} async-done(((f32[1024,1024]{1,0:T(8,128)}), f32[32,1024]{1,0:T(8,128)}) %reduce-scatter.20.cloned.1.call-update) | async-done | bytes 131088 | tf_op jit(solution)/shard_map/reduce_scatter | solution.py:321
  1181.0 144.5 %reduce-scatter.14.cloned.1.call-done = f32[32,1024]{1,0:T(8,128)} async-done(((f32[1024,1024]{1,0:T(8,128)}), f32[32,1024]{1,0:T(8,128)}) %reduce-scatter.14.cloned.1.call-update) | async-done | bytes 131088 | tf_op jit(solution)/shard_map/reduce_scatter | solution.py:318
  1325.5 211.7 %reduce-scatter.26.cloned.1.call-done = f32[144,1024]{1,0:T(8,128)} async-done(((f32[4608,1024]{1,0:T(8,128)}), f32[144,1024]{1,0:T(8,128)}) %reduce-scatter.26.cloned.1.call-update) | async-done | bytes 589840 | tf_op jit(solution)/shard_map/reduce_scatter | solution.py:325
  1537.2 213.0 %reduce-scatter.24.cloned.1.call-done = f32[32,4608]{1,0:T(8,128)} async-done(((f32[1024,4608]{1,0:T(8,128)}), f32[32,4608]{1,0:T(8,128)}) %reduce-scatter.24.cloned.1.call-update) | async-done | bytes 589840 | tf_op jit(solution)/shard_map/reduce_scatter | solution.py:324
  1750.2 212.8 %reduce-scatter.22.cloned.1.call-done = f32[32,4608]{1,0:T(8,128)} async-done(((f32[1024,4608]{1,0:T(8,128)}), f32[32,4608]{1,0:T(8,128)}) %reduce-scatter.22.cloned.1.call-update) | async-done | bytes 589840 | tf_op jit(solution)/shard_map/reduce_scatter | solution.py:323
  (200 shorter events, 68.4 us)
Async XLA Ops:
  7.2 60.4 %all-gather.10.cloned.1.call-start = ((), (), s32[]{:S(2)}) async-start(), calls=%async_computation.17 | async-start | bytes 1081344 | tf_op jit(solution)/shard_map/all_gather | solution.py:95
  7.9 115.4 %all-gather.14.cloned.1.call-start = ((), (), s32[]{:S(2)}) async-start(), calls=%async_computation.19 | async-start | bytes 1081344 | tf_op jit(solution)/shard_map/all_gather | solution.py:94
  8.7 173.1 %all-gather.18.cloned.1.call-start = ((), (), s32[]{:S(2)}) async-start(), calls=%async_computation.21 | async-start | bytes 2162688 | tf_op jit(solution)/shard_map/all_gather | solution.py:93
  53.1 132.3 %copy-start.25 = (f32[1024]{0:T(1024)}, f32[1024]{0:T(1024)S(1)}, u32[]{:S(2)}) copy-start(f32[1024]{0:T(1024)S(1)} %convert_element_type.147) | copy-start | bytes 12292
  54.9 24.5 %copy-start.41 = (f32[128]{0:T(128)}, f32[128]{0:T(128)S(1)}, u32[]{:S(2)}) copy-start(f32[128]{0:T(128)S(1)} %fusion.45) | copy-start | bytes 1540
  54.9 211.6 %copy-start.33 = (f32[128]{0:T(128)}, f32[128]{0:T(128)S(1)}, u32[]{:S(2)}) copy-start(f32[128]{0:T(128)S(1)} %fusion.81) | copy-start | bytes 1540
  69.9 7.9 all-to-all-start
  73.2 150.2 %all-gather.12.cloned.1.call-start = ((), (), s32[]{:S(2)}) async-start(), calls=%async_computation.18 | async-start | bytes 1179648 | tf_op jit(solution)/shard_map/all_gather | solution.py:145
  78.5 186.5 %all-gather.16.cloned.1.call-start = ((), (), s32[]{:S(2)}) async-start(), calls=%async_computation.20 | async-start | bytes 1179648 | tf_op jit(solution)/shard_map/all_gather | solution.py:144
  79.3 187.2 %copy-start.37 = (f32[64]{0:T(128)}, f32[64]{0:T(128)S(1)}, u32[]{:S(2)}) copy-start(f32[64]{0:T(128)S(1)} %get-tuple-element.36) | copy-start | bytes 772
  79.3 187.2 %copy-start.38 = (f32[64]{0:T(128)}, f32[64]{0:T(128)S(1)}, u32[]{:S(2)}) copy-start(f32[64]{0:T(128)S(1)} %get-tuple-element.37) | copy-start | bytes 772
  79.5 105.9 %copy-start.24 = (f32[128,32]{0,1:T(8,128)}, f32[128,32]{0,1:T(8,128)S(1)}, u32[]{:S(2)}) copy-start(f32[128,32]{0,1:T(8,128)S(1)} %get-tuple-element.39) | copy-start | bytes 49156
  134.1 188.9 %all-gather.20.cloned.1.call-start = ((), (), s32[]{:S(2)}) async-start(), calls=%async_computation.22 | async-start | bytes 2162688 | tf_op jit(solution)/shard_map/all_gather | solution.py:96
  134.7 271.7 %all-gather.24.cloned.1.call-start = ((), (), s32[]{:S(2)}) async-start(), calls=%async_computation.24 | async-start | bytes 9732096 | tf_op jit(solution)/shard_map/all_gather | solution.py:99
  135.4 354.0 %all-gather.22.cloned.1.call-start = ((), (), s32[]{:S(2)}) async-start(), calls=%async_computation.23 | async-start | bytes 9732096 | tf_op jit(solution)/shard_map/all_gather | solution.py:98
  136.2 436.3 %all-gather.26.cloned.1.call-start = ((), (), s32[]{:S(2)}) async-start(), calls=%async_computation.25 | async-start | bytes 9732096 | tf_op jit(solution)/shard_map/all_gather | solution.py:100
  185.4 81.1 %all-to-all-start.2 = ((bf16[128,4,256]{0,2,1:T(8,128)(2,1)}), bf16[128,4,256]{0,2,1:T(8,128)(2,1)S(1)}, u32[]{:S(2)}, u32[]{:S(2)}) async-start(bf16[128,4,256]{0,2,1:T(8,128)(2,1)} %bitcast.15), calls=%async_computation.2 | async-start | bytes 524288 | tf_op jit(solution)/shard_map/all_to_all | solution.py:128
  266.5 15.5 copy-start.2
  266.9 15.1 copy-start.13
  266.9 15.1 copy-start.3
  282.0 15.3 copy-start.32
  282.0 15.2 copy-start.4
  282.0 15.2 copy-start.20
  297.3 15.5 copy-start.35
  297.3 25.9 %copy-start.1 = (bf16[128,1024]{1,0:T(8,128)(2,1)S(1)}, bf16[128,1024]{1,0:T(8,128)(2,1)}, u32[]{:S(2)}) copy-start(bf16[128,1024]{1,0:T(8,128)(2,1)} %param.13) | copy-start | bytes 786436
  312.7 10.4 copy-start.21
  313.6 9.6 all-to-all-start.3
  317.2 267.4 %copy-start.30 = (f32[1024]{0:T(1024)}, f32[1024]{0:T(1024)S(1)}, u32[]{:S(2)}) copy-start(f32[1024]{0:T(1024)S(1)} %convert_element_type.155) | copy-start | bytes 12292
  323.1 89.7 %copy-start.15 = (bf16[4,128,256]{1,2,0:T(8,128)(2,1)}, bf16[4,128,256]{1,2,0:T(8,128)(2,1)S(1)}, u32[]{:S(2)}) copy-start(bf16[4,128,256]{1,2,0:T(8,128)(2,1)S(1)} %all-to-all-done.3) | copy-start | bytes 786436
  325.4 259.2 %copy-start.39 = (f32[128]{0:T(128)}, f32[128]{0:T(128)S(1)}, u32[]{:S(2)}) copy-start(f32[128]{0:T(128)S(1)} %fusion.82) | copy-start | bytes 1540
  412.9 159.5 %copy-start.19 = (bf16[128,1024]{1,0:T(8,128)(2,1)S(1)}, bf16[128,1024]{1,0:T(8,128)(2,1)}, u32[]{:S(2)}) copy-start(bf16[128,1024]{1,0:T(8,128)(2,1)} %param.25) | copy-start | bytes 786436
  572.4 9.0 copy-start
  581.4 10.8 copy-start.9
  581.4 10.8 copy-start.10
  584.5 8.6 copy-start.6
  594.8 9.4 all-to-all-start.4
  598.2 90.6 %reduce-scatter.12.cloned.1.call-start = ((), (), s32[]{:S(2)}) async-start(), calls=%async_computation.27 | async-start | bytes 1179648 | tf_op jit(solution)/shard_map/reduce_scatter | solution.py:282
  606.1 17.6 copy-start.22
  626.0 129.5 %reduce-scatter.10.cloned.1.call-start = ((), (), s32[]{:S(2)}) async-start(), calls=%async_computation.26 | async-start | bytes 1179648 | tf_op jit(solution)/shard_map/reduce_scatter | solution.py:279
  626.1 23.3 %copy-start.14 = (bf16[512,2,2,64]{0,3,2,1:T(8,128)(2,1)S(1)}, bf16[512,2,2,64]{0,3,2,1:T(8,128)(2,1)}, u32[]{:S(2)}) copy-start(bf16[512,2,2,64]{0,3,2,1:T(8,128)(2,1)} %copy-done.13) | copy-start | bytes 786436
  661.4 105.5 %copy-start.8 = (f32[128,512]{0,1:T(8,128)S(1)}, f32[128,512]{0,1:T(8,128)}, u32[]{:S(2)}) copy-start(f32[128,512]{0,1:T(8,128)} %copy-done.7) | copy-start | bytes 786436
  663.7 233.2 %reduce-scatter.18.cloned.1.call-start = ((), (), s32[]{:S(2)}) async-start(), calls=%async_computation.30 | async-start | bytes 2162688 | tf_op jit(solution)/shard_map/reduce_scatter | solution.py:320
  701.9 334.0 %reduce-scatter.16.cloned.1.call-start = ((), (), s32[]{:S(2)}) async-start(), calls=%async_computation.29 | async-start | bytes 2162688 | tf_op jit(solution)/shard_map/reduce_scatter | solution.py:319
  773.2 407.8 %reduce-scatter.20.cloned.1.call-start = ((), (), s32[]{:S(2)}) async-start(), calls=%async_computation.31 | async-start | bytes 4325376 | tf_op jit(solution)/shard_map/reduce_scatter | solution.py:321
  777.1 548.4 %reduce-scatter.14.cloned.1.call-start = ((), (), s32[]{:S(2)}) async-start(), calls=%async_computation.28 | async-start | bytes 4325376 | tf_op jit(solution)/shard_map/reduce_scatter | solution.py:318
  803.8 733.4 %reduce-scatter.26.cloned.1.call-start = ((), (), s32[]{:S(2)}) async-start(), calls=%async_computation.34 | async-start | bytes 19464192 | tf_op jit(solution)/shard_map/reduce_scatter | solution.py:325
  812.8 937.4 %reduce-scatter.24.cloned.1.call-start = ((), (), s32[]{:S(2)}) async-start(), calls=%async_computation.33 | async-start | bytes 19464192 | tf_op jit(solution)/shard_map/reduce_scatter | solution.py:324
  822.0 1141.0 %reduce-scatter.22.cloned.1.call-start = ((), (), s32[]{:S(2)}) async-start(), calls=%async_computation.32 | async-start | bytes 19464192 | tf_op jit(solution)/shard_map/reduce_scatter | solution.py:323
  (16 other events, 77.0 us)
Sparse Core Ops, SparseCore 0:
  11.0 56.5 all-gather.9
  70.5 52.7 all-gather.13
  126.3 55.3 all-gather.17
  184.3 39.0 all-gather.11
  226.0 38.9 all-gather.15
  267.8 55.1 all-gather.19
  326.0 80.3 all-gather.23
  409.3 80.0 all-gather.21
  492.4 80.0 all-gather.25
  626.1 62.6 reduce-scatter.11
  692.2 63.2 reduce-scatter.9
  758.2 138.6 reduce-scatter.17
  899.7 136.1 reduce-scatter.15
  1038.6 142.3 reduce-scatter.19
  1183.7 141.7 reduce-scatter.13
  1332.4 204.7 reduce-scatter.25
  1544.1 206.0 reduce-scatter.23
  1757.0 205.9 reduce-scatter.21
where the time goes:
time: 1980 us; the launch traced here: 1970 us
  waiting for transfers between devices  1580 us (80%)
  matrix products  180 us (9%)
  blocking collectives  114 us (6%)
  other arithmetic  35.8 us (2%)
  local copies, waits for them, and re-layouts  24.7 us (1%)
    reduce_scatter x1, waiting for transfers between devices, local(): lax.psum_scatter(up_grad, ('head', 'blk'), scatter_dimension=0, tiled=True)  213 us
    reduce_scatter x1, waiting for transfers between devices, local(): lax.psum_scatter(gate_grad, ('head', 'blk'), scatter_dimension=0, tiled=T...  213 us
    reduce_scatter x1, waiting for transfers between devices, local(): lax.psum_scatter(down_grad, ('head', 'blk'), scatter_dimension=0, tiled=T...  212 us
    reduce_scatter x1, waiting for transfers between devices, local(): lax.psum_scatter(out_proj_grad, ('head', 'blk'), scatter_dimension=0, til...  145 us
    reduce_scatter x1, waiting for transfers between devices, local(): lax.psum_scatter(query_grad, ('head', 'blk'), scatter_dimension=0, tiled=...  145 us
    reduce_scatter x1, waiting for transfers between devices, local(): lax.psum_scatter(key_grad, ('head', 'blk'), scatter_dimension=0, tiled=True)  139 us
    unnamed x2, blocking collectives  81.2 us
    all_gather x1, waiting for transfers between devices, local(): lax.all_gather(w_up, ('head', 'blk'), axis=0, tiled=True)  80.8 us
  transfers between devices with their start and end apart: 22, of which 21 were waited for; matrix products, arithmetic and copies ran while one was open for 10% of the time, Pallas kernels for 0%

commit v1 on v0

v1 whole, which is shorter than its diff:
```python
import functools
import math

import jax
import jax.numpy as jnp
from jax import lax
from jax.experimental import pallas as pl
from jax.experimental.pallas import tpu as pltpu
from jax.sharding import PartitionSpec as P

EPS = 1e-05
THETA = 1000000.0
NEG = -1e30
CORES = 2
INNER = 2
MESH = pl.DeviceIdType.MESH
F32 = jnp.float32
BF16 = jnp.bfloat16


def here():
    head = lax.axis_index("head")
    blk = lax.axis_index("blk")
    return head // CORES, head % CORES, blk // INNER, blk % INNER


def device(y, c, z, x):
    return (y * CORES + c, z * INNER + x)


def rank(y, c, x):
    return (y * CORES + c) * INNER + x


def plane_peers(place):
    y, c, z, x = place
    peers = []
    for bits in range(1, 8):
        py = 1 - y if bits & 4 else y
        pc = 1 - c if bits & 2 else c
        px = 1 - x if bits & 1 else x
        peers.append((device(py, pc, z, px), rank(py, pc, px), (py * CORES + pc, px)))
    return peers


def line_peers(place):
    y, c, z, x = place
    outer = lax.axis_size("blk") // INNER
    forth = [lax.rem(z + k, outer) for k in range(1, outer)]
    back = [lax.rem(z + outer - k, outer) for k in range(1, outer)]
    return [(device(y, c, f, x), f, b) for f, b in zip(forth, back)]


def greet(devices):
    barrier = pltpu.get_barrier_semaphore()
    for dev in devices:
        pl.semaphore_signal(barrier, inc=1, device_id=dev, device_id_type=MESH)
    pl.semaphore_wait(barrier, len(devices))


class Mail:
    def __init__(self, sems):
        self.sends, self.recvs = sems
        self.used = 0
        self.open = []

    def take(self, count):
        first = self.used
        self.used += count
        return first

    def send(self, slot, src, dst, dev):
        copy = pltpu.make_async_remote_copy(
            src_ref=src,
            dst_ref=dst,
            send_sem=self.sends.at[slot],
            recv_sem=self.recvs.at[slot],
            device_id=dev,
            device_id_type=MESH,
        )
        copy.start()
        self.open.append(copy)

    def arrive(self, slot, dst, dev):
        pltpu.make_async_remote_copy(
            src_ref=dst,
            dst_ref=dst,
            send_sem=self.sends.at[slot],
            recv_sem=self.recvs.at[slot],
            device_id=dev,
            device_id_type=MESH,
        ).wait_recv()

    def close(self):
        for copy in self.open:
            copy.wait_send()


def near(place):
    y, c, z, x = place
    return device(y, 1 - c, z, x), device(y, c, z, 1 - x), device(1 - y, c, z, x)


class PlaneGather:
    COPIES = 11

    def __init__(self, mail, place, src, out):
        self.mail, self.place, self.src, self.out = mail, place, src, out
        self.base = mail.take(self.COPIES)
        half = src.shape[0] // 2
        self.top, self.bot = pl.ds(0, half), pl.ds(half, half)

    def begin(self):
        y, c, z, x = self.place
        pair, xn, yn = near(self.place)
        me = rank(y, c, x)
        send, base, src, out = self.mail.send, self.base, self.src, self.out
        top, bot = self.top, self.bot
        send(base + 0, src.at[top], out.at[me, top], xn)
        send(base + 1, src.at[bot], out.at[me, bot], yn)
        send(base + 2, src.at[bot], out.at[me, bot], xn)
        send(base + 3, src.at[top], out.at[me, top], yn)
        send(base + 4, src, out.at[me], pair)
        out[me] = src[...]

    def middle(self):
        y, c, z, x = self.place
        pair, xn, yn = near(self.place)
        xr, yr = rank(y, c, 1 - x), rank(1 - y, c, x)
        send, arrive, base, out = self.mail.send, self.mail.arrive, self.base, self.out
        top, bot = self.top, self.bot
        arrive(base + 0, out.at[xr, top], xn)
        send(base + 5, out.at[xr, top], out.at[xr, top], yn)
        arrive(base + 1, out.at[yr, bot], yn)
        send(base + 6, out.at[yr, bot], out.at[yr, bot], xn)
        arrive(base + 2, out.at[xr, bot], xn)
        send(base + 7, out.at[xr], out.at[xr], pair)
        arrive(base + 3, out.at[yr, top], yn)
        send(base + 8, out.at[yr], out.at[yr], pair)

    def end(self):
        y, c, z, x = self.place
        pair, xn, yn = near(self.place)
        dr = rank(1 - y, c, 1 - x)
        send, arrive, base, out = self.mail.send, self.mail.arrive, self.base, self.out
        top, bot = self.top, self.bot
        arrive(base + 5, out.at[dr, top], yn)
        send(base + 9, out.at[dr, top], out.at[dr, top], pair)
        arrive(base + 6, out.at[dr, bot], xn)
        send(base + 10, out.at[dr, bot], out.at[dr, bot], pair)
        arrive(base + 4, out.at[rank(y, 1 - c, x)], pair)
        arrive(base + 7, out.at[rank(y, 1 - c, 1 - x)], pair)
        arrive(base + 8, out.at[rank(1 - y, 1 - c, x)], pair)
        far = rank(1 - y, 1 - c, 1 - x)
        arrive(base + 9, out.at[far, top], pair)
        arrive(base + 10, out.at[far, bot], pair)


class PlaneScatter:
    COPIES = 10

    def __init__(self, mail, place, parts, out, bufs):
        self.mail, self.place, self.parts, self.out = mail, place, parts, out
        self.first, self.held, self.via_x, self.via_y, self.last = bufs
        self.base = mail.take(self.COPIES)
        half = out.shape[0] // 2
        self.top, self.bot = pl.ds(0, half), pl.ds(half, half)

    @staticmethod
    def scratch(rows, cols):
        half = rows // 2
        return [
            pltpu.VMEM((2, 2, rows, cols), BF16),
            pltpu.VMEM((2, 2, rows, cols), BF16),
            pltpu.VMEM((2, half, cols), BF16),
            pltpu.VMEM((2, half, cols), BF16),
            pltpu.VMEM((4, half, cols), BF16),
        ]

    def begin(self):
        y, c, z, x = self.place
        pair, xn, yn = near(self.place)
        for slot, (py, px) in enumerate(((1 - y, 1 - x), (y, 1 - x), (1 - y, x), (y, x))):
            self.mail.send(
                self.base + slot,
                self.parts.at[rank(py, 1 - c, px)],
                self.first.at[py, px],
                pair,
            )

    def joined(self, slot, py, px):
        y, c, z, x = self.place
        pair, xn, yn = near(self.place)
        self.mail.arrive(self.base + slot, self.first.at[py, px], pair)
        return self.parts[rank(py, c, px)].astype(F32) + self.first[py, px].astype(F32)

    def middle(self):
        y, c, z, x = self.place
        pair, xn, yn = near(self.place)
        send, base, held = self.mail.send, self.base, self.held
        top, bot = self.top, self.bot
        held[1 - y, 1 - x] = self.joined(0, 1 - y, 1 - x).astype(BF16)
        send(base + 4, held.at[1 - y, 1 - x, top], self.via_x.at[1 - y], xn)
        send(base + 5, held.at[1 - y, 1 - x, bot], self.via_y.at[1 - x], yn)
        held[y, 1 - x] = self.joined(1, y, 1 - x).astype(BF16)
        send(base + 6, held.at[y, 1 - x, top], self.via_x.at[y], xn)
        held[1 - y, x] = self.joined(2, 1 - y, x).astype(BF16)
        send(base + 7, held.at[1 - y, x, bot], self.via_y.at[x], yn)
        self.out[...] = self.joined(3, y, x)

    def end(self):
        y, c, z, x = self.place
        pair, xn, yn = near(self.place)
        send, arrive, base, held = self.mail.send, self.mail.arrive, self.base, self.held
        top, bot, last, out = self.top, self.bot, self.last, self.out
        arrive(base + 4, self.via_x.at[1 - y], xn)
        last[0] = (held[1 - y, x, top].astype(F32) + self.via_x[1 - y].astype(F32)).astype(BF16)
        send(base + 8, last.at[0], last.at[2], yn)
        arrive(base + 5, self.via_y.at[1 - x], yn)
        last[1] = (held[y, 1 - x, bot].astype(F32) + self.via_y[1 - x].astype(F32)).astype(BF16)
        send(base + 9, last.at[1], last.at[3], xn)
        arrive(base + 6, self.via_x.at[y], xn)
        out[top] = out[top] + self.via_x[y].astype(F32)
        arrive(base + 7, self.via_y.at[x], yn)
        out[bot] = out[bot] + self.via_y[x].astype(F32)
        arrive(base + 8, last.at[2], yn)
        out[top] = out[top] + last[2].astype(F32)
        arrive(base + 9, last.at[3], xn)
        out[bot] = out[bot] + last[3].astype(F32)


class PlaneSwap:
    COPIES = 7

    def __init__(self, mail, place, src, out):
        self.mail, self.place, self.src, self.out = mail, place, src, out
        self.base = mail.take(self.COPIES)

    def begin(self):
        y, c, z, x = self.place
        me = rank(y, c, x)
        for slot, (dev, other, _) in enumerate(plane_peers(self.place)):
            self.mail.send(self.base + slot, self.src.at[other], self.out.at[me], dev)
        self.out[me] = self.src[me]

    def end(self):
        for slot, (dev, other, _) in enumerate(plane_peers(self.place)):
            self.mail.arrive(self.base + slot, self.out.at[other], dev)


def call(body, name, ident, outs, args, copies, scratch=()):
    spec = pl.BlockSpec(memory_space=pltpu.VMEM)
    return pl.pallas_call(
        body,
        name=name,
        out_shape=tuple(jax.ShapeDtypeStruct(shape, dtype) for shape, dtype in outs),
        in_specs=[spec] * len(args),
        out_specs=tuple([spec] * len(outs)),
        scratch_shapes=[
            pltpu.SemaphoreType.DMA((copies,)),
            pltpu.SemaphoreType.DMA((copies,)),
            *scratch,
        ],
        compiler_params=pltpu.CompilerParams(
            collective_id=ident, has_side_effects=True, vmem_limit_bytes=60 * 1024 * 1024
        ),
    )(*args)


def start_kernel(x_ref, w_ref, g_ref, gu_ref, xp_ref, wq_ref, gain_ref, gus_ref, ss, rs):
    place = y, c, z, x = here()
    me = rank(y, c, x)
    head = y * CORES + c
    mail = Mail((ss, rs))
    peers, line = plane_peers(place), line_peers(place)
    greet([p[0] for p in peers] + [p[0] for p in line])
    w_base, g_base = mail.take(7), mail.take(7)
    zw_base, zg_base = mail.take(len(line)), mail.take(len(line))
    for slot, (dev, other, _) in enumerate(peers):
        mail.send(g_base + slot, g_ref, gain_ref.at[z, me], dev)
        mail.send(w_base + slot, w_ref.at[other], wq_ref.at[head, z, x], dev)
    gain_ref[z, me] = g_ref[...]
    wq_ref[head, z, x] = w_ref[me]
    rows = PlaneGather(mail, place, x_ref, xp_ref)
    swap = PlaneSwap(mail, place, gu_ref, gus_ref)
    rows.begin()
    for slot, (dev, other, (oh, ox)) in enumerate(peers):
        mail.arrive(g_base + slot, gain_ref.at[z, other], dev)
        mail.arrive(w_base + slot, wq_ref.at[oh, z, ox], dev)
    for slot, (dev, _, _) in enumerate(line):
        mail.send(zg_base + slot, gain_ref.at[z], gain_ref.at[z], dev)
        mail.send(zw_base + slot, wq_ref.at[:, z], wq_ref.at[:, z], dev)
    rows.middle()
    swap.begin()
    rows.end()
    for slot, (dev, _, back) in enumerate(line):
        mail.arrive(zg_base + slot, gain_ref.at[back], dev)
        mail.arrive(zw_base + slot, wq_ref.at[:, back], dev)
    swap.end()
    mail.close()


def line_kernel(kv_ref, og_ref, kvs_ref, ogs_ref, ss, rs):
    place = y, c, z, x = here()
    mail = Mail((ss, rs))
    line = line_peers(place)
    greet([p[0] for p in line] + list(near(place)))
    base = mail.take(len(line))
    for slot, (dev, _, _) in enumerate(line):
        mail.send(base + slot, kv_ref, kvs_ref.at[z], dev)
    rows = PlaneGather(mail, place, og_ref, ogs_ref)
    rows.begin()
    kvs_ref[z] = kv_ref[...]
    rows.middle()
    rows.end()
    for slot, (dev, _, back) in enumerate(line):
        mail.arrive(base + slot, kvs_ref.at[back], dev)
    mail.close()


def gather_kernel(src_ref, out_ref, ss, rs):
    place = here()
    mail = Mail((ss, rs))
    greet(list(near(place)))
    rows = PlaneGather(mail, place, src_ref, out_ref)
    rows.begin()
    rows.middle()
    rows.end()
    mail.close()


def scatter_kernel(parts_ref, out_ref, ss, rs, *bufs):
    place = here()
    mail = Mail((ss, rs))
    greet(list(near(place)))
    rows = PlaneScatter(mail, place, parts_ref, out_ref, bufs)
    rows.begin()
    rows.middle()
    rows.end()
    mail.close()


def back_kernel(dkv_ref, parts_ref, kv_ref, out_ref, ss, rs, got, *bufs):
    place = y, c, z, x = here()
    mail = Mail((ss, rs))
    line = line_peers(place)
    greet([p[0] for p in line] + list(near(place)))
    base = mail.take(len(line))
    for slot, (dev, forth, _) in enumerate(line):
        mail.send(base + slot, dkv_ref.at[forth], got.at[slot], dev)
    rows = PlaneScatter(mail, place, parts_ref, out_ref, bufs)
    rows.begin()
    rows.middle()
    rows.end()
    total = dkv_ref[z].astype(F32)
    for slot, (dev, _, _) in enumerate(line):
        mail.arrive(base + slot, got.at[slot], dev)
        total = total + got[slot].astype(F32)
    kv_ref[...] = total
    mail.close()


def last_kernel(parts_ref, w_ref, gu_ref, out_ref, ws_ref, gus_ref, ss, rs, got, held, *bufs):
    place = y, c, z, x = here()
    me = rank(y, c, x)
    mail = Mail((ss, rs))
    peers, line = plane_peers(place), line_peers(place)
    greet([p[0] for p in line] + [p[0] for p in peers])
    base = mail.take(len(line))
    w_base = mail.take(7)
    for slot, (dev, forth, _) in enumerate(line):
        mail.send(base + slot, w_ref.at[:, forth], got.at[slot], dev)
    rows = PlaneScatter(mail, place, parts_ref, out_ref, bufs)
    swap = PlaneSwap(mail, place, gu_ref, gus_ref)
    rows.begin()
    rows.middle()
    swap.begin()
    rows.end()
    total = w_ref[:, z].astype(F32)
    for slot, (dev, _, _) in enumerate(line):
        mail.arrive(base + slot, got.at[slot], dev)
        total = total + got[slot].astype(F32)
    held[...] = total.reshape(held.shape)
    for slot, (dev, other, _) in enumerate(peers):
        mail.send(w_base + slot, held.at[other], ws_ref.at[me], dev)
    ws_ref[me] = held[me]
    for slot, (dev, other, _) in enumerate(peers):
        mail.arrive(w_base + slot, ws_ref.at[other], dev)
    swap.end()
    mail.close()


def small_kernel(v_ref, out_ref, ss, rs, got, held):
    place = y, c, z, x = here()
    me = rank(y, c, x)
    mail = Mail((ss, rs))
    peers, line = plane_peers(place), line_peers(place)
    greet([p[0] for p in line] + [p[0] for p in peers])
    p_base, z_base = mail.take(7), mail.take(len(line))
    for slot, (dev, other, _) in enumerate(peers):
        mail.send(p_base + slot, v_ref, got.at[me], dev)
    got[me] = v_ref[...]
    for slot, (dev, other, _) in enumerate(peers):
        mail.arrive(p_base + slot, got.at[other], dev)
    held[z] = jnp.sum(got[...], axis=0)
    for slot, (dev, _, _) in enumerate(line):
        mail.send(z_base + slot, held.at[z], held.at[z], dev)
    for slot, (dev, _, back) in enumerate(line):
        mail.arrive(z_base + slot, held.at[back], dev)
    out_ref[...] = jnp.sum(held[...], axis=0)
    mail.close()


def rms_norm(values, gain_vec):
    inverse = lax.rsqrt(jnp.mean(values * values, axis=-1, keepdims=True) + EPS)
    return values * inverse * gain_vec


def rotate(field_in, where_at):
    half_size = field_in.shape[-1] // 2
    frequency = jnp.exp(
        jnp.arange(half_size, dtype=F32) * F32(-2.0 * math.log(THETA) / field_in.shape[-1])
    )
    angles = where_at.astype(F32)[:, None] * frequency[None, :]
    cosine = jnp.cos(angles)[:, None, :]
    sine_part = jnp.sin(angles)[:, None, :]
    first_half = field_in[..., :half_size]
    second_half = field_in[..., half_size:]
    return jnp.concatenate(
        [
            first_half * cosine - second_half * sine_part,
            second_half * cosine + first_half * sine_part,
        ],
        axis=-1,
    )


def head_map(raw_rows, gain_vec, where_at):
    row_count = raw_rows.shape[0]
    shaped = raw_rows.reshape(row_count, -1, gain_vec.shape[0])
    return rotate(rms_norm(shaped, gain_vec), where_at).reshape(row_count, -1)


def shifts(outer, step):
    return [
        (z * INNER + x, ((z + step) % outer) * INNER + x)
        for z in range(outer)
        for x in range(INNER)
    ]


def line_gather(piece, axis, full_shape, z, outer):
    full = jnp.zeros(full_shape, piece.dtype)
    full = lax.dynamic_update_slice_in_dim(full, jnp.expand_dims(piece, axis), z, axis)
    for step in range(1, outer):
        got = lax.ppermute(piece, "blk", shifts(outer, step))
        full = lax.dynamic_update_slice_in_dim(
            full, jnp.expand_dims(got, axis), (z + outer - step) % outer, axis
        )
    return full


def line_scatter(parts, axis, z, outer):
    total = lax.dynamic_index_in_dim(parts, z, axis, keepdims=False).astype(F32)
    for step in range(1, outer):
        piece = lax.dynamic_index_in_dim(parts, (z + step) % outer, axis, keepdims=False)
        total = total + lax.ppermute(piece.astype(BF16), "blk", shifts(outer, step)).astype(F32)
    return total


def dot(a, b):
    return jnp.dot(a, b, preferred_element_type=F32)


def local(
    block_input,
    span_order,
    norm1_gain,
    w_query,
    key_weight,
    value_weight,
    qk_gain,
    w_out,
    norm2_gain,
    w_gate,
    w_up,
    w_down,
    out_grad,
):
    heads = lax.axis_size("head")
    blocks = lax.axis_size("blk")
    outer = blocks // INNER
    plane = heads * INNER
    z = lax.axis_index("blk") // INNER
    x_at = lax.axis_index("blk") % INNER
    rows, width = block_input.shape
    head_size = qk_gain.shape[1]
    w_rows = w_query.shape[0]
    f_rows = w_down.shape[0]
    q_cols = w_query.shape[1] // plane
    k_cols = key_weight.shape[1] // plane
    share = q_cols // k_cols
    a_cols = q_cols + 2 * k_cols
    ff = f_rows * outer
    tokens = plane * rows
    score_scale = float(head_size) ** (-0.5)

    by_place = span_order.reshape(heads, outer, INNER)
    own_spans = lax.dynamic_index_in_dim(by_place, z, 1, keepdims=False).reshape(plane)
    all_spans = by_place.transpose(1, 0, 2).reshape(outer * plane)
    inside = jnp.arange(rows, dtype=jnp.int32)
    tok_where = (own_spans[:, None] * rows + inside[None, :]).reshape(tokens)
    key_where = (all_spans[:, None] * rows + inside[None, :]).reshape(outer * tokens)

    w8 = jnp.concatenate(
        [
            w_query.reshape(w_rows, plane, q_cols),
            key_weight.reshape(w_rows, plane, k_cols),
            value_weight.reshape(w_rows, plane, k_cols),
        ],
        axis=-1,
    ).transpose(1, 0, 2)

    def cut(weight):
        shaped = weight.reshape(w_rows, heads, outer, INNER, f_rows)
        return shaped.transpose(1, 3, 0, 2, 4).reshape(plane, w_rows, ff)

    gu8 = jnp.concatenate([cut(w_gate), cut(w_up)], axis=-1)
    gains = jnp.zeros((16, 128), BF16)
    gains = gains.at[0, :w_rows].set(norm1_gain).at[1, :w_rows].set(norm2_gain)
    down_full = line_gather(w_down, 0, (outer, f_rows, width), z, outer).reshape(ff, width)
    out_all = lax.all_gather(w_out, "blk", axis=0, tiled=True)

    n_line = outer - 1
    x_all, wqkv, gains_all, gu_piece = call(
        start_kernel,
        "start",
        1,
        [
            ((plane, rows, width), BF16),
            ((heads, outer, INNER, w_rows, a_cols), BF16),
            ((outer, plane, 16, 128), BF16),
            ((plane, w_rows, 2 * ff), BF16),
        ],
        (block_input, w8, gains, gu8),
        14 + 2 * n_line + PlaneGather.COPIES + PlaneSwap.COPIES,
    )
    wqkv = wqkv.reshape(width, a_cols)
    gains_all = (
        gains_all[:, :, :2, :w_rows]
        .reshape(outer, heads, INNER, 2, w_rows)
        .transpose(3, 1, 0, 2, 4)
        .reshape(2, width)
        .astype(F32)
    )
    gain_one, gain_two = gains_all[0], gains_all[1]
    gu_full = line_gather(
        gu_piece.reshape(heads, INNER * w_rows, 2 * ff),
        1,
        (heads, outer, INNER * w_rows, 2 * ff),
        z,
        outer,
    ).reshape(width, 2 * ff)

    normed = rms_norm(x_all.reshape(tokens, width).astype(F32), gain_one).astype(BF16)
    qkv_raw = dot(normed, wqkv)
    q_raw = qkv_raw[:, :q_cols]
    k_raw = qkv_raw[:, q_cols : q_cols + k_cols]
    v_raw = qkv_raw[:, q_cols + k_cols :]

    def query_map(raw_rows, gain_vec):
        return head_map(raw_rows, gain_vec, tok_where)

    queries = query_map(q_raw, qk_gain[0]).astype(BF16)
    keys = query_map(k_raw, qk_gain[1]).astype(BF16)
    kv = jnp.concatenate([keys, v_raw.astype(BF16)], axis=-1)
    kv_all, og_all = call(
        line_kernel,
        "line",
        2,
        [((outer, tokens, 2 * k_cols), BF16), ((plane, rows, width), BF16)],
        (kv, out_grad),
        n_line + PlaneGather.COPIES,
    )
    og_all = og_all.reshape(tokens, width)
    k_all = kv_all[:, :, :k_cols].reshape(outer * tokens, k_cols)
    v_all = kv_all[:, :, k_cols:].reshape(outer * tokens, k_cols)
    q_three = queries.reshape(tokens, share, head_size)
    causal = key_where[None, :] <= tok_where[:, None]
    scores = jnp.einsum("qgd,nd->gqn", q_three, k_all, preferred_element_type=F32) * score_scale
    scores = jnp.where(causal, scores, NEG)
    row_max = jnp.max(scores, axis=-1)
    weights = jnp.where(causal, jnp.exp(scores - row_max[..., None]), 0.0)
    row_sum = jnp.sum(weights, axis=-1)
    mixed = jnp.einsum("gqn,nd->qgd", weights.astype(BF16), v_all, preferred_element_type=F32)
    attended3 = (mixed / row_sum.T[..., None]).astype(BF16)
    log_total = row_max + jnp.log(row_sum)
    attended = attended3.reshape(tokens, q_cols)

    out_mine = lax.dynamic_slice_in_dim(out_all, x_at * q_cols, q_cols, 0)

    def scatter(parts, name, ident):
        return call(
            scatter_kernel,
            name,
            ident,
            [((rows, width), F32)],
            (parts.astype(BF16).reshape(plane, rows, width),),
            PlaneScatter.COPIES,
            PlaneScatter.scratch(rows, width),
        )[0]

    def gather(block, name, ident):
        return call(
            gather_kernel,
            name,
            ident,
            [((plane, rows, width), BF16)],
            (block,),
            PlaneGather.COPIES,
        )[0].reshape(tokens, width)

    in_flat = block_input.astype(F32)
    middle = in_flat + scatter(dot(attended, out_mine), "mix", 3)
    normed2_own = rms_norm(middle, gain_two).astype(BF16)
    normed2 = gather(normed2_own, "widen", 4)

    gu_rows = dot(normed2, gu_full)
    gate_rows, up_rows = gu_rows[:, :ff], gu_rows[:, ff:]
    hidden, gate_back = jax.vjp(lambda a, b: jax.nn.silu(a) * b, gate_rows, up_rows)
    hidden = hidden.astype(BF16)
    dhidden = dot(og_all, down_full.T)
    dgate, dup = gate_back(dhidden)
    dgu = jnp.concatenate([dgate.astype(BF16), dup.astype(BF16)], axis=-1)
    dnormed2 = scatter(dot(dgu, gu_full.T), "narrow", 5)
    out_parts = dot(hidden, down_full).astype(BF16).reshape(plane, rows, width)
    gu_grad = dot(normed2.T, dgu)
    down_grad = dot(hidden.T, og_all)
    down_grad = line_scatter(down_grad.reshape(outer, f_rows, width), 0, z, outer)
    gu_grad = line_scatter(
        gu_grad.reshape(heads, outer, INNER * w_rows, 2 * ff), 1, z, outer
    ).reshape(plane, w_rows, 2 * ff)

    _, norm2_back = jax.vjp(rms_norm, middle, gain_two)
    dmiddle_norm, norm2_grad = norm2_back(dnormed2)
    dmiddle = out_grad.astype(F32) + dmiddle_norm
    dmid_all = gather(dmiddle.astype(BF16), "spread", 6)

    out_proj = dot(attended.T, dmid_all)
    out_proj = jnp.where(
        (jnp.arange(INNER) == x_at)[:, None, None], out_proj[None], 0.0
    ).reshape(INNER * q_cols, width)
    out_proj_grad = lax.psum_scatter(out_proj, "blk", scatter_dimension=0, tiled=True)
    dattended = dot(dmid_all, out_mine.T).astype(BF16)
    grad_three = dattended.reshape(tokens, share, head_size)
    delta = jnp.sum(grad_three.astype(F32) * attended3.astype(F32), axis=-1).T
    prob = jnp.where(causal, jnp.exp(scores - log_total[..., None]), 0.0)
    dvalues = jnp.einsum("gqn,qgd->nd", prob.astype(BF16), grad_three, preferred_element_type=F32)
    dprob = jnp.einsum("qgd,nd->gqn", grad_three, v_all, preferred_element_type=F32)
    dscore = (prob * (dprob - delta[..., None])).astype(BF16)
    dqueries = jnp.einsum("gqn,nd->qgd", dscore, k_all, preferred_element_type=F32) * score_scale
    dkeys = jnp.einsum("gqn,qgd->nd", dscore, q_three, preferred_element_type=F32) * score_scale
    dkv = jnp.concatenate([dkeys, dvalues], axis=-1).astype(BF16)
    dkv_own, ffn_out = call(
        back_kernel,
        "back",
        7,
        [((tokens, 2 * k_cols), F32), ((rows, width), F32)],
        (dkv.reshape(outer, tokens, 2 * k_cols), out_parts),
        n_line + PlaneScatter.COPIES,
        [pltpu.VMEM((n_line, tokens, 2 * k_cols), BF16)] + PlaneScatter.scratch(rows, width),
    )
    block_output = (middle + ffn_out).astype(BF16)
    dkv_own = dkv_own.astype(BF16)
    dqueries = dqueries.reshape(tokens, q_cols).astype(BF16)
    _, query_back = jax.vjp(query_map, q_raw, qk_gain[0])
    dq_raw, qgain_grad = query_back(dqueries.astype(F32))
    _, key_back = jax.vjp(query_map, k_raw, qk_gain[1])
    dk_raw, kgain_grad = key_back(dkv_own[:, :k_cols].astype(F32))
    dqkv = jnp.concatenate(
        [dq_raw.astype(BF16), dk_raw.astype(BF16), dkv_own[:, k_cols:]], axis=-1
    )
    wqkv_grad = dot(normed.T, dqkv).astype(BF16)
    dnormed, wqkv_own, gu_own = call(
        last_kernel,
        "last",
        8,
        [
            ((rows, width), F32),
            ((plane, w_rows, a_cols), F32),
            ((plane, w_rows, 2 * ff), BF16),
        ],
        (
            dot(dqkv, wqkv.T).astype(BF16).reshape(plane, rows, width),
            wqkv_grad.reshape(heads, outer, INNER, w_rows, a_cols),
            gu_grad.astype(BF16),
        ),
        n_line + 7 + PlaneScatter.COPIES + PlaneSwap.COPIES,
        [
            pltpu.VMEM((n_line, heads, INNER, w_rows, a_cols), BF16),
            pltpu.VMEM((plane, w_rows, a_cols), F32),
        ]
        + PlaneScatter.scratch(rows, width),
    )
    _, norm1_back = jax.vjp(rms_norm, in_flat, gain_one)
    dinput_norm, norm1_grad = norm1_back(dnormed)
    input_grad = (dmiddle + dinput_norm).astype(BF16)

    small = jnp.concatenate([norm1_grad, norm2_grad, qgain_grad, kgain_grad])
    small_rows = -(-small.shape[0] // 1024) * 8
    small = jnp.pad(small, (0, small_rows * 128 - small.shape[0])).reshape(small_rows, 128)
    summed = call(
        small_kernel,
        "small",
        9,
        [((small_rows, 128), F32)],
        (small,),
        7 + n_line,
        [pltpu.VMEM((plane, small_rows, 128), F32), pltpu.VMEM((outer, small_rows, 128), F32)],
    )[0].reshape(-1)
    own = (lax.axis_index("head") * blocks + lax.axis_index("blk")) * w_rows
    norm1_out = lax.dynamic_slice_in_dim(summed, own, w_rows)
    norm2_out = lax.dynamic_slice_in_dim(summed, width + own, w_rows)
    qk_gain_grad = summed[2 * width : 2 * width + 2 * head_size].reshape(2, head_size)

    def columns(blocks_in):
        return blocks_in.transpose(1, 0, 2).reshape(w_rows, -1)

    query_grad = columns(wqkv_own[:, :, :q_cols])
    key_grad = columns(wqkv_own[:, :, q_cols : q_cols + k_cols])
    value_grad = columns(wqkv_own[:, :, q_cols + k_cols :])

    def uncut(blocks_in):
        shaped = blocks_in.astype(F32).reshape(heads, INNER, w_rows, outer, f_rows)
        return shaped.transpose(2, 0, 3, 1, 4).reshape(w_rows, -1)

    gate_grad = uncut(gu_own[:, :, :ff])
    up_grad = uncut(gu_own[:, :, ff:])
    return (
        block_output,
        input_grad,
        norm1_out,
        query_grad,
        key_grad,
        value_grad,
        qk_gain_grad,
        out_proj_grad,
        norm2_out,
        gate_grad,
        up_grad,
        down_grad,
    )


def solution(mesh):
    split = P(("head", "blk"), None)
    line = P(("head", "blk"))
    in_specs = (split, P(), line, split, split, split, P(), split, line, split, split, split, split)
    out_specs = (split, split, line, split, split, split, P(), split, line, split, split, split)
    return jax.shard_map(local, mesh=mesh, in_specs=in_specs, out_specs=out_specs, check_vma=False)
```

time: 1980 us -> 608 us (0.31)
  waiting for transfers between devices: 1580 us -> 18.1 us
  Pallas kernels: 0 us -> 247 us
  blocking collectives: 114 us -> 36.7 us
  matrix products: 180 us -> 113 us
  other arithmetic: 35.8 us -> 85 us
  local copies, waits for them, and re-layouts: 24.7 us -> 55.2 us
    reduce_scatter x9 -> x1, waiting for transfers between devices: 1160 us -> 0.01 us  [local(): lax.psum_scatter(out_proj, 'blk', scatter_dimension=0, tiled=True)]
    all_gather x9 -> x0, waiting for transfers between devices: 411 us -> none  [the longest x1 80.8 us: local(): lax.all_gather(w_up, ('head', 'blk'), axis=0, tiled=True)]
    pallas_call x0 -> x9, Pallas kernels: none -> 247 us  [call(): pl.pallas_call(body, name=name, out_shape=tuple((jax.ShapeDtypeStruct(sha...]
    unnamed x2 -> x0, blocking collectives: 81.2 us -> none
    dot_general x27 -> x18, matrix products: 180 us -> 113 us  [the longest x12 33.2 us: dot(): return jnp.dot(a, b, preferred_element_type=F32)]
    all_gather x0 -> x1, blocking collectives: none -> 36.7 us  [local(): out_all = lax.all_gather(w_out, 'blk', axis=0, tiled=True)]
    all_to_all x4 -> x0, blocking collectives: 32.6 us -> none  [the longest x1 8.92 us: local(): lax.all_to_all(query_acc.reshape(group_rows, -1).astype(jnp.bfloat16), 'h...]
    convert_element_type x9 -> x11, other arithmetic: 3.47 us -> 33.4 us  [the longest x1 20.9 us: local(): prob.astype(BF16)]
  transfers between devices with their start and end apart: 22 -> 13, of which waited for: 21 -> 2; matrix products, arithmetic and copies ran while one was open for 10% -> 30% of each run, Pallas kernels for 0% -> 32%
where the time goes in v1:
time: 608 us; the launch traced here: 599 us
  Pallas kernels  247 us (41%)
  matrix products  113 us (19%)
  other arithmetic  85 us (14%)
  local copies, waits for them, and re-layouts  55.2 us (9%)
  blocking collectives  36.7 us (6%)
  starting transfers between devices  27.2 us (4%)
  waiting for transfers between devices  18.1 us (3%)
  between operations  15.7 us (3%)
    pallas_call x9, Pallas kernels, call(): pl.pallas_call(body, name=name, out_shape=tuple((jax.ShapeDtypeStruct(sha...  247 us
    all_gather x1, blocking collectives, local(): out_all = lax.all_gather(w_out, 'blk', axis=0, tiled=True)  36.7 us
    dot_general x12, matrix products, dot(): return jnp.dot(a, b, preferred_element_type=F32)  33.2 us
    dot_general x1, matrix products, local(): jnp.einsum('qgd,nd->gqn', grad_three, v_all, preferred_element_type=F32)  21.1 us
    convert_element_type x1, other arithmetic, local(): prob.astype(BF16)  20.9 us
    dot_general x1, matrix products, local(): jnp.einsum('gqn,nd->qgd', weights.astype(BF16), v_all, preferred_element_...  17.8 us
    ppermute x6, starting transfers between devices, line_scatter(): lax.ppermute(piece.astype(BF16), 'blk', shifts(outer, step)).astype(F32)  16.2 us
    dot_general x1, matrix products, local(): jnp.einsum('qgd,nd->gqn', q_three, k_all, preferred_element_type=F32)  16 us
  transfers between devices with their start and end apart: 13, of which 2 were waited for; matrix products, arithmetic and copies ran while one was open for 30% of the time, Pallas kernels for 32%

profile of v1, /device:TPU:0, one launch (start us, length us, event | category | flops | bytes accessed | tf_op | source)
XLA Modules:
  0.0 598.6 jit_solution(17122139358929937765)
XLA Ops:
  13.9 27.3 %start.1 = (bf16[8,128,1024]{2,1,0:T(8,128)(2,1)}, bf16[4,4,2,32,256]{4,3,2,1,0:T(8,128)(2,1)}, bf16[4,8,16,128]{3,2,1,0:T(8,128)(2,1)}, bf16[8,32,1152]{2,1,0:T(8,128)(2,1)}) custom-call(bf16[128,1024]{1,0:T(8,128)(2,1)} %x_ref.1, bf16[8,32,256]{2,1,0:T(8,128)(2,1)} %maximum_bitcast_fusion.1.w_ref, bf16[16,128]{1,0:T(8,128)(2,1)} %copy-done.62, ...), custom_call_target="tpu_custom_call" | custom-call | tf_op jit(solution)/shard_map/start/pallas_call | solution.py:253
  41.2 3.1 collective-permute-start.3
  44.3 2.4 collective-permute-start.4
  50.3 2.1 multiply_reduce_fusion
  55.6 4.0 broadcast_compare_fusion.1
  59.5 4.0 broadcast_compare_fusion
  67.8 3.1 fusion.51
  75.6 59.7 %line.1 = (bf16[4,1024,128]{2,1,0:T(8,128)(2,1)}, bf16[8,128,1024]{2,1,0:T(8,128)(2,1)}) custom-call(bf16[1024,128]{1,0:T(8,128)(2,1)} %pad_maximum_fusion.6.kv_ref, bf16[128,1024]{1,0:T(8,128)(2,1)} %og_ref.1), custom_call_target="tpu_custom_call" | custom-call | tf_op jit(solution)/shard_map/line/pallas_call | solution.py:253
  135.4 3.5 fusion.95
  138.9 36.7 %all_gather.3 = bf16[256,1024]{1,0:T(8,128)(2,1)} all-gather(bf16[32,1024]{1,0:T(8,128)(2,1)S(1)} %copy-done.57), channel_id=1, replica_groups=mesh['head'=4,'blk'=8] {'blk'}, dimensions={0}, use_global_device_ids=true | all-gather | bytes 589824 | tf_op jit(solution)/shard_map/all_gather | solution.py:532
  175.8 16.0 %fusion.7 = (f32[2,1024]{1,0:T(2,128)S(1)}, f32[4096,1024,2]{1,0,2:T(8,128)}) fusion(pred[1024,4096]{0,1:T(8,128)(4,1)} %broadcast_compare_fusion.1, bf16[4096,64,1]{1,0,2:T(8,128)(2,1)} %bitcast.272, bf16[1024,2,32]{0,2,1:T(8,128)(2,1)S(1)} %get-tuple-element.82, bf16[1024,2,32]{0,2,1:T(8,128)(2,1)S(1)} %get-tuple-element.81), kind=kOutput, calls=%fused_computation.11 | convolution fusion | flops 1099429888 | bytes 38543360 | tf_op jit(solution)/shard_map/qgd,nd->gqn/dot_general | solution.py:590
  191.9 15.1 %fusion.5 = f32[2,1024]{1,0:T(2,128)S(1)} fusion(f32[4096,1024,2]{1,0,2:T(8,128)} %get-tuple-element.109, f32[2,1024]{1,0:T(2,128)S(1)} %get-tuple-element.108, pred[1024,4096]{0,1:T(8,128)(4,1)S(1)} %copy-done.5), kind=kLoop, calls=%fused_computation.9 | loop fusion | flops 41940992 | bytes 37765120 | tf_op jit(solution)/shard_map/reduce_sum | solution.py:594
  207.0 17.8 %fusion.34 = bf16[1024,2,64]{0,2,1:T(8,128)(2,1)} fusion(bf16[4096,64,1]{1,0,2:T(8,128)(2,1)} %bitcast.289, f32[4096,1024,2]{1,0,2:T(8,128)} %get-tuple-element.109, f32[2,1024]{1,0:T(2,128)S(1)} %get-tuple-element.108, pred[1024,4096]{0,1:T(8,128)(4,1)} %broadcast_compare_fusion.1, f32[1024,2]{0,1:T(2,128)S(1)} %bitcast.302), kind=kOutput, calls=%fused_computation.63 | convolution fusion | flops 1115947008 | bytes 38551552 | tf_op jit(solution)/shard_map/gqn,nd->qgd/dot_general | solution.py:595
  224.7 3.1 convolution_convert_fusion.3
  227.8 14.7 %mix.1 = f32[128,1024]{1,0:T(8,128)} custom-call(bf16[8,128,1024]{2,1,0:T(8,128)(2,1)} %bitcast.266), custom_call_target="tpu_custom_call" | custom-call | tf_op jit(solution)/shard_map/mix/pallas_call | solution.py:253
  251.2 20.9 %fusion.2 = bf16[4096,2,1024]{2,0,1:T(8,128)(2,1)} fusion(f32[4096,1024,2]{1,0,2:T(8,128)} %get-tuple-element.109, f32[2,1024]{1,0:T(2,128)S(1)} %log_add_fusion, pred[4096,1024]{1,0:T(8,128)(4,1)S(1)} %copy-done.3), kind=kLoop, calls=%fused_computation.3 | loop fusion | flops 41943040 | bytes 54534144 | tf_op jit(solution)/shard_map/convert_element_type | solution.py:658
  273.0 14.8 %widen.1 = bf16[8,128,1024]{2,1,0:T(8,128)(2,1)} custom-call(bf16[128,1024]{1,0:T(8,128)(2,1)} %multiply_convert_fusion.3.src_ref), custom_call_target="tpu_custom_call" | custom-call | tf_op jit(solution)/shard_map/widen/pallas_call | solution.py:253
  287.8 4.1 copy.111
  291.8 2.9 collective-permute-start.2
  296.9 5.0 collective-permute-done.2
  301.9 2.3 bitcast_dynamic-update-slice_fusion.1
  304.3 1.9 bitcast_dynamic-update-slice_fusion
  308.2 4.5 fusion.99
  312.7 3.3 fusion.17
  316.0 6.7 %convolution_convert_fusion = bf16[1024,1024]{1,0:T(8,128)(2,1)} fusion(bf16[1024,1152]{1,0:T(8,128)(2,1)} %bitcast.42, bf16[1024,576]{0,1:T(8,128)(2,1)S(1)} %get-tuple-element.69, bf16[1024,576]{0,1:T(8,128)(2,1)S(1)} %get-tuple-element.68), kind=kOutput, calls=%fused_computation.35 | convolution fusion | flops 2421686272 | bytes 6815744 | tf_op jit(solution)/shard_map/dot_general | solution.py:472
  322.7 15.1 %narrow.1 = f32[128,1024]{1,0:T(8,128)} custom-call(bf16[8,128,1024]{2,1,0:T(8,128)(2,1)} %bitcast.278), custom_call_target="tpu_custom_call" | custom-call | tf_op jit(solution)/shard_map/narrow/pallas_call | solution.py:253
  341.1 14.9 %spread.1 = bf16[8,128,1024]{2,1,0:T(8,128)(2,1)} custom-call(bf16[128,1024]{1,0:T(8,128)(2,1)} %fusion.94.src_ref), custom_call_target="tpu_custom_call" | custom-call | tf_op jit(solution)/shard_map/spread/pallas_call | solution.py:253
  356.1 2.4 multiply_reduce_fusion.4
  358.5 21.1 %fusion.4 = bf16[2,1024,4096]{1,2,0:T(8,128)(2,1)} fusion(f32[4096,1024,2]{1,0,2:T(8,128)} %get-tuple-element.109, f32[2,1024]{1,0:T(2,128)S(1)} %bitcast.309, f32[2,1024]{1,0:T(2,128)S(1)} %log_add_fusion, pred[1024,4096]{0,1:T(8,128)(4,1)} %broadcast_compare_fusion.1, bf16[4096,64,1]{1,0,2:T(8,128)(2,1)} %bitcast.290, bf16[1024,2,64]{0,2,1:T(8,128)(2,1)S(1)} %bitcast.298), kind=kOutput, calls=%fused_computation.6 | convolution fusion | flops 1132462080 | bytes 55328768 | tf_op jit(solution)/shard_map/qgd,nd->gqn/dot_general | solution.py:659
  379.7 9.0 %fusion.27 = f32[1024,2,64]{0,2,1:T(8,128)S(1)} fusion(bf16[4096,64,1]{1,0,2:T(8,128)(2,1)S(1)} %bitcast.273, bf16[2,1024,4096]{1,2,0:T(8,128)(2,1)} %fusion.4), kind=kOutput, calls=%fused_computation.46 | convolution fusion | flops 1074135040 | bytes 17825792 | tf_op jit(solution)/shard_map/gqn,nd->qgd/dot_general | solution.py:661
  390.2 5.2 fusion.12
  397.2 3.2 convolution_convert_fusion.2
  404.2 3.0 collective-permute-start.11
  407.8 2.9 fusion.18
  412.0 2.2 collective-permute-start.6
  417.4 10.9 %fusion.21 = bf16[4,1024,64]{1,2,0:T(8,128)(2,1)S(1)} fusion(bf16[4,1024,2,1024]{3,1,0,2:T(8,128)(2,1)} %bitcast.263, bf16[1024,2,64,1]{0,2,3,1:T(8,128)(2,1)S(1)} %bitcast.299), kind=kOutput, calls=%fused_computation.41 | convolution fusion | flops 1074003968 | bytes 17563648 | tf_op jit(solution)/shard_map/gqn,qgd->nd/dot_general | solution.py:658
  430.4 58.7 %back.1 = (f32[1024,128]{1,0:T(8,128)}, f32[128,1024]{1,0:T(8,128)}) custom-call(bf16[4,1024,128]{2,1,0:T(8,128)(2,1)} %pad_maximum_fusion.3.dkv_ref, bf16[8,128,1024]{2,1,0:T(8,128)(2,1)} %bitcast.279), custom_call_target="tpu_custom_call" | custom-call | tf_op jit(solution)/shard_map/back/pallas_call | solution.py:253
  491.2 2.2 fusion.54
  500.3 7.4 %collective-permute-start.8 = (bf16[4,64,1152]{2,1,0:T(8,128)(2,1)}, bf16[4,64,1152]{2,1,0:T(8,128)(2,1)S(1)}, u32[]{:S(2)}, u32[]{:S(2)}) collective-permute-start(bf16[4,64,1152]{2,1,0:T(8,128)(2,1)} %get-tuple-element.71), channel_id=1, source_target_pairs={{0,6},{1,7},{2,0},{3,1},{4,2},{5,3},{6,4},{7,5},{8,14},{9,15},{10,... | collective-permute-start | bytes 1769480 | tf_op jit(solution)/shard_map/ppermute | solution.py:467
  507.7 2.2 convolution_convert_fusion.1
  511.4 2.3 fusion.49
  513.7 13.1 %collective-permute-done.8 = bf16[4,64,1152]{2,1,0:T(8,128)(2,1)S(1)} collective-permute-done((bf16[4,64,1152]{2,1,0:T(8,128)(2,1)}, bf16[4,64,1152]{2,1,0:T(8,128)(2,1)S(1)}, u32[]{:S(2)}, u32[]{:S(2)}) %collective-permute-start.8) | collective-permute-done | bytes 589856 | tf_op jit(solution)/shard_map/ppermute | solution.py:467
  526.8 2.7 fusion.30
  529.5 31.9 %last.1 = (f32[128,1024]{1,0:T(8,128)}, f32[8,32,256]{2,1,0:T(8,128)}, bf16[8,32,1152]{2,1,0:T(8,128)(2,1)}) custom-call(bf16[8,128,1024]{2,1,0:T(8,128)(2,1)} %bitcast.269, bf16[4,4,2,32,256]{4,3,2,1,0:T(8,128)(2,1)} %bitcast.297, bf16[8,32,1152]{2,1,0:T(8,128)(2,1)} %bitcast.277), custom_call_target="tpu_custom_call" | custom-call | tf_op jit(solution)/shard_map/last/pallas_call | solution.py:253
  561.4 2.1 slice_convert_fusion
  565.1 2.1 reshape.593
  569.9 2.1 reshape.595
  574.0 10.3 %small.1 = f32[24,128]{1,0:T(8,128)} custom-call(f32[24,128]{1,0:T(8,128)} %pad_bitcast_fusion.v_ref), custom_call_target="tpu_custom_call" | custom-call | tf_op jit(solution)/shard_map/small/pallas_call | solution.py:253
  (284 shorter events, 77.0 us)
Async XLA Ops:
  7.2 584.1 %reduce-scatter.2.cloned.1.call-start = ((), (), s32[]{:S(2)}) async-start(), calls=%async_computation.1 | async-start | bytes 1179648 | tf_op jit(solution)/shard_map/reduce_scatter | solution.py:653
  41.2 11.1 %copy-start.4 = (bf16[8,128,1024]{2,1,0:T(8,128)(2,1)S(1)}, bf16[8,128,1024]{2,1,0:T(8,128)(2,1)}, u32[]{:S(2)}) copy-start(bf16[8,128,1024]{2,1,0:T(8,128)(2,1)} %get-tuple-element.47) | copy-start | bytes 6291460
  41.2 260.7 %collective-permute-start.3 = (bf16[4,64,1152]{2,1,0:T(8,128)(2,1)}, bf16[4,64,1152]{2,1,0:T(8,128)(2,1)}, u32[]{:S(2)}, u32[]{:S(2)}) collective-permute-start(bf16[4,64,1152]{2,1,0:T(8,128)(2,1)} %bitcast.293), channel_id=1, source_target_pairs={{0,2},{1,3},{2,4},{3,5},{4,6},{5,7},{6,0},{7,1},{8,10},{9,11},{10,... | collective-permute-start | bytes 1769480 | tf_op jit(solution)/shard_map/ppermute | solution.py:456
  44.3 260.0 %collective-permute-start.4 = (bf16[4,64,1152]{2,1,0:T(8,128)(2,1)}, bf16[4,64,1152]{2,1,0:T(8,128)(2,1)}, u32[]{:S(2)}, u32[]{:S(2)}) collective-permute-start(bf16[4,64,1152]{2,1,0:T(8,128)(2,1)} %bitcast.294), channel_id=1, source_target_pairs={{0,4},{1,5},{2,6},{3,7},{4,0},{5,1},{6,2},{7,3},{8,12},{9,13},{10,... | collective-permute-start | bytes 1769480 | tf_op jit(solution)/shard_map/ppermute | solution.py:456
  46.7 259.6 %collective-permute-start.5 = (bf16[4,64,1152]{2,1,0:T(8,128)(2,1)}, bf16[4,64,1152]{2,1,0:T(8,128)(2,1)}, u32[]{:S(2)}, u32[]{:S(2)}) collective-permute-start(bf16[4,64,1152]{2,1,0:T(8,128)(2,1)} %bitcast.295), channel_id=1, source_target_pairs={{0,6},{1,7},{2,0},{3,1},{4,2},{5,3},{6,4},{7,5},{8,14},{9,15},{10,... | collective-permute-start | bytes 1769480 | tf_op jit(solution)/shard_map/ppermute | solution.py:456
  46.8 245.1 %collective-permute-start = (bf16[144,1024]{1,0:T(8,128)(2,1)}, bf16[144,1024]{1,0:T(8,128)(2,1)}, u32[]{:S(2)}, u32[]{:S(2)}) collective-permute-start(bf16[144,1024]{1,0:T(8,128)(2,1)} %param.28), channel_id=1, source_target_pairs={{0,2},{1,3},{2,4},{3,5},{4,6},{5,7},{6,0},{7,1},{8,10},{9,11},{10,... | collective-permute-start | bytes 884744 | tf_op jit(solution)/shard_map/ppermute | solution.py:456
  48.7 247.0 %collective-permute-start.1 = (bf16[144,1024]{1,0:T(8,128)(2,1)}, bf16[144,1024]{1,0:T(8,128)(2,1)}, u32[]{:S(2)}, u32[]{:S(2)}) collective-permute-start(bf16[144,1024]{1,0:T(8,128)(2,1)} %param.28), channel_id=1, source_target_pairs={{0,4},{1,5},{2,6},{3,7},{4,0},{5,1},{6,2},{7,3},{8,12},{9,13},{10,... | collective-permute-start | bytes 884744 | tf_op jit(solution)/shard_map/ppermute | solution.py:456
  49.3 18.5 %copy-start.67 = (f32[32]{0:T(128)}, f32[32]{0:T(128)S(1)}, u32[]{:S(2)}) copy-start(f32[32]{0:T(128)S(1)} %multiply_exponential_fusion) | copy-start | bytes 388
  54.2 218.8 %copy-start.6 = (f32[1024,256]{0,1:T(8,128)}, f32[1024,256]{0,1:T(8,128)S(1)}, u32[]{:S(2)}) copy-start(f32[1024,256]{0,1:T(8,128)S(1)} %fusion.98) | copy-start | bytes 3145732
  55.4 12.4 %copy-start.53 = (f32[1024]{0:T(1024)}, f32[1024]{0:T(1024)S(1)}, u32[]{:S(2)}) copy-start(f32[1024]{0:T(1024)S(1)} %get-tuple-element.107) | copy-start | bytes 12292
  63.5 112.0 %copy-start.49 = (f32[1024,2]{0,1:T(2,128)}, f32[1024,2]{0,1:T(2,128)S(1)}, u32[]{:S(2)}) copy-start(f32[1024,2]{0,1:T(2,128)S(1)} %fusion.77) | copy-start | bytes 24580
  63.6 10.3 %copy-start.65 = (f32[64]{0:T(128)}, f32[64]{0:T(128)S(1)}, u32[]{:S(2)}) copy-start(f32[64]{0:T(128)S(1)} %get-tuple-element.105) | copy-start | bytes 772
  63.6 112.0 %copy-start.63 = (f32[64]{0:T(128)}, f32[64]{0:T(128)S(1)}, u32[]{:S(2)}) copy-start(f32[64]{0:T(128)S(1)} %get-tuple-element.104) | copy-start | bytes 772
  65.8 9.8 %copy-start.58 = (f32[1024]{0:T(1024)}, f32[1024]{0:T(1024)S(1)}, u32[]{:S(2)}) copy-start(f32[1024]{0:T(1024)S(1)} %multiply_reduce_fusion.8) | copy-start | bytes 12292
  65.8 9.8 %copy-start.55 = (f32[1024]{0:T(1024)}, f32[1024]{0:T(1024)S(1)}, u32[]{:S(2)}) copy-start(f32[1024]{0:T(1024)S(1)} %fusion.78) | copy-start | bytes 12292
  66.4 109.3 %copy-start.30 = (f32[1024,32]{0,1:T(8,128)}, f32[1024,32]{0,1:T(8,128)S(1)}, u32[]{:S(2)}) copy-start(f32[1024,32]{0,1:T(8,128)S(1)} %get-tuple-element.100) | copy-start | bytes 393220
  66.4 109.3 %copy-start.32 = (f32[1024,32]{0,1:T(8,128)}, f32[1024,32]{0,1:T(8,128)S(1)}, u32[]{:S(2)}) copy-start(f32[1024,32]{0,1:T(8,128)S(1)} %get-tuple-element.101) | copy-start | bytes 393220
  75.6 63.2 %copy-start.57 = (bf16[32,1024]{1,0:T(8,128)(2,1)S(1)}, bf16[32,1024]{1,0:T(8,128)(2,1)}, u32[]{:S(2)}) copy-start(bf16[32,1024]{1,0:T(8,128)(2,1)} %param.24) | copy-start | bytes 196612
  175.8 16.1 %copy-start.39 = (bf16[1024,2,32]{0,2,1:T(8,128)(2,1)}, bf16[1024,2,32]{0,2,1:T(8,128)(2,1)S(1)}, u32[]{:S(2)}) copy-start(bf16[1024,2,32]{0,2,1:T(8,128)(2,1)S(1)} %get-tuple-element.81) | copy-start | bytes 393220
  175.8 16.1 %copy-start.41 = (bf16[1024,2,32]{0,2,1:T(8,128)(2,1)}, bf16[1024,2,32]{0,2,1:T(8,128)(2,1)S(1)}, u32[]{:S(2)}) copy-start(bf16[1024,2,32]{0,2,1:T(8,128)(2,1)S(1)} %get-tuple-element.82) | copy-start | bytes 393220
  175.8 16.1 %copy-start.5 = (pred[1024,4096]{0,1:T(8,128)(4,1)S(1)}, pred[1024,4096]{0,1:T(8,128)(4,1)}, u32[]{:S(2)}) copy-start(pred[1024,4096]{0,1:T(8,128)(4,1)} %broadcast_compare_fusion.1) | copy-start | bytes 12582916
  224.7 17.8 %copy-start.14 = (bf16[128,1024]{1,0:T(8,128)(2,1)S(1)}, bf16[128,1024]{1,0:T(8,128)(2,1)}, u32[]{:S(2)}) copy-start(bf16[128,1024]{1,0:T(8,128)(2,1)} %x_ref.1) | copy-start | bytes 786436
  251.2 20.9 %copy-start.8 = (f32[128,1024]{1,0:T(8,128)S(1)}, f32[128,1024]{1,0:T(8,128)}, u32[]{:S(2)}) copy-start(f32[128,1024]{1,0:T(8,128)} %get-tuple-element.67) | copy-start | bytes 1572868
  291.8 10.1 %collective-permute-start.2 = (bf16[144,1024]{1,0:T(8,128)(2,1)}, bf16[144,1024]{1,0:T(8,128)(2,1)S(1)}, u32[]{:S(2)}, u32[]{:S(2)}) collective-permute-start(bf16[144,1024]{1,0:T(8,128)(2,1)} %param.28), channel_id=1, source_target_pairs={{0,6},{1,7},{2,0},{3,1},{4,2},{5,3},{6,4},{7,5},{8,14},{9,15},{10,... | collective-permute-start | bytes 884744 | tf_op jit(solution)/shard_map/ppermute | solution.py:456
  295.7 12.4 %copy-start.10 = (bf16[8,128,1024]{2,1,0:T(8,128)(2,1)S(1)}, bf16[8,128,1024]{2,1,0:T(8,128)(2,1)}, u32[]{:S(2)}) copy-start(bf16[8,128,1024]{2,1,0:T(8,128)(2,1)} %widen.1) | copy-start | bytes 6291460
  301.9 10.7 %copy-start.28 = (bf16[4,144,1024]{2,1,0:T(8,128)(2,1)}, bf16[4,144,1024]{2,1,0:T(8,128)(2,1)S(1)}, u32[]{:S(2)}) copy-start(bf16[4,144,1024]{2,1,0:T(8,128)(2,1)S(1)} %bitcast_dynamic-update-slice_fusion.3) | copy-start | bytes 3538948
  322.7 16.5 %copy-start.17 = (bf16[128,1024]{1,0:T(8,128)(2,1)S(1)}, bf16[128,1024]{1,0:T(8,128)(2,1)}, u32[]{:S(2)}) copy-start(bf16[128,1024]{1,0:T(8,128)(2,1)} %og_ref.1) | copy-start | bytes 786436
  337.9 18.2 %copy-start.34 = (bf16[256,1024]{1,0:T(8,128)(2,1)S(1)}, bf16[256,1024]{1,0:T(8,128)(2,1)}, u32[]{:S(2)}) copy-start(bf16[256,1024]{1,0:T(8,128)(2,1)} %all_gather.3) | copy-start | bytes 1572868
  337.9 18.2 %copy-start.35 = (bf16[1024,2,64]{0,2,1:T(8,128)(2,1)S(1)}, bf16[1024,2,64]{0,2,1:T(8,128)(2,1)}, u32[]{:S(2)}) copy-start(bf16[1024,2,64]{0,2,1:T(8,128)(2,1)} %fusion.34) | copy-start | bytes 786436
  358.5 21.1 %copy-start.47 = (bf16[1024,128]{0,1:T(8,128)(2,1)}, bf16[1024,128]{0,1:T(8,128)(2,1)S(1)}, u32[]{:S(2)}) copy-start(bf16[1024,128]{0,1:T(8,128)(2,1)S(1)} %get-tuple-element.111) | copy-start | bytes 786436
  358.5 21.1 %copy-start.13 = (bf16[4,1024,64]{2,1,0:T(8,128)(2,1)S(1)}, bf16[4,1024,64]{2,1,0:T(8,128)(2,1)}, u32[]{:S(2)}) copy-start(bf16[4,1024,64]{2,1,0:T(8,128)(2,1)} %get-tuple-element.77) | copy-start | bytes 1572868
  379.7 10.5 %copy-start.2 = (bf16[2,1024,4096]{1,2,0:T(8,128)(2,1)S(1)}, bf16[2,1024,4096]{1,2,0:T(8,128)(2,1)}, u32[]{:S(2)}) copy-start(bf16[2,1024,4096]{1,2,0:T(8,128)(2,1)} %fusion.4) | copy-start | bytes 50331652
  379.7 10.5 %copy-start.40 = (bf16[1024,2,32]{0,2,1:T(8,128)(2,1)S(1)}, bf16[1024,2,32]{0,2,1:T(8,128)(2,1)}, u32[]{:S(2)}) copy-start(bf16[1024,2,32]{0,2,1:T(8,128)(2,1)} %copy-done.39) | copy-start | bytes 393220
  379.7 10.5 %copy-start.42 = (bf16[1024,2,32]{0,2,1:T(8,128)(2,1)S(1)}, bf16[1024,2,32]{0,2,1:T(8,128)(2,1)}, u32[]{:S(2)}) copy-start(bf16[1024,2,32]{0,2,1:T(8,128)(2,1)} %copy-done.41) | copy-start | bytes 393220
  403.0 97.3 %collective-permute-start.10 = (bf16[144,1024]{1,0:T(8,128)(2,1)}, bf16[144,1024]{1,0:T(8,128)(2,1)}, u32[]{:S(2)}, u32[]{:S(2)}) collective-permute-start(bf16[144,1024]{1,0:T(8,128)(2,1)} %get-tuple-element.76), channel_id=1, source_target_pairs={{0,4},{1,5},{2,6},{3,7},{4,0},{5,1},{6,2},{7,3},{8,12},{9,13},{10,... | collective-permute-start | bytes 884744 | tf_op jit(solution)/shard_map/ppermute | solution.py:467
  404.2 107.2 %collective-permute-start.11 = (bf16[144,1024]{1,0:T(8,128)(2,1)}, bf16[144,1024]{1,0:T(8,128)(2,1)}, u32[]{:S(2)}, u32[]{:S(2)}) collective-permute-start(bf16[144,1024]{1,0:T(8,128)(2,1)} %get-tuple-element.75), channel_id=1, source_target_pairs={{0,6},{1,7},{2,0},{3,1},{4,2},{5,3},{6,4},{7,5},{8,14},{9,15},{10,... | collective-permute-start | bytes 884744 | tf_op jit(solution)/shard_map/ppermute | solution.py:467
  407.2 104.2 %collective-permute-start.9 = (bf16[144,1024]{1,0:T(8,128)(2,1)}, bf16[144,1024]{1,0:T(8,128)(2,1)}, u32[]{:S(2)}, u32[]{:S(2)}) collective-permute-start(bf16[144,1024]{1,0:T(8,128)(2,1)} %get-tuple-element.74), channel_id=1, source_target_pairs={{0,2},{1,3},{2,4},{3,5},{4,6},{5,7},{6,0},{7,1},{8,10},{9,11},{10,... | collective-permute-start | bytes 884744 | tf_op jit(solution)/shard_map/ppermute | solution.py:467
  412.0 101.7 %collective-permute-start.6 = (bf16[4,64,1152]{2,1,0:T(8,128)(2,1)}, bf16[4,64,1152]{2,1,0:T(8,128)(2,1)}, u32[]{:S(2)}, u32[]{:S(2)}) collective-permute-start(bf16[4,64,1152]{2,1,0:T(8,128)(2,1)} %get-tuple-element.70), channel_id=1, source_target_pairs={{0,2},{1,3},{2,4},{3,5},{4,6},{5,7},{6,0},{7,1},{8,10},{9,11},{10,... | collective-permute-start | bytes 1769480 | tf_op jit(solution)/shard_map/ppermute | solution.py:467
  414.2 99.5 %collective-permute-start.7 = (bf16[4,64,1152]{2,1,0:T(8,128)(2,1)}, bf16[4,64,1152]{2,1,0:T(8,128)(2,1)}, u32[]{:S(2)}, u32[]{:S(2)}) collective-permute-start(bf16[4,64,1152]{2,1,0:T(8,128)(2,1)} %get-tuple-element.72), channel_id=1, source_target_pairs={{0,4},{1,5},{2,6},{3,7},{4,0},{5,1},{6,2},{7,3},{8,12},{9,13},{10,... | collective-permute-start | bytes 1769480 | tf_op jit(solution)/shard_map/ppermute | solution.py:467
  430.4 60.7 %copy-start.54 = (f32[1024]{0:T(1024)S(1)}, f32[1024]{0:T(1024)}, u32[]{:S(2)}) copy-start(f32[1024]{0:T(1024)} %copy-done.53) | copy-start | bytes 12292
  430.4 60.7 %copy-start.68 = (f32[32]{0:T(128)S(1)}, f32[32]{0:T(128)}, u32[]{:S(2)}) copy-start(f32[32]{0:T(128)} %copy-done.67) | copy-start | bytes 388
  495.4 12.3 %copy-start.22 = (bf16[4,4,2,32,256]{4,3,2,1,0:T(8,128)(2,1)S(1)}, bf16[4,4,2,32,256]{4,3,2,1,0:T(8,128)(2,1)}, u32[]{:S(2)}) copy-start(bf16[4,4,2,32,256]{4,3,2,1,0:T(8,128)(2,1)} %get-tuple-element.49) | copy-start | bytes 1572868
  500.3 26.6 %collective-permute-start.8 = (bf16[4,64,1152]{2,1,0:T(8,128)(2,1)}, bf16[4,64,1152]{2,1,0:T(8,128)(2,1)S(1)}, u32[]{:S(2)}, u32[]{:S(2)}) collective-permute-start(bf16[4,64,1152]{2,1,0:T(8,128)(2,1)} %get-tuple-element.71), channel_id=1, source_target_pairs={{0,6},{1,7},{2,0},{3,1},{4,2},{5,3},{6,4},{7,5},{8,14},{9,15},{10,... | collective-permute-start | bytes 1769480 | tf_op jit(solution)/shard_map/ppermute | solution.py:467
  569.9 19.7 %copy-start.38 = (f32[8,32,256]{2,1,0:T(8,128)S(1)}, f32[8,32,256]{2,1,0:T(8,128)}, u32[]{:S(2)}) copy-start(f32[8,32,256]{2,1,0:T(8,128)} %get-tuple-element.56) | copy-start | bytes 786436
  569.9 20.4 %copy-start.12 = (f32[128,1024]{1,0:T(8,128)S(1)}, f32[128,1024]{1,0:T(8,128)}, u32[]{:S(2)}) copy-start(f32[128,1024]{1,0:T(8,128)} %narrow.1) | copy-start | bytes 1572868
  569.9 20.4 %copy-start.18 = (bf16[128,1024]{1,0:T(8,128)(2,1)S(1)}, bf16[128,1024]{1,0:T(8,128)(2,1)}, u32[]{:S(2)}) copy-start(bf16[128,1024]{1,0:T(8,128)(2,1)} %og_ref.1) | copy-start | bytes 786436
  569.9 20.4 %copy-start.24 = (f32[128,1024]{1,0:T(8,128)S(1)}, f32[128,1024]{1,0:T(8,128)}, u32[]{:S(2)}) copy-start(f32[128,1024]{1,0:T(8,128)} %get-tuple-element.55) | copy-start | bytes 1572868
  572.0 18.3 %copy-start.45 = (f32[128,1024]{1,0:T(8,128)S(1)}, f32[128,1024]{1,0:T(8,128)}, u32[]{:S(2)}) copy-start(f32[128,1024]{1,0:T(8,128)} %get-tuple-element.53) | copy-start | bytes 1572868
  (46 other events, 208.1 us)
Sparse Core Ops, SparseCore 0:
  500.2 72.1 reduce-scatter.1

commit v2 on v1

--- a/solution.py
+++ b/solution.py
@@ -10,7 +10,6 @@
 
 EPS = 1e-05
 THETA = 1000000.0
-NEG = -1e30
 CORES = 2
 INNER = 2
 MESH = pl.DeviceIdType.MESH
@@ -69,27 +68,23 @@
         self.used += count
         return first
 
-    def send(self, slot, src, dst, dev):
-        copy = pltpu.make_async_remote_copy(
+    def copy(self, slot, src, dst, dev, landing=None):
+        return pltpu.make_async_remote_copy(
             src_ref=src,
             dst_ref=dst,
             send_sem=self.sends.at[slot],
-            recv_sem=self.recvs.at[slot],
+            recv_sem=self.recvs.at[slot if landing is None else landing],
             device_id=dev,
             device_id_type=MESH,
         )
+
+    def send(self, slot, src, dst, dev, landing=None):
+        copy = self.copy(slot, src, dst, dev, landing)
         copy.start()
         self.open.append(copy)
 
     def arrive(self, slot, dst, dev):
-        pltpu.make_async_remote_copy(
-            src_ref=dst,
-            dst_ref=dst,
-            send_sem=self.sends.at[slot],
-            recv_sem=self.recvs.at[slot],
-            device_id=dev,
-            device_id_type=MESH,
-        ).wait_recv()
+        self.copy(slot, dst, dst, dev).wait_recv()
 
     def close(self):
         for copy in self.open:
@@ -248,6 +243,122 @@
             self.mail.arrive(self.base + slot, self.out.at[other], dev)
 
 
+def blk_peers(place):
+    y, c, z, x = place
+    outer = lax.axis_size("blk") // INNER
+    others = [device(y, c, lax.rem(z + k, outer), 1 - x) for k in range(1, outer)]
+    return [p[0] for p in line_peers(place)] + others
+
+
+class RowsOut:
+    def __init__(self, mail, place, src, out):
+        self.mail, self.place, self.src, self.out = mail, place, src, out
+        self.outer = lax.axis_size("blk") // INNER
+        self.per = self.outer // INNER
+        self.base = mail.take(self.outer)
+
+    def first(self):
+        y, c, z, x = self.place
+        return self.mail.copy(
+            self.base,
+            self.src,
+            self.out.at[lax.rem(z, self.per), x],
+            device(y, c, z, 1 - x),
+            self.base + lax.rem(z, self.per) * INNER + x,
+        )
+
+    def begin(self):
+        y, c, z, x = self.place
+        to = z // self.per
+        landing = self.base + lax.rem(z, self.per) * INNER + x
+        place_there = self.out.at[lax.rem(z, self.per), x]
+
+        @pl.when(to != x)
+        def _():
+            self.first().start()
+
+        @pl.when(to == x)
+        def _():
+            self.out[lax.rem(z, self.per), x] = self.src[...]
+
+        for k in range(1, self.outer):
+            dev = device(y, c, lax.rem(z + k, self.outer), to)
+            self.mail.send(self.base + k, self.src, place_there, dev, landing)
+
+    def end(self):
+        y, c, z, x = self.place
+
+        @pl.when(z // self.per != x)
+        def _():
+            self.first().wait_send()
+
+        for j in range(self.per):
+            for ox in range(INNER):
+                oz = x * self.per + j
+                own = (oz == z) & (x * 0 + ox == x)
+
+                @pl.when(jnp.logical_not(own))
+                def _():
+                    self.mail.arrive(
+                        self.base + j * INNER + ox, self.out.at[j, ox], device(y, c, oz, ox)
+                    )
+
+
+class RowsBack:
+    def __init__(self, mail, place, parts, got, out):
+        self.mail, self.place, self.parts, self.got, self.out = mail, place, parts, got, out
+        self.outer = lax.axis_size("blk") // INNER
+        self.per = self.outer // INNER
+        self.base = mail.take(self.outer)
+
+    def copies(self):
+        y, c, z, x = self.place
+        for j in range(self.per):
+            for ox in range(INNER):
+                oz = x * self.per + j
+                own = (oz == z) & (x * 0 + ox == x)
+                copy = self.mail.copy(
+                    self.base + j * INNER + ox,
+                    self.parts.at[j, ox],
+                    self.got.at[z],
+                    device(y, c, oz, ox),
+                    self.base + z,
+                )
+                yield j, ox, own, copy
+
+    def begin(self):
+        y, c, z, x = self.place
+        for j, ox, own, copy in self.copies():
+
+            @pl.when(own)
+            def _():
+                self.got[z] = self.parts[j, ox]
+
+            @pl.when(jnp.logical_not(own))
+            def _():
+                copy.start()
+
+    def end(self):
+        y, c, z, x = self.place
+        for j, ox, own, copy in self.copies():
+
+            @pl.when(jnp.logical_not(own))
+            def _():
+                copy.wait_send()
+
+        to = z // self.per
+        for oz in range(self.outer):
+
+            @pl.when(jnp.logical_not((z == oz) & (to == x)))
+            def _():
+                self.mail.arrive(self.base + oz, self.got.at[oz], device(y, c, z * 0 + oz, to))
+
+        total = self.got[0].astype(F32)
+        for oz in range(1, self.outer):
+            total = total + self.got[oz].astype(F32)
+        self.out[...] = total
+
+
 def call(body, name, ident, outs, args, copies, scratch=()):
     spec = pl.BlockSpec(memory_space=pltpu.VMEM)
     return pl.pallas_call(
@@ -267,13 +378,15 @@
     )(*args)
 
 
-def start_kernel(x_ref, w_ref, g_ref, gu_ref, xp_ref, wq_ref, gain_ref, gus_ref, ss, rs):
+def start_kernel(
+    x_ref, w_ref, g_ref, gu_ref, wo_ref, xp_ref, wq_ref, gain_ref, gus_ref, wos_ref, ss, rs
+):
     place = y, c, z, x = here()
     me = rank(y, c, x)
     head = y * CORES + c
     mail = Mail((ss, rs))
     peers, line = plane_peers(place), line_peers(place)
-    greet([p[0] for p in peers] + [p[0] for p in line])
+    greet([p[0] for p in peers] + blk_peers(place))
     w_base, g_base = mail.take(7), mail.take(7)
     zw_base, zg_base = mail.take(len(line)), mail.take(len(line))
     for slot, (dev, other, _) in enumerate(peers):
@@ -283,7 +396,9 @@
     wq_ref[head, z, x] = w_ref[me]
     rows = PlaneGather(mail, place, x_ref, xp_ref)
     swap = PlaneSwap(mail, place, gu_ref, gus_ref)
+    block = RowsOut(mail, place, wo_ref, wos_ref)
     rows.begin()
+    block.begin()
     for slot, (dev, other, (oh, ox)) in enumerate(peers):
         mail.arrive(g_base + slot, gain_ref.at[z, other], dev)
         mail.arrive(w_base + slot, wq_ref.at[oh, z, ox], dev)
@@ -296,6 +411,7 @@
     for slot, (dev, _, back) in enumerate(line):
         mail.arrive(zg_base + slot, gain_ref.at[back], dev)
         mail.arrive(zw_base + slot, wq_ref.at[:, back], dev)
+    block.end()
     swap.end()
     mail.close()
 
@@ -340,16 +456,19 @@
     mail.close()
 
 
-def back_kernel(dkv_ref, parts_ref, kv_ref, out_ref, ss, rs, got, *bufs):
+def back_kernel(dkv_ref, parts_ref, op_ref, kv_ref, out_ref, ops_ref, ss, rs, got, op_got, *bufs):
     place = y, c, z, x = here()
     mail = Mail((ss, rs))
     line = line_peers(place)
-    greet([p[0] for p in line] + list(near(place)))
+    pair, xn, yn = near(place)
+    greet(blk_peers(place) + [pair, xn, yn])
     base = mail.take(len(line))
     for slot, (dev, forth, _) in enumerate(line):
         mail.send(base + slot, dkv_ref.at[forth], got.at[slot], dev)
     rows = PlaneScatter(mail, place, parts_ref, out_ref, bufs)
+    block = RowsBack(mail, place, op_ref, op_got, ops_ref)
     rows.begin()
+    block.begin()
     rows.middle()
     rows.end()
     total = dkv_ref[z].astype(F32)
@@ -357,6 +476,7 @@
         mail.arrive(base + slot, got.at[slot], dev)
         total = total + got[slot].astype(F32)
     kv_ref[...] = total
+    block.end()
     mail.close()
 
 
@@ -411,6 +531,159 @@
     mail.close()
 
 
+SPANS = 4
+LOG2E = math.log2(math.e)
+NT = (((1,), (1,)), ((), ()))
+
+
+def lanes(shape):
+    return lax.broadcasted_iota(jnp.int32, shape, len(shape) - 1)
+
+
+def stack_left(block, size):
+    wide = block.astype(F32)
+    left = lanes(wide.shape) < size
+    first = jnp.where(left, wide, 0.0)
+    second = jnp.where(left, pltpu.roll(wide, size, 1), 0.0)
+    return jnp.concatenate([first, second], axis=0).astype(BF16)
+
+
+def stack_right(block, size):
+    wide = block.astype(F32)
+    right = lanes(wide.shape) >= size
+    first = jnp.where(right, pltpu.roll(wide, size, 1), 0.0)
+    second = jnp.where(right, wide, 0.0)
+    return jnp.concatenate([first, second], axis=0).astype(BF16)
+
+
+def forward_kernel(own_ref, at_ref, q_ref, kv_ref, out_ref, lse_ref, keys, ones):
+    count, rows, size2 = q_ref.shape
+    size = size2 // 2
+    scale = float(size) ** (-0.5) * LOG2E
+    step = SPANS * rows
+
+    def place_rows(p, carry):
+        block = kv_ref[at_ref[p]]
+        keys[pl.ds(p * rows, rows)] = block
+        ones[pl.ds(p * rows, rows)] = jnp.where(lanes(block.shape) < size, 1.0, block).astype(BF16)
+        return carry
+
+    lax.fori_loop(0, kv_ref.shape[0], place_rows, 0)
+
+    def one_block(r, carry):
+        place = own_ref[r]
+        queries = stack_left(q_ref[r], size)
+
+        def weights(c):
+            part = keys[pl.ds(c * step, step)]
+            scores = lax.dot_general(queries, part, NT, preferred_element_type=F32)
+            return jnp.exp2(scores * scale)
+
+        def mix(c, held, total):
+            part = ones[pl.ds(c * step, step)]
+            return total + jnp.dot(held.astype(BF16), part, preferred_element_type=F32)
+
+        def full(c, total):
+            return mix(c, weights(c), total)
+
+        last = place // SPANS
+        total = lax.fori_loop(0, last, full, jnp.zeros((2 * rows, size2), F32))
+        held = weights(last)
+        row = lax.broadcasted_iota(jnp.int32, held.shape, 0)
+        row = jnp.where(row >= rows, row - rows, row) + (place - last * SPANS) * rows
+        held = jnp.where(lanes(held.shape) <= row, held, 0.0)
+        total = mix(last, held, total)
+        divided = total / total[:, :1]
+        left = lanes((rows, size2)) < size
+        out_ref[r] = jnp.where(left, pltpu.roll(divided[:rows], size, 1), divided[rows:]).astype(
+            BF16
+        )
+        lse_ref[r] = jnp.log2(total.T[:8])
+        return carry
+
+    lax.fori_loop(0, count, one_block, 0)
+
+
+def backward_kernel(
+    own_ref, at_ref, q_ref, kv_ref, out_ref, do_ref, lse_ref, dq_ref, dkv_ref, keys, turned, sums
+):
+    count, rows, size2 = q_ref.shape
+    size = size2 // 2
+    scale = float(size) ** (-0.5)
+    step = SPANS * rows
+    spans = kv_ref.shape[0]
+
+    def place_rows(p, carry):
+        block = kv_ref[at_ref[p]]
+        keys[pl.ds(p * rows, rows)] = block
+        turned[:, pl.ds(p * rows, rows)] = block.astype(F32).T.astype(BF16)
+        return carry
+
+    lax.fori_loop(0, spans, place_rows, 0)
+    sums[...] = jnp.zeros_like(sums)
+
+    def one_block(r, carry):
+        place = own_ref[r]
+        queries = stack_left(q_ref[r], size)
+        grads = stack_right(do_ref[r], size)
+        both = (do_ref[r].astype(F32) * out_ref[r].astype(F32)).T
+        delta = jnp.concatenate(
+            [jnp.sum(both[:size], axis=0)[None], jnp.sum(both[size:], axis=0)[None]], axis=1
+        )
+        lse = lse_ref[r][:1]
+
+        def one_step(c, total, masked):
+            at = pl.ds(pl.multiple_of(c * step, step), step)
+            part = keys[at]
+            scores = lax.dot_general(part, queries, NT, preferred_element_type=F32)
+            prob = jnp.exp2(scores * (scale * LOG2E) - lse)
+            if masked:
+                key = lax.broadcasted_iota(jnp.int32, prob.shape, 0)
+                row = lanes(prob.shape)
+                row = jnp.where(row >= rows, row - rows, row) + (place - c * SPANS) * rows
+                prob = jnp.where(key <= row, prob, 0.0)
+            dprob = lax.dot_general(part, grads, NT, preferred_element_type=F32)
+            dscore = (prob * (dprob - delta)).astype(BF16)
+            sums[at] += jnp.dot(dscore, queries, preferred_element_type=F32) + jnp.dot(
+                prob.astype(BF16), grads, preferred_element_type=F32
+            )
+            return total + jnp.dot(turned[:, at], dscore, preferred_element_type=F32)
+
+        last = place // SPANS
+        total = lax.fori_loop(
+            0, last, lambda c, t: one_step(c, t, False), jnp.zeros((size2, 2 * rows), F32)
+        )
+        total = one_step(last, total, True).T * scale
+        left = lanes((rows, size2)) < size
+        dq_ref[r] = jnp.where(left, total[:rows], pltpu.roll(total[rows:], size, 1)).astype(BF16)
+        return carry
+
+    lax.fori_loop(0, count, one_block, 0)
+
+    def give_rows(p, carry):
+        block = sums[pl.ds(p * rows, rows)]
+        factor = jnp.where(lanes(block.shape) < size, scale, 1.0)
+        dkv_ref[at_ref[p]] = (block * factor).astype(BF16)
+        return carry
+
+    lax.fori_loop(0, spans, give_rows, 0)
+
+
+def attention(body, name, own, at, args, outs, scratch, flops):
+    vmem = pl.BlockSpec(memory_space=pltpu.VMEM)
+    smem = pl.BlockSpec(memory_space=pltpu.SMEM)
+    return pl.pallas_call(
+        body,
+        name=name,
+        out_shape=tuple(jax.ShapeDtypeStruct(shape, dtype) for shape, dtype in outs),
+        in_specs=[smem, smem] + [vmem] * len(args),
+        out_specs=tuple([vmem] * len(outs)),
+        scratch_shapes=scratch,
+        cost_estimate=pl.CostEstimate(flops=flops, bytes_accessed=4 << 20, transcendentals=0),
+        compiler_params=pltpu.CompilerParams(vmem_limit_bytes=60 * 1024 * 1024),
+    )(own, at, *args)
+
+
 def rms_norm(values, gain_vec):
     inverse = lax.rsqrt(jnp.mean(values * values, axis=-1, keepdims=True) + EPS)
     return values * inverse * gain_vec
@@ -492,25 +765,21 @@
     outer = blocks // INNER
     plane = heads * INNER
     z = lax.axis_index("blk") // INNER
-    x_at = lax.axis_index("blk") % INNER
     rows, width = block_input.shape
     head_size = qk_gain.shape[1]
     w_rows = w_query.shape[0]
     f_rows = w_down.shape[0]
     q_cols = w_query.shape[1] // plane
     k_cols = key_weight.shape[1] // plane
-    share = q_cols // k_cols
     a_cols = q_cols + 2 * k_cols
     ff = f_rows * outer
     tokens = plane * rows
-    score_scale = float(head_size) ** (-0.5)
 
     by_place = span_order.reshape(heads, outer, INNER)
     own_spans = lax.dynamic_index_in_dim(by_place, z, 1, keepdims=False).reshape(plane)
     all_spans = by_place.transpose(1, 0, 2).reshape(outer * plane)
     inside = jnp.arange(rows, dtype=jnp.int32)
     tok_where = (own_spans[:, None] * rows + inside[None, :]).reshape(tokens)
-    key_where = (all_spans[:, None] * rows + inside[None, :]).reshape(outer * tokens)
 
     w8 = jnp.concatenate(
         [
@@ -529,10 +798,9 @@
     gains = jnp.zeros((16, 128), BF16)
     gains = gains.at[0, :w_rows].set(norm1_gain).at[1, :w_rows].set(norm2_gain)
     down_full = line_gather(w_down, 0, (outer, f_rows, width), z, outer).reshape(ff, width)
-    out_all = lax.all_gather(w_out, "blk", axis=0, tiled=True)
 
     n_line = outer - 1
-    x_all, wqkv, gains_all, gu_piece = call(
+    x_all, wqkv, gains_all, gu_piece, out_mine = call(
         start_kernel,
         "start",
         1,
@@ -541,10 +809,12 @@
             ((heads, outer, INNER, w_rows, a_cols), BF16),
             ((outer, plane, 16, 128), BF16),
             ((plane, w_rows, 2 * ff), BF16),
+            ((outer // INNER, INNER, w_rows, width), BF16),
         ],
-        (block_input, w8, gains, gu8),
-        14 + 2 * n_line + PlaneGather.COPIES + PlaneSwap.COPIES,
-    )
+        (block_input, w8, gains, gu8, w_out),
+        14 + 2 * n_line + PlaneGather.COPIES + PlaneSwap.COPIES + outer,
+    )
+    out_mine = out_mine.reshape(q_cols, width)
     wqkv = wqkv.reshape(width, a_cols)
     gains_all = (
         gains_all[:, :, :2, :w_rows]
@@ -583,21 +853,28 @@
         n_line + PlaneGather.COPIES,
     )
     og_all = og_all.reshape(tokens, width)
-    k_all = kv_all[:, :, :k_cols].reshape(outer * tokens, k_cols)
-    v_all = kv_all[:, :, k_cols:].reshape(outer * tokens, k_cols)
-    q_three = queries.reshape(tokens, share, head_size)
-    causal = key_where[None, :] <= tok_where[:, None]
-    scores = jnp.einsum("qgd,nd->gqn", q_three, k_all, preferred_element_type=F32) * score_scale
-    scores = jnp.where(causal, scores, NEG)
-    row_max = jnp.max(scores, axis=-1)
-    weights = jnp.where(causal, jnp.exp(scores - row_max[..., None]), 0.0)
-    row_sum = jnp.sum(weights, axis=-1)
-    mixed = jnp.einsum("gqn,nd->qgd", weights.astype(BF16), v_all, preferred_element_type=F32)
-    attended3 = (mixed / row_sum.T[..., None]).astype(BF16)
-    log_total = row_max + jnp.log(row_sum)
-    attended = attended3.reshape(tokens, q_cols)
-
-    out_mine = lax.dynamic_slice_in_dim(out_all, x_at * q_cols, q_cols, 0)
+    spans = outer * plane
+    span_at = jnp.sum(
+        jnp.where(
+            all_spans[:, None] == jnp.arange(spans, dtype=jnp.int32)[None, :],
+            jnp.arange(spans, dtype=jnp.int32)[:, None],
+            0,
+        ),
+        axis=0,
+    )
+    q_blocks = queries.reshape(plane, rows, q_cols)
+    kv_blocks = kv_all.reshape(spans, rows, q_cols)
+    attended, log_total = attention(
+        forward_kernel,
+        "attend",
+        own_spans,
+        span_at,
+        (q_blocks, kv_blocks),
+        [((plane, rows, q_cols), BF16), ((plane, 8, 2 * rows), F32)],
+        [pltpu.VMEM((spans * rows, q_cols), BF16), pltpu.VMEM((spans * rows, q_cols), BF16)],
+        8 * tokens * spans * rows * q_cols,
+    )
+    attended_rows = attended.reshape(tokens, q_cols)
 
     def scatter(parts, name, ident):
         return call(
@@ -621,7 +898,7 @@
         )[0].reshape(tokens, width)
 
     in_flat = block_input.astype(F32)
-    middle = in_flat + scatter(dot(attended, out_mine), "mix", 3)
+    middle = in_flat + scatter(dot(attended_rows, out_mine), "mix", 3)
     normed2_own = rms_norm(middle, gain_two).astype(BF16)
     normed2 = gather(normed2_own, "widen", 4)
 
@@ -646,33 +923,42 @@
     dmiddle = out_grad.astype(F32) + dmiddle_norm
     dmid_all = gather(dmiddle.astype(BF16), "spread", 6)
 
-    out_proj = dot(attended.T, dmid_all)
-    out_proj = jnp.where(
-        (jnp.arange(INNER) == x_at)[:, None, None], out_proj[None], 0.0
-    ).reshape(INNER * q_cols, width)
-    out_proj_grad = lax.psum_scatter(out_proj, "blk", scatter_dimension=0, tiled=True)
+    out_proj = dot(attended_rows.T, dmid_all)
     dattended = dot(dmid_all, out_mine.T).astype(BF16)
-    grad_three = dattended.reshape(tokens, share, head_size)
-    delta = jnp.sum(grad_three.astype(F32) * attended3.astype(F32), axis=-1).T
-    prob = jnp.where(causal, jnp.exp(scores - log_total[..., None]), 0.0)
-    dvalues = jnp.einsum("gqn,qgd->nd", prob.astype(BF16), grad_three, preferred_element_type=F32)
-    dprob = jnp.einsum("qgd,nd->gqn", grad_three, v_all, preferred_element_type=F32)
-    dscore = (prob * (dprob - delta[..., None])).astype(BF16)
-    dqueries = jnp.einsum("gqn,nd->qgd", dscore, k_all, preferred_element_type=F32) * score_scale
-    dkeys = jnp.einsum("gqn,qgd->nd", dscore, q_three, preferred_element_type=F32) * score_scale
-    dkv = jnp.concatenate([dkeys, dvalues], axis=-1).astype(BF16)
-    dkv_own, ffn_out = call(
+    dqueries, dkv = attention(
+        backward_kernel,
+        "attend_back",
+        own_spans,
+        span_at,
+        (q_blocks, kv_blocks, attended, dattended.reshape(plane, rows, q_cols), log_total),
+        [((plane, rows, q_cols), BF16), ((spans, rows, q_cols), BF16)],
+        [
+            pltpu.VMEM((spans * rows, q_cols), BF16),
+            pltpu.VMEM((q_cols, spans * rows), BF16),
+            pltpu.VMEM((spans * rows, q_cols), F32),
+        ],
+        20 * tokens * spans * rows * q_cols,
+    )
+    dkv_own, ffn_out, out_proj_grad = call(
         back_kernel,
         "back",
         7,
-        [((tokens, 2 * k_cols), F32), ((rows, width), F32)],
-        (dkv.reshape(outer, tokens, 2 * k_cols), out_parts),
-        n_line + PlaneScatter.COPIES,
-        [pltpu.VMEM((n_line, tokens, 2 * k_cols), BF16)] + PlaneScatter.scratch(rows, width),
+        [((tokens, 2 * k_cols), F32), ((rows, width), F32), ((w_rows, width), F32)],
+        (
+            dkv.reshape(outer, tokens, 2 * k_cols),
+            out_parts,
+            out_proj.astype(BF16).reshape(outer // INNER, INNER, w_rows, width),
+        ),
+        n_line + PlaneScatter.COPIES + outer,
+        [
+            pltpu.VMEM((n_line, tokens, 2 * k_cols), BF16),
+            pltpu.VMEM((outer, w_rows, width), BF16),
+        ]
+        + PlaneScatter.scratch(rows, width),
     )
     block_output = (middle + ffn_out).astype(BF16)
     dkv_own = dkv_own.astype(BF16)
-    dqueries = dqueries.reshape(tokens, q_cols).astype(BF16)
+    dqueries = dqueries.reshape(tokens, q_cols)
     _, query_back = jax.vjp(query_map, q_raw, qk_gain[0])
     dq_raw, qgain_grad = query_back(dqueries.astype(F32))
     _, key_back = jax.vjp(query_map, k_raw, qk_gain[1])

time: 608 us -> 453 us (0.75)
  matrix products: 113 us -> 32 us
  other arithmetic: 85 us -> 38 us
  blocking collectives: 36.7 us -> 0 us
  Pallas kernels: 247 us -> 281 us
  between operations: 15.7 us -> 1.84 us
    dot_general x6 -> x0, matrix products: 80 us -> none  [the longest x1 21.1 us: local(): jnp.einsum('qgd,nd->gqn', grad_three, v_all, preferred_element_type=F32)]
    pallas_call x0 -> x2, Pallas kernels: none -> 43.1 us  [attention(): pl.pallas_call(body, name=name, out_shape=tuple((jax.ShapeDtypeStruct(sha...]
    all_gather x1 -> x0, blocking collectives: 36.7 us -> none  [local(): out_all = lax.all_gather(w_out, 'blk', axis=0, tiled=True)]
    convert_element_type x1, other arithmetic: 20.9 us -> 0.07 us  [rotate(): angles = where_at.astype(F32)[:, None] * frequency[None, :]]
    reduce_sum x1, other arithmetic: 15.1 us -> 0.61 us  [local(): jnp.sum(jnp.where(all_spans[:, None] == jnp.arange(spans, dtype=jnp.int32...]
    pallas_call x9, Pallas kernels: 247 us -> 238 us  [call(): pl.pallas_call(body, name=name, out_shape=tuple((jax.ShapeDtypeStruct(sha...]
    le x2 -> x0, other arithmetic: 7.93 us -> none  [local(): causal = key_where[None, :] <= tok_where[:, None]]
    ppermute x6, waiting for transfers between devices: 13.1 us -> 6.01 us  [line_scatter(): lax.ppermute(piece.astype(BF16), 'blk', shifts(outer, step)).astype(F32)]
  transfers between devices with their start and end apart: 13 -> 12, of which waited for: 2 -> 2; matrix products, arithmetic and copies ran while one was open for 30% -> 17% of each run, Pallas kernels for 32% -> 47%
where the time goes in v2:
time: 453 us; the launch traced here: 447 us
  Pallas kernels  281 us (62%)
  local copies, waits for them, and re-layouts  52.7 us (12%)
  other arithmetic  38 us (8%)
  matrix products  32 us (7%)
  starting transfers between devices  26.1 us (6%)
  waiting for transfers between devices  14.8 us (3%)
    pallas_call x9, Pallas kernels, call(): pl.pallas_call(body, name=name, out_shape=tuple((jax.ShapeDtypeStruct(sha...  238 us
    pallas_call x2, Pallas kernels, attention(): pl.pallas_call(body, name=name, out_shape=tuple((jax.ShapeDtypeStruct(sha...  43.1 us
    dot_general x12, matrix products, dot(): return jnp.dot(a, b, preferred_element_type=F32)  32 us
    ppermute x6, starting transfers between devices, line_scatter(): lax.ppermute(piece.astype(BF16), 'blk', shifts(outer, step)).astype(F32)  14.9 us
    ppermute x6, starting transfers between devices, line_gather(): got = lax.ppermute(piece, 'blk', shifts(outer, step))  11.2 us
  transfers between devices with their start and end apart: 12, of which 2 were waited for; matrix products, arithmetic and copies ran while one was open for 17% of the time, Pallas kernels for 47%

profile of v2, /device:TPU:0, one launch (start us, length us, event | category | flops | bytes accessed | tf_op | source)
XLA Modules:
  0.0 446.6 jit_solution(589228528080726570)
XLA Ops:
  0.7 1.9 reshape.514
  7.3 30.5 %start.1 = (bf16[8,128,1024]{2,1,0:T(8,128)(2,1)}, bf16[4,4,2,32,256]{4,3,2,1,0:T(8,128)(2,1)}, bf16[4,8,16,128]{3,2,1,0:T(8,128)(2,1)}, bf16[8,32,1152]{2,1,0:T(8,128)(2,1)}, bf16[2,2,32,1024]{3,2,1,0:T(8,128)(2,1)}) custom-call(bf16[128,1024]{1,0:T(8,128)(2,1)} %x_ref.1, bf16[8,32,256]{2,1,0:T(8,128)(2,1)} %maximum_bitcast_fusion.1.w_ref, ...), custom_call_target="tpu_custom_call" | custom-call | tf_op jit(solution)/shard_map/start/pallas_call | solution.py:364
  39.0 2.6 collective-permute-start.4
  41.7 2.4 collective-permute-start
  45.4 2.1 multiply_reduce_fusion
  54.6 3.1 fusion.26
  57.8 1.7 copy.137
  62.6 1.8 pad_maximum_fusion.6.kv_ref
  64.4 67.0 %line.1 = (bf16[4,1024,128]{2,1,0:T(8,128)(2,1)}, bf16[8,128,1024]{2,1,0:T(8,128)(2,1)}) custom-call(bf16[1024,128]{1,0:T(8,128)(2,1)} %pad_maximum_fusion.6.kv_ref, bf16[128,1024]{1,0:T(8,128)(2,1)} %og_ref.1), custom_call_target="tpu_custom_call" | custom-call | tf_op jit(solution)/shard_map/line/pallas_call | solution.py:364
  131.4 17.2 %attend.1 = (bf16[8,128,128]{2,1,0:T(8,128)(2,1)}, f32[8,8,256]{2,1,0:T(8,128)}) custom-call(s32[8]{0:T(128)} %copy-done.38, s32[32]{0:T(128)} %select_reduce_fusion.at_ref, bf16[8,128,128]{2,1,0:T(8,128)(2,1)} %copy.110.q_ref, bf16[32,128,128]{2,1,0:T(8,128)(2,1)} %bitcast.238), custom_call_target="tpu_custom_call" | custom-call | flops 4294967296 | bytes 4194304 | tf_op jit(solution)/shard_map/attend/pallas_call | solution.py:675
  148.7 3.0 convolution_convert_fusion.3
  151.7 15.5 %mix.1 = f32[128,1024]{1,0:T(8,128)} custom-call(bf16[8,128,1024]{2,1,0:T(8,128)(2,1)} %bitcast.198), custom_call_target="tpu_custom_call" | custom-call | tf_op jit(solution)/shard_map/mix/pallas_call | solution.py:364
  167.2 1.9 multiply_reduce_fusion.5
  169.2 1.9 fusion.1
  175.7 14.6 %widen.1 = bf16[8,128,1024]{2,1,0:T(8,128)(2,1)} custom-call(bf16[128,1024]{1,0:T(8,128)(2,1)} %multiply_convert_fusion.3.src_ref), custom_call_target="tpu_custom_call" | custom-call | tf_op jit(solution)/shard_map/widen/pallas_call | solution.py:364
  190.2 4.0 copy.121
  194.2 4.6 %collective-permute-start.2 = (bf16[144,1024]{1,0:T(8,128)(2,1)}, bf16[144,1024]{1,0:T(8,128)(2,1)S(1)}, u32[]{:S(2)}, u32[]{:S(2)}) collective-permute-start(bf16[144,1024]{1,0:T(8,128)(2,1)} %param.28), channel_id=1, source_target_pairs={{0,6},{1,7},{2,0},{3,1},{4,2},{5,3},{6,4},{7,5},{8,14},{9,15},{10,... | collective-permute-start | bytes 884744 | tf_op jit(solution)/shard_map/ppermute | solution.py:729
  200.8 8.7 %collective-permute-done.2 = bf16[144,1024]{1,0:T(8,128)(2,1)S(1)} collective-permute-done((bf16[144,1024]{1,0:T(8,128)(2,1)}, bf16[144,1024]{1,0:T(8,128)(2,1)S(1)}, u32[]{:S(2)}, u32[]{:S(2)}) %collective-permute-start.2) | collective-permute-done | bytes 294944 | tf_op jit(solution)/shard_map/ppermute | solution.py:729
  209.6 1.9 bitcast_dynamic-update-slice_fusion.1
  211.5 1.9 bitcast_dynamic-update-slice_fusion
  213.4 1.9 bitcast_dynamic-update-slice_fusion.2
  215.4 4.5 %fusion.61 = f32[1024,1152]{0,1:T(8,128)S(1)} fusion(bf16[1024,1024]{1,0:T(8,128)(2,1)S(1)} %bitcast.201, bf16[1024,1152]{1,0:T(8,128)(2,1)} %bitcast.35), kind=kOutput, calls=%fused_computation.160 | convolution fusion | flops 2415919104 | bytes 9175040 | tf_op jit(solution)/shard_map/dot_general | solution.py:745
  219.8 2.3 fusion.4
  222.1 3.2 convolution_convert_fusion.2
  227.8 2.2 collective-permute-start.10
  230.0 1.9 collective-permute-start.11
  232.1 6.0 %convolution_convert_fusion = bf16[1024,1024]{1,0:T(8,128)(2,1)} fusion(bf16[1024,1152]{1,0:T(8,128)(2,1)} %bitcast.35, bf16[1024,576]{0,1:T(8,128)(2,1)S(1)} %get-tuple-element.81, bf16[1024,576]{0,1:T(8,128)(2,1)S(1)} %get-tuple-element.80), kind=kOutput, calls=%fused_computation.16 | convolution fusion | flops 2421686272 | bytes 6815744 | tf_op jit(solution)/shard_map/dot_general | solution.py:745
  238.1 2.9 fusion.5
  241.0 2.2 copy-done.18
  244.7 4.2 collective-permute-start.7
  248.9 15.5 %narrow.1 = f32[128,1024]{1,0:T(8,128)} custom-call(bf16[8,128,1024]{2,1,0:T(8,128)(2,1)} %bitcast.206), custom_call_target="tpu_custom_call" | custom-call | tf_op jit(solution)/shard_map/narrow/pallas_call | solution.py:364
  265.7 2.0 fusion.57.src_ref
  267.7 14.9 %spread.1 = bf16[8,128,1024]{2,1,0:T(8,128)(2,1)} custom-call(bf16[128,1024]{1,0:T(8,128)(2,1)} %fusion.57.src_ref), custom_call_target="tpu_custom_call" | custom-call | tf_op jit(solution)/shard_map/spread/pallas_call | solution.py:364
  282.6 2.9 fusion.8
  287.0 25.9 %attend_back.1 = (bf16[8,128,128]{2,1,0:T(8,128)(2,1)}, bf16[32,128,128]{2,1,0:T(8,128)(2,1)}) custom-call(s32[8]{0:T(128)} %copy-done.38, s32[32]{0:T(128)} %select_reduce_fusion.at_ref, bf16[8,128,128]{2,1,0:T(8,128)(2,1)} %copy.110.q_ref, bf16[32,128,128]{2,1,0:T(8,128)(2,1)} %bitcast.239, bf16[8,128,128]{2,1,0:T(8,128)(2,1)} %get-tuple-element.57.out_ref, ...), custom_call_target="tpu_custom_call" | custom-call | flops 10737418240 | bytes 4194304 | tf_op jit(solution)/shard_map/attend_back/pallas_call | solution.py:675
  314.2 38.6 %back.1 = (f32[1024,128]{1,0:T(8,128)}, f32[128,1024]{1,0:T(8,128)}, f32[32,1024]{1,0:T(8,128)}) custom-call(bf16[4,1024,128]{2,1,0:T(8,128)(2,1)} %bitcast.220, bf16[8,128,1024]{2,1,0:T(8,128)(2,1)} %bitcast.212, bf16[2,2,32,1024]{3,2,1,0:T(8,128)(2,1)} %bitcast.223), custom_call_target="tpu_custom_call" | custom-call | tf_op jit(solution)/shard_map/back/pallas_call | solution.py:364
  354.7 2.2 fusion.29
  361.2 6.3 %collective-permute-start.8 = (bf16[4,64,1152]{2,1,0:T(8,128)(2,1)}, bf16[4,64,1152]{2,1,0:T(8,128)(2,1)S(1)}, u32[]{:S(2)}, u32[]{:S(2)}) collective-permute-start(bf16[4,64,1152]{2,1,0:T(8,128)(2,1)} %get-tuple-element.83), channel_id=1, source_target_pairs={{0,6},{1,7},{2,0},{3,1},{4,2},{5,3},{6,4},{7,5},{8,14},{9,15},{10,... | collective-permute-start | bytes 1769480 | tf_op jit(solution)/shard_map/ppermute | solution.py:740
  367.5 2.1 convolution_convert_fusion.1
  371.2 2.3 fusion.24
  373.5 6.0 %collective-permute-done.8 = bf16[4,64,1152]{2,1,0:T(8,128)(2,1)S(1)} collective-permute-done((bf16[4,64,1152]{2,1,0:T(8,128)(2,1)}, bf16[4,64,1152]{2,1,0:T(8,128)(2,1)S(1)}, u32[]{:S(2)}, u32[]{:S(2)}) %collective-permute-start.8) | collective-permute-done | bytes 589856 | tf_op jit(solution)/shard_map/ppermute | solution.py:740
  379.5 2.7 fusion.11
  382.2 31.0 %last.1 = (f32[128,1024]{1,0:T(8,128)}, f32[8,32,256]{2,1,0:T(8,128)}, bf16[8,32,1152]{2,1,0:T(8,128)(2,1)}) custom-call(bf16[8,128,1024]{2,1,0:T(8,128)(2,1)} %bitcast.202, bf16[4,4,2,32,256]{4,3,2,1,0:T(8,128)(2,1)} %bitcast.228, bf16[8,32,1152]{2,1,0:T(8,128)(2,1)} %bitcast.205), custom_call_target="tpu_custom_call" | custom-call | tf_op jit(solution)/shard_map/last/pallas_call | solution.py:364
  416.5 2.1 slice_convert_fusion
  420.2 2.1 reshape.557
  422.3 1.8 reshape.566
  425.0 2.1 reshape.559
  429.0 10.4 %small.1 = f32[24,128]{1,0:T(8,128)} custom-call(f32[24,128]{1,0:T(8,128)} %pad_bitcast_fusion.v_ref), custom_call_target="tpu_custom_call" | custom-call | tf_op jit(solution)/shard_map/small/pallas_call | solution.py:364
  (192 shorter events, 54.2 us)
Async XLA Ops:
  0.6 4.2 copy-start
  0.7 2.5 copy-start.30
  2.5 2.0 copy-start.32
  2.8 1.9 copy-start.33
  3.1 2.7 copy-start.36
  4.0 2.6 copy-start.39
  37.8 9.7 %copy-start.3 = (bf16[8,128,1024]{2,1,0:T(8,128)(2,1)S(1)}, bf16[8,128,1024]{2,1,0:T(8,128)(2,1)}, u32[]{:S(2)}) copy-start(bf16[8,128,1024]{2,1,0:T(8,128)(2,1)} %get-tuple-element.53) | copy-start | bytes 6291460
  37.8 171.7 %collective-permute-start.3 = (bf16[4,64,1152]{2,1,0:T(8,128)(2,1)}, bf16[4,64,1152]{2,1,0:T(8,128)(2,1)}, u32[]{:S(2)}, u32[]{:S(2)}) collective-permute-start(bf16[4,64,1152]{2,1,0:T(8,128)(2,1)} %bitcast.224), channel_id=1, source_target_pairs={{0,2},{1,3},{2,4},{3,5},{4,6},{5,7},{6,0},{7,1},{8,10},{9,11},{10,... | collective-permute-start | bytes 1769480 | tf_op jit(solution)/shard_map/ppermute | solution.py:729
  39.0 172.5 %collective-permute-start.4 = (bf16[4,64,1152]{2,1,0:T(8,128)(2,1)}, bf16[4,64,1152]{2,1,0:T(8,128)(2,1)}, u32[]{:S(2)}, u32[]{:S(2)}) collective-permute-start(bf16[4,64,1152]{2,1,0:T(8,128)(2,1)} %bitcast.225), channel_id=1, source_target_pairs={{0,4},{1,5},{2,6},{3,7},{4,0},{5,1},{6,2},{7,3},{8,12},{9,13},{10,... | collective-permute-start | bytes 1769480 | tf_op jit(solution)/shard_map/ppermute | solution.py:729
  41.6 171.8 %collective-permute-start.5 = (bf16[4,64,1152]{2,1,0:T(8,128)(2,1)}, bf16[4,64,1152]{2,1,0:T(8,128)(2,1)}, u32[]{:S(2)}, u32[]{:S(2)}) collective-permute-start(bf16[4,64,1152]{2,1,0:T(8,128)(2,1)} %bitcast.226), channel_id=1, source_target_pairs={{0,6},{1,7},{2,0},{3,1},{4,2},{5,3},{6,4},{7,5},{8,14},{9,15},{10,... | collective-permute-start | bytes 1769480 | tf_op jit(solution)/shard_map/ppermute | solution.py:729
  41.7 152.5 %collective-permute-start = (bf16[144,1024]{1,0:T(8,128)(2,1)}, bf16[144,1024]{1,0:T(8,128)(2,1)}, u32[]{:S(2)}, u32[]{:S(2)}) collective-permute-start(bf16[144,1024]{1,0:T(8,128)(2,1)} %param.28), channel_id=1, source_target_pairs={{0,2},{1,3},{2,4},{3,5},{4,6},{5,7},{6,0},{7,1},{8,10},{9,11},{10,... | collective-permute-start | bytes 884744 | tf_op jit(solution)/shard_map/ppermute | solution.py:729
  44.1 155.7 %collective-permute-start.1 = (bf16[144,1024]{1,0:T(8,128)(2,1)}, bf16[144,1024]{1,0:T(8,128)(2,1)}, u32[]{:S(2)}, u32[]{:S(2)}) collective-permute-start(bf16[144,1024]{1,0:T(8,128)(2,1)} %param.28), channel_id=1, source_target_pairs={{0,4},{1,5},{2,6},{3,7},{4,0},{5,1},{6,2},{7,3},{8,12},{9,13},{10,... | collective-permute-start | bytes 884744 | tf_op jit(solution)/shard_map/ppermute | solution.py:729
  49.3 126.3 %copy-start.4 = (f32[1024,256]{0,1:T(8,128)}, f32[1024,256]{0,1:T(8,128)S(1)}, u32[]{:S(2)}) copy-start(f32[1024,256]{0,1:T(8,128)S(1)} %fusion.60) | copy-start | bytes 3145732
  49.4 3.5 copy-start.35
  50.5 7.3 %copy-start.38 = (s32[8]{0:T(128)}, s32[8]{0:T(128)S(1)}, u32[]{:S(2)}) copy-start(s32[8]{0:T(128)S(1)} %reshape.508.own_ref) | copy-start | bytes 100
  54.6 5.1 %copy-start.19 = (f32[1024,32]{0,1:T(8,128)}, f32[1024,32]{0,1:T(8,128)S(1)}, u32[]{:S(2)}) copy-start(f32[1024,32]{0,1:T(8,128)S(1)} %get-tuple-element.110) | copy-start | bytes 393220
  54.6 5.1 %copy-start.21 = (f32[1024,32]{0,1:T(8,128)}, f32[1024,32]{0,1:T(8,128)S(1)}, u32[]{:S(2)}) copy-start(f32[1024,32]{0,1:T(8,128)S(1)} %get-tuple-element.111) | copy-start | bytes 393220
  131.4 17.3 %copy-start.23 = (bf16[2,2,32,1024]{3,2,1,0:T(8,128)(2,1)S(1)}, bf16[2,2,32,1024]{3,2,1,0:T(8,128)(2,1)}, u32[]{:S(2)}) copy-start(bf16[2,2,32,1024]{3,2,1,0:T(8,128)(2,1)} %get-tuple-element.58) | copy-start | bytes 786436
  148.7 18.5 %copy-start.10 = (bf16[128,1024]{1,0:T(8,128)(2,1)S(1)}, bf16[128,1024]{1,0:T(8,128)(2,1)}, u32[]{:S(2)}) copy-start(bf16[128,1024]{1,0:T(8,128)(2,1)} %x_ref.1) | copy-start | bytes 786436
  171.1 2.6 copy-start.6
  194.2 15.3 %collective-permute-start.2 = (bf16[144,1024]{1,0:T(8,128)(2,1)}, bf16[144,1024]{1,0:T(8,128)(2,1)S(1)}, u32[]{:S(2)}, u32[]{:S(2)}) collective-permute-start(bf16[144,1024]{1,0:T(8,128)(2,1)} %param.28), channel_id=1, source_target_pairs={{0,6},{1,7},{2,0},{3,1},{4,2},{5,3},{6,4},{7,5},{8,14},{9,15},{10,... | collective-permute-start | bytes 884744 | tf_op jit(solution)/shard_map/ppermute | solution.py:729
  200.8 14.6 %copy-start.8 = (bf16[8,128,1024]{2,1,0:T(8,128)(2,1)S(1)}, bf16[8,128,1024]{2,1,0:T(8,128)(2,1)}, u32[]{:S(2)}) copy-start(bf16[8,128,1024]{2,1,0:T(8,128)(2,1)} %widen.1) | copy-start | bytes 6291460
  215.4 4.5 %copy-start.40 = (bf16[8,128,1024]{2,1,0:T(8,128)(2,1)S(1)}, bf16[8,128,1024]{2,1,0:T(8,128)(2,1)}, u32[]{:S(2)}) copy-start(bf16[8,128,1024]{2,1,0:T(8,128)(2,1)} %get-tuple-element.59) | copy-start | bytes 6291460
  226.7 5.4 %copy-start.26 = (f32[4,144,1024]{2,1,0:T(8,128)}, f32[4,144,1024]{2,1,0:T(8,128)S(1)}, u32[]{:S(2)}) copy-start(f32[4,144,1024]{2,1,0:T(8,128)S(1)} %fusion.62) | copy-start | bytes 7077892
  227.8 133.4 %collective-permute-start.10 = (bf16[144,1024]{1,0:T(8,128)(2,1)}, bf16[144,1024]{1,0:T(8,128)(2,1)}, u32[]{:S(2)}, u32[]{:S(2)}) collective-permute-start(bf16[144,1024]{1,0:T(8,128)(2,1)} %get-tuple-element.88), channel_id=1, source_target_pairs={{0,4},{1,5},{2,6},{3,7},{4,0},{5,1},{6,2},{7,3},{8,12},{9,13},{10,... | collective-permute-start | bytes 884744 | tf_op jit(solution)/shard_map/ppermute | solution.py:740
  230.0 141.1 %collective-permute-start.11 = (bf16[144,1024]{1,0:T(8,128)(2,1)}, bf16[144,1024]{1,0:T(8,128)(2,1)}, u32[]{:S(2)}, u32[]{:S(2)}) collective-permute-start(bf16[144,1024]{1,0:T(8,128)(2,1)} %get-tuple-element.87), channel_id=1, source_target_pairs={{0,6},{1,7},{2,0},{3,1},{4,2},{5,3},{6,4},{7,5},{8,14},{9,15},{10,... | collective-permute-start | bytes 884744 | tf_op jit(solution)/shard_map/ppermute | solution.py:740
  231.9 139.3 %collective-permute-start.9 = (bf16[144,1024]{1,0:T(8,128)(2,1)}, bf16[144,1024]{1,0:T(8,128)(2,1)}, u32[]{:S(2)}, u32[]{:S(2)}) collective-permute-start(bf16[144,1024]{1,0:T(8,128)(2,1)} %get-tuple-element.86), channel_id=1, source_target_pairs={{0,2},{1,3},{2,4},{3,5},{4,6},{5,7},{6,0},{7,1},{8,10},{9,11},{10,... | collective-permute-start | bytes 884744 | tf_op jit(solution)/shard_map/ppermute | solution.py:740
  232.1 6.0 %copy-start.14 = (bf16[1024,1024]{1,0:T(8,128)(2,1)S(1)}, bf16[1024,1024]{1,0:T(8,128)(2,1)}, u32[]{:S(2)}) copy-start(bf16[1024,1024]{1,0:T(8,128)(2,1)} %copy.121) | copy-start | bytes 6291460
  241.0 2.2 copy-start.18
  244.5 21.2 %copy-start.11 = (bf16[128,1024]{1,0:T(8,128)(2,1)S(1)}, bf16[128,1024]{1,0:T(8,128)(2,1)}, u32[]{:S(2)}) copy-start(bf16[128,1024]{1,0:T(8,128)(2,1)} %og_ref.1) | copy-start | bytes 786436
  244.5 129.0 %collective-permute-start.6 = (bf16[4,64,1152]{2,1,0:T(8,128)(2,1)}, bf16[4,64,1152]{2,1,0:T(8,128)(2,1)}, u32[]{:S(2)}, u32[]{:S(2)}) collective-permute-start(bf16[4,64,1152]{2,1,0:T(8,128)(2,1)} %get-tuple-element.82), channel_id=1, source_target_pairs={{0,2},{1,3},{2,4},{3,5},{4,6},{5,7},{6,0},{7,1},{8,10},{9,11},{10,... | collective-permute-start | bytes 1769480 | tf_op jit(solution)/shard_map/ppermute | solution.py:740
  244.7 128.8 %collective-permute-start.7 = (bf16[4,64,1152]{2,1,0:T(8,128)(2,1)}, bf16[4,64,1152]{2,1,0:T(8,128)(2,1)}, u32[]{:S(2)}, u32[]{:S(2)}) collective-permute-start(bf16[4,64,1152]{2,1,0:T(8,128)(2,1)} %get-tuple-element.84), channel_id=1, source_target_pairs={{0,4},{1,5},{2,6},{3,7},{4,0},{5,1},{6,2},{7,3},{8,12},{9,13},{10,... | collective-permute-start | bytes 1769480 | tf_op jit(solution)/shard_map/ppermute | solution.py:740
  265.7 16.9 %copy-start.25 = (bf16[8,128,128]{2,1,0:T(8,128)(2,1)S(1)}, bf16[8,128,128]{2,1,0:T(8,128)(2,1)}, u32[]{:S(2)}) copy-start(bf16[8,128,128]{2,1,0:T(8,128)(2,1)} %get-tuple-element.57.out_ref) | copy-start | bytes 786436
  267.7 17.9 %copy-start.24 = (bf16[2,2,32,1024]{3,2,1,0:T(8,128)(2,1)S(1)}, bf16[2,2,32,1024]{3,2,1,0:T(8,128)(2,1)}, u32[]{:S(2)}) copy-start(bf16[2,2,32,1024]{3,2,1,0:T(8,128)(2,1)} %get-tuple-element.58) | copy-start | bytes 786436
  282.6 3.0 copy-start.2
  287.0 27.1 %copy-start.20 = (f32[1024,32]{0,1:T(8,128)S(1)}, f32[1024,32]{0,1:T(8,128)}, u32[]{:S(2)}) copy-start(f32[1024,32]{0,1:T(8,128)} %copy-done.19) | copy-start | bytes 393220
  287.0 27.1 %copy-start.22 = (f32[1024,32]{0,1:T(8,128)S(1)}, f32[1024,32]{0,1:T(8,128)}, u32[]{:S(2)}) copy-start(f32[1024,32]{0,1:T(8,128)} %copy-done.21) | copy-start | bytes 393220
  352.8 4.2 copy-start.7
  358.7 8.8 %copy-start.16 = (bf16[4,4,2,32,256]{4,3,2,1,0:T(8,128)(2,1)S(1)}, bf16[4,4,2,32,256]{4,3,2,1,0:T(8,128)(2,1)}, u32[]{:S(2)}) copy-start(bf16[4,4,2,32,256]{4,3,2,1,0:T(8,128)(2,1)} %get-tuple-element.55) | copy-start | bytes 1572868
  361.0 8.6 %copy-start.13 = (bf16[1024,1024]{1,0:T(8,128)(2,1)S(1)}, bf16[1024,1024]{1,0:T(8,128)(2,1)}, u32[]{:S(2)}) copy-start(bf16[1024,1024]{1,0:T(8,128)(2,1)} %fusion.1) | copy-start | bytes 6291460
  361.2 18.3 %collective-permute-start.8 = (bf16[4,64,1152]{2,1,0:T(8,128)(2,1)}, bf16[4,64,1152]{2,1,0:T(8,128)(2,1)S(1)}, u32[]{:S(2)}, u32[]{:S(2)}) collective-permute-start(bf16[4,64,1152]{2,1,0:T(8,128)(2,1)} %get-tuple-element.83), channel_id=1, source_target_pairs={{0,6},{1,7},{2,0},{3,1},{4,2},{5,3},{6,4},{7,5},{8,14},{9,15},{10,... | collective-permute-start | bytes 1769480 | tf_op jit(solution)/shard_map/ppermute | solution.py:740
  424.9 17.7 %copy-start.28 = (f32[32,8,64]{2,0,1:T(8,128)S(1)}, f32[32,8,64]{2,0,1:T(8,128)}, u32[]{:S(2)}) copy-start(f32[32,8,64]{2,0,1:T(8,128)} %get-tuple-element.101) | copy-start | bytes 196612
  424.9 18.5 %copy-start.9 = (f32[128,1024]{1,0:T(8,128)S(1)}, f32[128,1024]{1,0:T(8,128)}, u32[]{:S(2)}) copy-start(f32[128,1024]{1,0:T(8,128)} %narrow.1) | copy-start | bytes 1572868
  424.9 18.4 %copy-start.12 = (bf16[128,1024]{1,0:T(8,128)(2,1)S(1)}, bf16[128,1024]{1,0:T(8,128)(2,1)}, u32[]{:S(2)}) copy-start(bf16[128,1024]{1,0:T(8,128)(2,1)} %og_ref.1) | copy-start | bytes 786436
  425.0 18.4 %copy-start.17 = (f32[128,1024]{1,0:T(8,128)S(1)}, f32[128,1024]{1,0:T(8,128)}, u32[]{:S(2)}) copy-start(f32[128,1024]{1,0:T(8,128)} %get-tuple-element.66) | copy-start | bytes 1572868
  427.1 16.3 %copy-start.29 = (f32[128,1024]{1,0:T(8,128)S(1)}, f32[128,1024]{1,0:T(8,128)}, u32[]{:S(2)}) copy-start(f32[128,1024]{1,0:T(8,128)} %get-tuple-element.63) | copy-start | bytes 1572868
  428.3 17.4 %copy-start.31 = (f32[32,1024]{1,0:T(8,128)S(1)}, f32[32,1024]{1,0:T(8,128)}, u32[]{:S(2)}) copy-start(f32[32,1024]{1,0:T(8,128)} %get-tuple-element.137) | copy-start | bytes 393220
  440.8 5.5 %copy-start.1 = (bf16[32,1024]{1,0:T(8,128)(2,1)S(1)}, bf16[32,1024]{1,0:T(8,128)(2,1)}, u32[]{:S(2)}) copy-start(bf16[32,1024]{1,0:T(8,128)(2,1)} %param.20) | copy-start | bytes 196612
  (6 other events, 8.5 us)

commit v3 on v2

--- a/solution.py
+++ b/solution.py
@@ -10,11 +10,14 @@
 
 EPS = 1e-05
 THETA = 1000000.0
+LANES = 128
 CORES = 2
 INNER = 2
 MESH = pl.DeviceIdType.MESH
 F32 = jnp.float32
 BF16 = jnp.bfloat16
+NT = (((1,), (1,)), ((), ()))
+TN = (((0,), (0,)), ((), ()))
 
 
 def here():
@@ -154,8 +157,9 @@
 class PlaneScatter:
     COPIES = 10
 
-    def __init__(self, mail, place, parts, out, bufs):
+    def __init__(self, mail, place, parts, out, bufs, make=None):
         self.mail, self.place, self.parts, self.out = mail, place, parts, out
+        self.make = make or (lambda block: None)
         self.first, self.held, self.via_x, self.via_y, self.last = bufs
         self.base = mail.take(self.COPIES)
         half = out.shape[0] // 2
@@ -176,6 +180,7 @@
         y, c, z, x = self.place
         pair, xn, yn = near(self.place)
         for slot, (py, px) in enumerate(((1 - y, 1 - x), (y, 1 - x), (1 - y, x), (y, x))):
+            self.make(rank(py, 1 - c, px))
             self.mail.send(
                 self.base + slot,
                 self.parts.at[rank(py, 1 - c, px)],
@@ -186,6 +191,7 @@
     def joined(self, slot, py, px):
         y, c, z, x = self.place
         pair, xn, yn = near(self.place)
+        self.make(rank(py, c, px))
         self.mail.arrive(self.base + slot, self.first.at[py, px], pair)
         return self.parts[rank(py, c, px)].astype(F32) + self.first[py, px].astype(F32)
 
@@ -224,6 +230,41 @@
         out[bot] = out[bot] + last[3].astype(F32)
 
 
+class LineGather:
+    def __init__(self, mail, place, src, out):
+        self.mail, self.place, self.src, self.out = mail, place, src, out
+        self.line = line_peers(place)
+        self.base = mail.take(len(self.line))
+
+    def begin(self):
+        z = self.place[2]
+        for slot, (dev, _, _) in enumerate(self.line):
+            self.mail.send(self.base + slot, self.src, self.out.at[z], dev)
+        self.out[z] = self.src[...]
+
+    def end(self):
+        for slot, (dev, _, back) in enumerate(self.line):
+            self.mail.arrive(self.base + slot, self.out.at[back], dev)
+
+
+class LineScatter:
+    def __init__(self, mail, place, parts, got):
+        self.mail, self.place, self.parts, self.got = mail, place, parts, got
+        self.line = line_peers(place)
+        self.base = mail.take(len(self.line))
+
+    def begin(self):
+        for slot, (dev, forth, _) in enumerate(self.line):
+            self.mail.send(self.base + slot, self.parts.at[forth], self.got.at[slot], dev)
+
+    def end(self):
+        total = self.parts[self.place[2]].astype(F32)
+        for slot, (dev, _, _) in enumerate(self.line):
+            self.mail.arrive(self.base + slot, self.got.at[slot], dev)
+            total = total + self.got[slot].astype(F32)
+        return total
+
+
 class PlaneSwap:
     COPIES = 7
 
@@ -378,166 +419,477 @@
     )(*args)
 
 
+def lanes(shape):
+    return lax.broadcasted_iota(jnp.int32, shape, len(shape) - 1)
+
+
+def rms_of(values):
+    return lax.rsqrt(jnp.mean(values * values, axis=-1, keepdims=True) + EPS)
+
+
+def rms_back(values, gain_vec, grad):
+    inverse = rms_of(values)
+    shaped = grad * gain_vec
+    mean = jnp.mean(values * shaped, axis=-1, keepdims=True)
+    dgain = jnp.sum(grad * values * inverse, axis=0, keepdims=True)
+    return inverse * shaped - values * (inverse * inverse * inverse * mean), dgain
+
+
+def per_head(values, size):
+    left = lanes(values.shape) < size
+    first = jnp.sum(jnp.where(left, values, 0.0), axis=-1, keepdims=True)
+    second = jnp.sum(jnp.where(left, 0.0, values), axis=-1, keepdims=True)
+    return jnp.where(left, first, second)
+
+
+def head_rms(values, size):
+    return lax.rsqrt(per_head(values * values, size) * (1.0 / size) + EPS)
+
+
+def swap_halves(values, size):
+    half = size // 2
+    width = values.shape[-1]
+    first = lanes(values.shape) % size < half
+    return jnp.where(first, pltpu.roll(values, width - half, 1), pltpu.roll(values, half, 1))
+
+
+def turn(cos_ref, sin_ref, r):
+    cos, sin = cos_ref[r], sin_ref[r]
+    return (
+        jnp.concatenate([cos, cos, cos, cos], axis=0).T,
+        jnp.concatenate([-sin, sin, -sin, sin], axis=0).T,
+    )
+
+
+def head_forward(raw, gain_vec, cos, sin, size):
+    values = raw * head_rms(raw, size) * gain_vec
+    return values * cos + swap_halves(values, size) * sin
+
+
+def head_back(raw, gain_vec, cos, sin, size, grad):
+    grad = grad * cos - swap_halves(grad, size) * sin
+    inverse = head_rms(raw, size)
+    shaped = grad * gain_vec
+    mean = per_head(raw * shaped, size) * (1.0 / size)
+    dgain = jnp.sum(grad * raw * inverse, axis=0, keepdims=True)
+    return inverse * shaped - raw * (inverse * inverse * inverse * mean), dgain
+
+
 def start_kernel(
-    x_ref, w_ref, g_ref, gu_ref, wo_ref, xp_ref, wq_ref, gain_ref, gus_ref, wos_ref, ss, rs
+    x_ref, q_ref, k_ref, v_ref, g1_ref, g2_ref, gu_ref, wo_ref,
+    xp_ref, wq_ref, gain_ref, gus_ref, wos_ref,
+    ss, rs, w_ref, g_ref, gs_ref,
 ):
     place = y, c, z, x = here()
     me = rank(y, c, x)
     head = y * CORES + c
     mail = Mail((ss, rs))
     peers, line = plane_peers(place), line_peers(place)
+    plane, w_rows, cols = w_ref.shape
+    q_cols = q_ref.shape[1] // plane
+    k_cols = k_ref.shape[1] // plane
+    g_ref[...] = jnp.zeros_like(g_ref)
+    g_ref[0:1, :w_rows] = g1_ref[...]
+    g_ref[1:2, :w_rows] = g2_ref[...]
+    keys, values = k_ref[...].astype(F32), v_ref[...].astype(F32)
+    for p in range(plane):
+        at = slice(p * k_cols, (p + 1) * k_cols)
+        pair = jnp.concatenate([keys[:, at], values[:, at]], axis=1)
+        w_ref[p, :, :q_cols] = q_ref[:, p * q_cols : (p + 1) * q_cols]
+        w_ref[p, :, q_cols:] = pair.astype(BF16)
     greet([p[0] for p in peers] + blk_peers(place))
     w_base, g_base = mail.take(7), mail.take(7)
     zw_base, zg_base = mail.take(len(line)), mail.take(len(line))
     for slot, (dev, other, _) in enumerate(peers):
-        mail.send(g_base + slot, g_ref, gain_ref.at[z, me], dev)
+        mail.send(g_base + slot, g_ref, gs_ref.at[z, me], dev)
         mail.send(w_base + slot, w_ref.at[other], wq_ref.at[head, z, x], dev)
-    gain_ref[z, me] = g_ref[...]
+    gs_ref[z, me] = g_ref[...]
     wq_ref[head, z, x] = w_ref[me]
     rows = PlaneGather(mail, place, x_ref, xp_ref)
     swap = PlaneSwap(mail, place, gu_ref, gus_ref)
     block = RowsOut(mail, place, wo_ref, wos_ref)
     rows.begin()
-    block.begin()
     for slot, (dev, other, (oh, ox)) in enumerate(peers):
-        mail.arrive(g_base + slot, gain_ref.at[z, other], dev)
+        mail.arrive(g_base + slot, gs_ref.at[z, other], dev)
         mail.arrive(w_base + slot, wq_ref.at[oh, z, ox], dev)
     for slot, (dev, _, _) in enumerate(line):
-        mail.send(zg_base + slot, gain_ref.at[z], gain_ref.at[z], dev)
+        mail.send(zg_base + slot, gs_ref.at[z], gs_ref.at[z], dev)
         mail.send(zw_base + slot, wq_ref.at[:, z], wq_ref.at[:, z], dev)
+    block.begin()
     rows.middle()
     swap.begin()
     rows.end()
     for slot, (dev, _, back) in enumerate(line):
-        mail.arrive(zg_base + slot, gain_ref.at[back], dev)
+        mail.arrive(zg_base + slot, gs_ref.at[back], dev)
         mail.arrive(zw_base + slot, wq_ref.at[:, back], dev)
+    heads, outer = wq_ref.shape[:2]
+    gain_ref[...] = jnp.zeros_like(gain_ref)
+    for row in range(2):
+        gain_ref[row : row + 1] = jnp.concatenate(
+            [
+                gs_ref[oz, oh * INNER + ox].astype(F32)[row : row + 1, :w_rows]
+                for oh in range(heads)
+                for oz in range(outer)
+                for ox in range(INNER)
+            ],
+            axis=1,
+        )
     block.end()
     swap.end()
     mail.close()
 
 
-def line_kernel(kv_ref, og_ref, kvs_ref, ogs_ref, ss, rs):
+def line_kernel(
+    x_ref, w_ref, gain_ref, qk_ref, cos_ref, sin_ref, og_ref,
+    q_ref, kvs_ref, raw_ref, norm_ref, ogs_ref,
+    ss, rs, kv_ref,
+):
     place = y, c, z, x = here()
     mail = Mail((ss, rs))
     line = line_peers(place)
     greet([p[0] for p in line] + list(near(place)))
-    base = mail.take(len(line))
-    for slot, (dev, _, _) in enumerate(line):
-        mail.send(base + slot, kv_ref, kvs_ref.at[z], dev)
     rows = PlaneGather(mail, place, og_ref, ogs_ref)
+    base = mail.take(2 * len(line))
     rows.begin()
+    count, tok, _ = x_ref.shape
+    q_cols = q_ref.shape[2]
+    size = q_cols // 2
+    gain_one = gain_ref[0:1]
+    gain_q, gain_k = qk_ref[0:1], qk_ref[1:2]
+
+    def one_block(r, carry):
+        block = x_ref[r].astype(F32)
+        normed = (block * rms_of(block) * gain_one).astype(BF16)
+        norm_ref[r] = normed
+        raw = jnp.dot(normed, w_ref[...], preferred_element_type=F32)
+        raw_ref[r] = raw
+        cos, sin = turn(cos_ref, sin_ref, r)
+        q_ref[r] = head_forward(raw[:, :q_cols], gain_q, cos, sin, size).astype(BF16)
+        pair = raw[:, q_cols:]
+        turned = head_forward(pair, gain_k, cos, sin, size)
+        kv_ref[r] = jnp.where(lanes(pair.shape) < size, turned, pair).astype(BF16)
+        return carry
+
+    half = count // 2
+    for part in range(2):
+        lax.fori_loop(part * half, (part + 1) * half, one_block, 0)
+        at = pl.ds(part * half, half)
+        for slot, (dev, _, _) in enumerate(line):
+            mail.send(base + 2 * slot + part, kv_ref.at[at], kvs_ref.at[z, at], dev)
     kvs_ref[z] = kv_ref[...]
     rows.middle()
     rows.end()
-    for slot, (dev, _, back) in enumerate(line):
-        mail.arrive(base + slot, kvs_ref.at[back], dev)
+    for part in range(2):
+        at = pl.ds(part * half, half)
+        for slot, (dev, _, back) in enumerate(line):
+            mail.arrive(base + 2 * slot + part, kvs_ref.at[back, at], dev)
     mail.close()
 
 
-def gather_kernel(src_ref, out_ref, ss, rs):
+def mix_kernel(
+    att_ref, wo_ref, x_ref, gain_ref, wd_ref,
+    mid_ref, n2_ref, wds_ref,
+    ss, rs, parts, own, *bufs,
+):
+    place = here()
+    mail = Mail((ss, rs))
+    greet([p[0] for p in line_peers(place)] + list(near(place)))
+    down = LineGather(mail, place, wd_ref, wds_ref)
+
+    def make(block):
+        parts[block] = jnp.dot(
+            att_ref[block], wo_ref[...], preferred_element_type=F32
+        ).astype(BF16)
+
+    summed = PlaneScatter(mail, place, parts, mid_ref, bufs, make)
+    rows = PlaneGather(mail, place, own, n2_ref)
+    summed.begin()
+    down.begin()
+    summed.middle()
+    summed.end()
+    middle = x_ref[...].astype(F32) + mid_ref[...]
+    mid_ref[...] = middle
+    own[...] = (middle * rms_of(middle) * gain_ref[1:2]).astype(BF16)
+    rows.begin()
+    rows.middle()
+    rows.end()
+    down.end()
+    mail.close()
+
+
+def narrow_kernel(
+    parts_ref, mid_ref, og_ref, gain_ref,
+    dmid_ref, dmids_ref, g2_ref,
+    ss, rs, own, *bufs,
+):
     place = here()
     mail = Mail((ss, rs))
     greet(list(near(place)))
-    rows = PlaneGather(mail, place, src_ref, out_ref)
+    summed = PlaneScatter(mail, place, parts_ref, dmid_ref, bufs)
+    rows = PlaneGather(mail, place, own, dmids_ref)
+    summed.begin()
+    summed.middle()
+    summed.end()
+    back, dgain = rms_back(mid_ref[...], gain_ref[1:2], dmid_ref[...])
+    dmiddle = og_ref[...].astype(F32) + back
+    dmid_ref[...] = dmiddle
+    own[...] = dmiddle.astype(BF16)
+    g2_ref[...] = dgain
     rows.begin()
     rows.middle()
     rows.end()
     mail.close()
 
 
-def scatter_kernel(parts_ref, out_ref, ss, rs, *bufs):
+def back_kernel(
+    dkv_ref, parts_ref, op_ref, mid_ref,
+    kv_ref, out_ref, ops_ref,
+    ss, rs, acc, got, op_got, *bufs,
+):
     place = here()
     mail = Mail((ss, rs))
-    greet(list(near(place)))
-    rows = PlaneScatter(mail, place, parts_ref, out_ref, bufs)
-    rows.begin()
-    rows.middle()
-    rows.end()
-    mail.close()
-
-
-def back_kernel(dkv_ref, parts_ref, op_ref, kv_ref, out_ref, ops_ref, ss, rs, got, op_got, *bufs):
-    place = y, c, z, x = here()
-    mail = Mail((ss, rs))
-    line = line_peers(place)
-    pair, xn, yn = near(place)
-    greet(blk_peers(place) + [pair, xn, yn])
-    base = mail.take(len(line))
-    for slot, (dev, forth, _) in enumerate(line):
-        mail.send(base + slot, dkv_ref.at[forth], got.at[slot], dev)
-    rows = PlaneScatter(mail, place, parts_ref, out_ref, bufs)
+    greet(blk_peers(place) + list(near(place)))
+    line = LineScatter(mail, place, dkv_ref, got)
+    rows = PlaneScatter(mail, place, parts_ref, acc, bufs)
     block = RowsBack(mail, place, op_ref, op_got, ops_ref)
+    line.begin()
     rows.begin()
     block.begin()
     rows.middle()
     rows.end()
-    total = dkv_ref[z].astype(F32)
-    for slot, (dev, _, _) in enumerate(line):
-        mail.arrive(base + slot, got.at[slot], dev)
-        total = total + got[slot].astype(F32)
-    kv_ref[...] = total
+    out_ref[...] = (mid_ref[...] + acc[...]).astype(BF16)
+    kv_ref[...] = line.end().astype(BF16)
     block.end()
     mail.close()
 
 
-def last_kernel(parts_ref, w_ref, gu_ref, out_ref, ws_ref, gus_ref, ss, rs, got, held, *bufs):
+def last_kernel(
+    dq_ref, dkv_ref, raw_ref, norm_ref, w_ref, qk_ref, cos_ref, sin_ref,
+    x_ref, dmid_ref, gain_ref, g2_ref, dg_ref, *refs,
+):
+    outer = lax.axis_size("blk") // INNER
+    gu_refs, refs = refs[:outer], refs[outer:]
+    (in_ref, ws_ref, gus_ref, down_ref, small_ref,
+     ss, rs, dqkv, parts, acc, grads, got, held, gu_own, dg_got, small, p_got, z_got, *bufs) = refs
     place = y, c, z, x = here()
     me = rank(y, c, x)
     mail = Mail((ss, rs))
     peers, line = plane_peers(place), line_peers(place)
     greet([p[0] for p in line] + [p[0] for p in peers])
-    base = mail.take(len(line))
-    w_base = mail.take(7)
-    for slot, (dev, forth, _) in enumerate(line):
-        mail.send(base + slot, w_ref.at[:, forth], got.at[slot], dev)
-    rows = PlaneScatter(mail, place, parts_ref, out_ref, bufs)
-    swap = PlaneSwap(mail, place, gu_ref, gus_ref)
+    swap = PlaneSwap(mail, place, gu_own, gus_ref)
+    weights = LineScatter(mail, place, grads, got)
+    down = LineScatter(mail, place, dg_ref, dg_got)
+    total = gu_refs[0][...].astype(F32)
+    for ref in gu_refs[1:]:
+        total = total + ref[...].astype(F32)
+    gu_own[...] = total.astype(BF16).reshape(gu_own.shape)
+    swap.begin()
+
+    count, tok, q_cols = dq_ref.shape
+    size = q_cols // 2
+    gain_q, gain_k = qk_ref[0:1], qk_ref[1:2]
+
+    def one_block(r, sums):
+        cos, sin = turn(cos_ref, sin_ref, r)
+        raw_q, raw_k = raw_ref[r, :, :q_cols], raw_ref[r, :, q_cols:]
+        dq, q_sum = head_back(raw_q, gain_q, cos, sin, size, dq_ref[r].astype(F32))
+        dkv = dkv_ref[r].astype(F32)
+        dk, k_sum = head_back(raw_k, gain_k, cos, sin, size, dkv)
+        dqkv[r, :, :q_cols] = dq.astype(BF16)
+        dqkv[r, :, q_cols:] = jnp.where(lanes(dk.shape) < size, dk, dkv).astype(BF16)
+        return sums[0] + q_sum, sums[1] + k_sum
+
+    zero = jnp.zeros((1, q_cols), F32)
+    q_sum, k_sum = lax.fori_loop(0, count, one_block, (zero, zero))
+
+    width = norm_ref.shape[2]
+    flat = dqkv[...].reshape(count * tok, -1)
+    w_grad = lax.dot_general(
+        norm_ref[...].reshape(count * tok, width),
+        flat,
+        (((0,), (0,)), ((), ())),
+        preferred_element_type=F32,
+    ).astype(BF16)
+    heads, w_rows = grads.shape[1], grads.shape[3]
+    stride = INNER * w_rows
+    for oz in range(outer):
+        for oh in range(heads):
+            first = (oh * outer + oz) * stride
+            grads[oz, oh] = w_grad[first : first + stride].reshape(INNER, w_rows, -1)
+    weights.begin()
+
+    def make(block):
+        parts[block] = lax.dot_general(
+            dqkv[block], w_ref[...], NT, preferred_element_type=F32
+        ).astype(BF16)
+
+    rows = PlaneScatter(mail, place, parts, acc, bufs, make)
     rows.begin()
     rows.middle()
-    swap.begin()
+    down.begin()
     rows.end()
-    total = w_ref[:, z].astype(F32)
-    for slot, (dev, _, _) in enumerate(line):
-        mail.arrive(base + slot, got.at[slot], dev)
-        total = total + got[slot].astype(F32)
-    held[...] = total.reshape(held.shape)
+    back, dgain = rms_back(x_ref[...].astype(F32), gain_ref[0:1], acc[...])
+    in_ref[...] = (dmid_ref[...] + back).astype(BF16)
+    small[...] = jnp.zeros_like(small)
+    small[0:1] = dgain
+    small[1:2] = g2_ref[...]
+    small[2:3, :q_cols] = q_sum
+    small[3:4, :q_cols] = k_sum
+    p_base, z_base, w_base = mail.take(7), mail.take(len(line)), mail.take(7)
+    for slot, (dev, other, _) in enumerate(peers):
+        mail.send(p_base + slot, small, p_got.at[me], dev)
+    p_got[me] = small[...]
+    held[...] = weights.end().reshape(held.shape)
     for slot, (dev, other, _) in enumerate(peers):
         mail.send(w_base + slot, held.at[other], ws_ref.at[me], dev)
     ws_ref[me] = held[me]
     for slot, (dev, other, _) in enumerate(peers):
+        mail.arrive(p_base + slot, p_got.at[other], dev)
+    z_got[z] = jnp.sum(p_got[...], axis=0)
+    for slot, (dev, _, _) in enumerate(line):
+        mail.send(z_base + slot, z_got.at[z], z_got.at[z], dev)
+    swap.end()
+    down_ref[...] = down.end()
+    for slot, (dev, other, _) in enumerate(peers):
         mail.arrive(w_base + slot, ws_ref.at[other], dev)
-    swap.end()
+    for slot, (dev, _, back) in enumerate(line):
+        mail.arrive(z_base + slot, z_got.at[back], dev)
+    small_ref[...] = jnp.sum(z_got[...], axis=0)
     mail.close()
 
 
-def small_kernel(v_ref, out_ref, ss, rs, got, held):
-    place = y, c, z, x = here()
-    me = rank(y, c, x)
-    mail = Mail((ss, rs))
-    peers, line = plane_peers(place), line_peers(place)
-    greet([p[0] for p in line] + [p[0] for p in peers])
-    p_base, z_base = mail.take(7), mail.take(len(line))
-    for slot, (dev, other, _) in enumerate(peers):
-        mail.send(p_base + slot, v_ref, got.at[me], dev)
-    got[me] = v_ref[...]
-    for slot, (dev, other, _) in enumerate(peers):
-        mail.arrive(p_base + slot, got.at[other], dev)
-    held[z] = jnp.sum(got[...], axis=0)
-    for slot, (dev, _, _) in enumerate(line):
-        mail.send(z_base + slot, held.at[z], held.at[z], dev)
-    for slot, (dev, _, back) in enumerate(line):
-        mail.arrive(z_base + slot, held.at[back], dev)
-    out_ref[...] = jnp.sum(held[...], axis=0)
-    mail.close()
+def finish_kernel(own_ref, ws_ref, gus_ref, small_ref, *refs):
+    n1_ref, n2_ref, q_ref, k_ref, v_ref, qk_ref, gate_ref, up_ref = refs[-8:]
+    passed = refs[:-8]
+    for src, dst in zip(passed[: len(passed) // 2], passed[len(passed) // 2 :]):
+        dst[...] = src[...]
+    plane, w_rows, _ = ws_ref.shape
+    q_cols = q_ref.shape[1] // plane
+    k_cols = q_cols // 2
+    for p in range(0, plane, 2):
+        one, two = ws_ref[p], ws_ref[p + 1]
+        q_ref[:, p * q_cols : (p + 1) * q_cols] = one[:, :q_cols]
+        q_ref[:, (p + 1) * q_cols : (p + 2) * q_cols] = two[:, :q_cols]
+        at = slice(p * k_cols, (p + 2) * k_cols)
+        left = lanes((w_rows, q_cols)) < k_cols
+        one, two = one[:, q_cols:], two[:, q_cols:]
+        k_ref[:, at] = jnp.where(left, one, pltpu.roll(two, k_cols, 1))
+        v_ref[:, at] = jnp.where(left, pltpu.roll(one, k_cols, 1), two)
+    width = small_ref.shape[1]
+    move = lax.rem(width - own_ref[0], width)
+    totals = pltpu.roll(small_ref[...], move, 1)
+    n1_ref[...] = totals[0:1, :w_rows]
+    n2_ref[...] = totals[1:2, :w_rows]
+    sums = small_ref[...]
+    query = sums[2:3, :k_cols] + sums[2:3, k_cols : 2 * k_cols]
+    qk_ref[...] = jnp.concatenate([query, sums[3:4, :k_cols]], axis=0)
+    outer = lax.axis_size("blk") // INNER
+    heads = plane // INNER
+    ff = gus_ref.shape[2] // 2
+    main = ff // LANES * LANES
+    tail = ff - main
+    f_rows = ff // outer
+    for col, out in ((0, gate_ref), (1, up_ref)):
+        for oh in range(heads):
+            cols = []
+            for ox in range(INNER):
+                block = gus_ref[oh * INNER + ox].astype(F32)
+                rest = 2 * main + col * tail
+                cols.append(
+                    jnp.concatenate(
+                        [block[:, col * main : (col + 1) * main], block[:, rest : rest + tail]],
+                        axis=1,
+                    )
+                )
+            span = INNER * ff
+            out[:, oh * span : (oh + 1) * span] = jnp.concatenate(
+                [
+                    cols[ox][:, oz * f_rows : (oz + 1) * f_rows]
+                    for oz in range(outer)
+                    for ox in range(INNER)
+                ],
+                axis=1,
+            )
+
+
+def feed_kernel(z_ref, n2_ref, og_ref, wd_ref, *refs):
+    outer = lax.axis_size("blk") // INNER
+    pieces, refs = refs[:outer], refs[outer:]
+    out_ref, dn_ref, dg_ref = refs[:3]
+    chunks = refs[3 : 3 + outer]
+    wgu, hid, dgu, gg = refs[3 + outer :]
+    z = z_ref[0]
+    heads, stride, _ = pieces[0].shape
+    ff = wd_ref.shape[0]
+    main = ff // LANES * LANES
+    tail = ff - main
+    for k, piece in enumerate(pieces):
+        oz = lax.rem(z + outer - k, outer)
+        for oh in range(heads):
+            at = pl.multiple_of((oh * outer + oz) * stride, stride)
+            wgu[pl.ds(at, stride)] = piece[oh]
+    plane, rows, width = n2_ref.shape
+
+    def both(gate, up, dhid):
+        sig = 1.0 / (1.0 + jnp.exp(-gate))
+        act = gate * sig
+        return act * up, dhid * up * (sig * (1.0 + gate * (1.0 - sig))), dhid * act
+
+    def one_block(b, carry):
+        pair = pl.ds(2 * b, 2)
+        at = pl.ds(pl.multiple_of(b * 2 * rows, 2 * rows), 2 * rows)
+        block = n2_ref[pair].reshape(2 * rows, width)
+        grad = og_ref[pair].reshape(2 * rows, width)
+        gu = jnp.dot(block, wgu[...], preferred_element_type=F32)
+        dhid = lax.dot_general(grad, wd_ref[...], NT, preferred_element_type=F32)
+        h, dgate, dup = both(gu[:, :main], gu[:, main : 2 * main], dhid[:, :main])
+        hid[at, :main] = h.astype(BF16)
+        dgu[at, :main] = dgate.astype(BF16)
+        dgu[at, main : 2 * main] = dup.astype(BF16)
+        ends = gu[:, 2 * main :]
+        left = lanes(ends.shape) < tail
+        other = pltpu.roll(ends, tail, 1)
+        dend = dhid[:, main:]
+        dend = jnp.concatenate([dend, dend], axis=1)
+        h, dgate, dup = both(jnp.where(left, ends, other), jnp.where(left, other, ends), dend)
+        hid[at, main:] = h[:, :tail].astype(BF16)
+        dgu[at, 2 * main :] = jnp.where(left, dgate, dup).astype(BF16)
+        down = jnp.dot(hid[at], wd_ref[...], preferred_element_type=F32)
+        out_ref[pair] = down.astype(BF16).reshape(2, rows, width)
+        narrow = lax.dot_general(dgu[at], wgu[...], NT, preferred_element_type=F32)
+        dn_ref[pair] = narrow.astype(BF16).reshape(2, rows, width)
+        return carry
+
+    lax.fori_loop(0, plane // 2, one_block, 0)
+    n2_width = width // heads
+    w_rows = stride // INNER
+
+    def one_head(oh, carry):
+        cols = pl.ds(pl.multiple_of(oh * n2_width, n2_width), n2_width)
+        grad = lax.dot_general(
+            n2_ref[:, :, cols].reshape(plane * rows, n2_width),
+            dgu[...],
+            TN,
+            preferred_element_type=F32,
+        )
+        for oz in range(outer):
+            for ox in range(INNER):
+                first = oz * stride + ox * w_rows
+                gg[oz, oh * INNER + ox] = grad[first : first + w_rows].astype(BF16)
+        return carry
+
+    lax.fori_loop(0, heads, one_head, 0)
+    for k, chunk in enumerate(chunks):
+        chunk[...] = gg[lax.rem(z + k, outer)]
+    grads = og_ref[...].reshape(plane * rows, width)
+    f_rows = ff // outer
+    down = lax.dot_general(hid[...], grads, TN, preferred_element_type=F32)
+    for oz in range(outer):
+        dg_ref[oz] = down[oz * f_rows : (oz + 1) * f_rows].astype(BF16)
 
 
 SPANS = 4
 LOG2E = math.log2(math.e)
-NT = (((1,), (1,)), ((), ()))
-
-
-def lanes(shape):
-    return lax.broadcasted_iota(jnp.int32, shape, len(shape) - 1)
 
 
 def stack_left(block, size):
@@ -669,49 +1021,19 @@
     lax.fori_loop(0, spans, give_rows, 0)
 
 
-def attention(body, name, own, at, args, outs, scratch, flops):
+def local_call(body, name, scalars, args, outs, scratch, flops):
     vmem = pl.BlockSpec(memory_space=pltpu.VMEM)
     smem = pl.BlockSpec(memory_space=pltpu.SMEM)
     return pl.pallas_call(
         body,
         name=name,
         out_shape=tuple(jax.ShapeDtypeStruct(shape, dtype) for shape, dtype in outs),
-        in_specs=[smem, smem] + [vmem] * len(args),
+        in_specs=[smem] * len(scalars) + [vmem] * len(args),
         out_specs=tuple([vmem] * len(outs)),
         scratch_shapes=scratch,
-        cost_estimate=pl.CostEstimate(flops=flops, bytes_accessed=4 << 20, transcendentals=0),
+        cost_estimate=pl.CostEstimate(flops=flops, bytes_accessed=8 << 20, transcendentals=0),
         compiler_params=pltpu.CompilerParams(vmem_limit_bytes=60 * 1024 * 1024),
-    )(own, at, *args)
-
-
-def rms_norm(values, gain_vec):
-    inverse = lax.rsqrt(jnp.mean(values * values, axis=-1, keepdims=True) + EPS)
-    return values * inverse * gain_vec
-
-
-def rotate(field_in, where_at):
-    half_size = field_in.shape[-1] // 2
-    frequency = jnp.exp(
-        jnp.arange(half_size, dtype=F32) * F32(-2.0 * math.log(THETA) / field_in.shape[-1])
-    )
-    angles = where_at.astype(F32)[:, None] * frequency[None, :]
-    cosine = jnp.cos(angles)[:, None, :]
-    sine_part = jnp.sin(angles)[:, None, :]
-    first_half = field_in[..., :half_size]
-    second_half = field_in[..., half_size:]
-    return jnp.concatenate(
-        [
-            first_half * cosine - second_half * sine_part,
-            second_half * cosine + first_half * sine_part,
-        ],
-        axis=-1,
-    )
-
-
-def head_map(raw_rows, gain_vec, where_at):
-    row_count = raw_rows.shape[0]
-    shaped = raw_rows.reshape(row_count, -1, gain_vec.shape[0])
-    return rotate(rms_norm(shaped, gain_vec), where_at).reshape(row_count, -1)
+    )(*scalars, *args)
 
 
 def shifts(outer, step):
@@ -720,29 +1042,6 @@
         for z in range(outer)
         for x in range(INNER)
     ]
-
-
-def line_gather(piece, axis, full_shape, z, outer):
-    full = jnp.zeros(full_shape, piece.dtype)
-    full = lax.dynamic_update_slice_in_dim(full, jnp.expand_dims(piece, axis), z, axis)
-    for step in range(1, outer):
-        got = lax.ppermute(piece, "blk", shifts(outer, step))
-        full = lax.dynamic_update_slice_in_dim(
-            full, jnp.expand_dims(got, axis), (z + outer - step) % outer, axis
-        )
-    return full
-
-
-def line_scatter(parts, axis, z, outer):
-    total = lax.dynamic_index_in_dim(parts, z, axis, keepdims=False).astype(F32)
-    for step in range(1, outer):
-        piece = lax.dynamic_index_in_dim(parts, (z + step) % outer, axis, keepdims=False)
-        total = total + lax.ppermute(piece.astype(BF16), "blk", shifts(outer, step)).astype(F32)
-    return total
-
-
-def dot(a, b):
-    return jnp.dot(a, b, preferred_element_type=F32)
 
 
 def local(
@@ -766,272 +1065,264 @@
     plane = heads * INNER
     z = lax.axis_index("blk") // INNER
     rows, width = block_input.shape
-    head_size = qk_gain.shape[1]
+    size = qk_gain.shape[1]
     w_rows = w_query.shape[0]
     f_rows = w_down.shape[0]
     q_cols = w_query.shape[1] // plane
-    k_cols = key_weight.shape[1] // plane
-    a_cols = q_cols + 2 * k_cols
+    a_cols = 2 * q_cols
     ff = f_rows * outer
-    tokens = plane * rows
-
-    by_place = span_order.reshape(heads, outer, INNER)
-    own_spans = lax.dynamic_index_in_dim(by_place, z, 1, keepdims=False).reshape(plane)
-    all_spans = by_place.transpose(1, 0, 2).reshape(outer * plane)
-    inside = jnp.arange(rows, dtype=jnp.int32)
-    tok_where = (own_spans[:, None] * rows + inside[None, :]).reshape(tokens)
-
-    w8 = jnp.concatenate(
-        [
-            w_query.reshape(w_rows, plane, q_cols),
-            key_weight.reshape(w_rows, plane, k_cols),
-            value_weight.reshape(w_rows, plane, k_cols),
-        ],
-        axis=-1,
-    ).transpose(1, 0, 2)
+    spans = outer * plane
+    n_line = outer - 1
+    stride = INNER * w_rows
 
     def cut(weight):
         shaped = weight.reshape(w_rows, heads, outer, INNER, f_rows)
         return shaped.transpose(1, 3, 0, 2, 4).reshape(plane, w_rows, ff)
 
-    gu8 = jnp.concatenate([cut(w_gate), cut(w_up)], axis=-1)
-    gains = jnp.zeros((16, 128), BF16)
-    gains = gains.at[0, :w_rows].set(norm1_gain).at[1, :w_rows].set(norm2_gain)
-    down_full = line_gather(w_down, 0, (outer, f_rows, width), z, outer).reshape(ff, width)
-
-    n_line = outer - 1
-    x_all, wqkv, gains_all, gu_piece, out_mine = call(
+    main = ff // LANES * LANES
+    gate8, up8 = cut(w_gate), cut(w_up)
+    gu8 = jnp.concatenate(
+        [gate8[..., :main], up8[..., :main], gate8[..., main:], up8[..., main:]], axis=-1
+    )
+
+    x_all, wqkv, gains, gu_piece, out_mine = call(
         start_kernel,
         "start",
         1,
         [
             ((plane, rows, width), BF16),
             ((heads, outer, INNER, w_rows, a_cols), BF16),
-            ((outer, plane, 16, 128), BF16),
+            ((8, width), F32),
             ((plane, w_rows, 2 * ff), BF16),
             ((outer // INNER, INNER, w_rows, width), BF16),
         ],
-        (block_input, w8, gains, gu8, w_out),
+        (
+            block_input,
+            w_query,
+            key_weight,
+            value_weight,
+            norm1_gain.reshape(1, w_rows),
+            norm2_gain.reshape(1, w_rows),
+            gu8,
+            w_out,
+        ),
         14 + 2 * n_line + PlaneGather.COPIES + PlaneSwap.COPIES + outer,
-    )
+        [
+            pltpu.VMEM((plane, w_rows, a_cols), BF16),
+            pltpu.VMEM((16, LANES), BF16),
+            pltpu.VMEM((outer, plane, 16, LANES), BF16),
+        ],
+    )
+    wqkv = wqkv.reshape(width, a_cols)
     out_mine = out_mine.reshape(q_cols, width)
-    wqkv = wqkv.reshape(width, a_cols)
-    gains_all = (
-        gains_all[:, :, :2, :w_rows]
-        .reshape(outer, heads, INNER, 2, w_rows)
-        .transpose(3, 1, 0, 2, 4)
-        .reshape(2, width)
-        .astype(F32)
-    )
-    gain_one, gain_two = gains_all[0], gains_all[1]
-    gu_full = line_gather(
-        gu_piece.reshape(heads, INNER * w_rows, 2 * ff),
-        1,
-        (heads, outer, INNER * w_rows, 2 * ff),
-        z,
-        outer,
-    ).reshape(width, 2 * ff)
-
-    normed = rms_norm(x_all.reshape(tokens, width).astype(F32), gain_one).astype(BF16)
-    qkv_raw = dot(normed, wqkv)
-    q_raw = qkv_raw[:, :q_cols]
-    k_raw = qkv_raw[:, q_cols : q_cols + k_cols]
-    v_raw = qkv_raw[:, q_cols + k_cols :]
-
-    def query_map(raw_rows, gain_vec):
-        return head_map(raw_rows, gain_vec, tok_where)
-
-    queries = query_map(q_raw, qk_gain[0]).astype(BF16)
-    keys = query_map(k_raw, qk_gain[1]).astype(BF16)
-    kv = jnp.concatenate([keys, v_raw.astype(BF16)], axis=-1)
-    kv_all, og_all = call(
+    gu_piece = gu_piece.reshape(heads, stride, 2 * ff)
+    gu_pieces = [gu_piece] + [
+        lax.ppermute(gu_piece, "blk", shifts(outer, step)) for step in range(1, outer)
+    ]
+
+    by_place = span_order.reshape(heads, outer, INNER)
+    own_spans = lax.dynamic_index_in_dim(by_place, z, 1, keepdims=False).reshape(plane)
+    all_spans = by_place.transpose(1, 0, 2).reshape(spans)
+    every = jnp.arange(spans, dtype=jnp.int32)
+    span_at = jnp.sum(jnp.where(all_spans[:, None] == every[None, :], every[:, None], 0), axis=0)
+    where_at = own_spans[:, None] * rows + jnp.arange(rows, dtype=jnp.int32)[None, :]
+    half = size // 2
+    frequency = jnp.exp(jnp.arange(half, dtype=F32) * F32(-2.0 * math.log(THETA) / size))
+    angles = where_at.astype(F32)[:, None, :] * frequency[None, :, None]
+    cosine, sine = jnp.cos(angles), jnp.sin(angles)
+    ones = jnp.ones((size,), F32)
+    qk_rows = jnp.stack(
+        [
+            jnp.concatenate([qk_gain[0], qk_gain[0]]),
+            jnp.concatenate([qk_gain[1], ones]),
+        ]
+    )
+
+    queries, kv_all, raw, normed, og_all = call(
         line_kernel,
         "line",
         2,
-        [((outer, tokens, 2 * k_cols), BF16), ((plane, rows, width), BF16)],
-        (kv, out_grad),
-        n_line + PlaneGather.COPIES,
-    )
-    og_all = og_all.reshape(tokens, width)
-    spans = outer * plane
-    span_at = jnp.sum(
-        jnp.where(
-            all_spans[:, None] == jnp.arange(spans, dtype=jnp.int32)[None, :],
-            jnp.arange(spans, dtype=jnp.int32)[:, None],
-            0,
-        ),
-        axis=0,
-    )
-    q_blocks = queries.reshape(plane, rows, q_cols)
+        [
+            ((plane, rows, q_cols), BF16),
+            ((outer, plane, rows, q_cols), BF16),
+            ((plane, rows, a_cols), F32),
+            ((plane, rows, width), BF16),
+            ((plane, rows, width), BF16),
+        ],
+        (x_all, wqkv, gains, qk_rows, cosine, sine, out_grad),
+        2 * n_line + PlaneGather.COPIES,
+        [pltpu.VMEM((plane, rows, q_cols), BF16)],
+    )
     kv_blocks = kv_all.reshape(spans, rows, q_cols)
-    attended, log_total = attention(
+    pairs = plane * rows * spans * rows * q_cols
+    attended, log_total = local_call(
         forward_kernel,
         "attend",
-        own_spans,
-        span_at,
-        (q_blocks, kv_blocks),
+        (own_spans, span_at),
+        (queries, kv_blocks),
         [((plane, rows, q_cols), BF16), ((plane, 8, 2 * rows), F32)],
         [pltpu.VMEM((spans * rows, q_cols), BF16), pltpu.VMEM((spans * rows, q_cols), BF16)],
-        8 * tokens * spans * rows * q_cols,
-    )
-    attended_rows = attended.reshape(tokens, q_cols)
-
-    def scatter(parts, name, ident):
-        return call(
-            scatter_kernel,
-            name,
-            ident,
-            [((rows, width), F32)],
-            (parts.astype(BF16).reshape(plane, rows, width),),
-            PlaneScatter.COPIES,
-            PlaneScatter.scratch(rows, width),
-        )[0]
-
-    def gather(block, name, ident):
-        return call(
-            gather_kernel,
-            name,
-            ident,
-            [((plane, rows, width), BF16)],
-            (block,),
-            PlaneGather.COPIES,
-        )[0].reshape(tokens, width)
-
-    in_flat = block_input.astype(F32)
-    middle = in_flat + scatter(dot(attended_rows, out_mine), "mix", 3)
-    normed2_own = rms_norm(middle, gain_two).astype(BF16)
-    normed2 = gather(normed2_own, "widen", 4)
-
-    gu_rows = dot(normed2, gu_full)
-    gate_rows, up_rows = gu_rows[:, :ff], gu_rows[:, ff:]
-    hidden, gate_back = jax.vjp(lambda a, b: jax.nn.silu(a) * b, gate_rows, up_rows)
-    hidden = hidden.astype(BF16)
-    dhidden = dot(og_all, down_full.T)
-    dgate, dup = gate_back(dhidden)
-    dgu = jnp.concatenate([dgate.astype(BF16), dup.astype(BF16)], axis=-1)
-    dnormed2 = scatter(dot(dgu, gu_full.T), "narrow", 5)
-    out_parts = dot(hidden, down_full).astype(BF16).reshape(plane, rows, width)
-    gu_grad = dot(normed2.T, dgu)
-    down_grad = dot(hidden.T, og_all)
-    down_grad = line_scatter(down_grad.reshape(outer, f_rows, width), 0, z, outer)
-    gu_grad = line_scatter(
-        gu_grad.reshape(heads, outer, INNER * w_rows, 2 * ff), 1, z, outer
-    ).reshape(plane, w_rows, 2 * ff)
-
-    _, norm2_back = jax.vjp(rms_norm, middle, gain_two)
-    dmiddle_norm, norm2_grad = norm2_back(dnormed2)
-    dmiddle = out_grad.astype(F32) + dmiddle_norm
-    dmid_all = gather(dmiddle.astype(BF16), "spread", 6)
-
-    out_proj = dot(attended_rows.T, dmid_all)
-    dattended = dot(dmid_all, out_mine.T).astype(BF16)
-    dqueries, dkv = attention(
+        4 * pairs,
+    )
+    middle, normed2, down_full = call(
+        mix_kernel,
+        "mix",
+        3,
+        [((rows, width), F32), ((plane, rows, width), BF16), ((outer, f_rows, width), BF16)],
+        (attended, out_mine, block_input, gains, w_down),
+        n_line + PlaneScatter.COPIES + PlaneGather.COPIES,
+        [pltpu.VMEM((plane, rows, width), BF16), pltpu.VMEM((rows, width), BF16)]
+        + PlaneScatter.scratch(rows, width),
+    )
+    down_full = down_full.reshape(ff, width)
+
+    out_parts, dn_parts, down_grad, *gu_grads = local_call(
+        feed_kernel,
+        "feed",
+        (jnp.reshape(z, (1,)).astype(jnp.int32),),
+        (normed2, og_all, down_full, *gu_pieces),
+        [
+            ((plane, rows, width), BF16),
+            ((plane, rows, width), BF16),
+            ((outer, f_rows, width), BF16),
+        ]
+        + [((plane, w_rows, 2 * ff), BF16)] * outer,
+        [
+            pltpu.VMEM((width, 2 * ff), BF16),
+            pltpu.VMEM((plane * rows, ff), BF16),
+            pltpu.VMEM((plane * rows, 2 * ff), BF16),
+            pltpu.VMEM((outer, plane, w_rows, 2 * ff), BF16),
+        ],
+        18 * plane * rows * width * ff,
+    )
+    gu_sums = [gu_grads[0]] + [
+        lax.ppermute(gu_grads[step], "blk", shifts(outer, step)) for step in range(1, outer)
+    ]
+    dmiddle, dmid_all, norm2_grad = call(
+        narrow_kernel,
+        "narrow",
+        4,
+        [((rows, width), F32), ((plane, rows, width), BF16), ((1, width), F32)],
+        (dn_parts, middle, out_grad, gains),
+        PlaneScatter.COPIES + PlaneGather.COPIES,
+        [pltpu.VMEM((rows, width), BF16)] + PlaneScatter.scratch(rows, width),
+    )
+
+    dmid_rows = dmid_all.reshape(plane * rows, width)
+    out_proj = lax.dot_general(
+        attended.reshape(plane * rows, q_cols), dmid_rows, TN, preferred_element_type=F32
+    )
+    dattended = lax.dot_general(dmid_rows, out_mine, NT, preferred_element_type=F32).astype(BF16)
+    dqueries, dkv = local_call(
         backward_kernel,
         "attend_back",
-        own_spans,
-        span_at,
-        (q_blocks, kv_blocks, attended, dattended.reshape(plane, rows, q_cols), log_total),
+        (own_spans, span_at),
+        (queries, kv_blocks, attended, dattended.reshape(plane, rows, q_cols), log_total),
         [((plane, rows, q_cols), BF16), ((spans, rows, q_cols), BF16)],
         [
             pltpu.VMEM((spans * rows, q_cols), BF16),
             pltpu.VMEM((q_cols, spans * rows), BF16),
             pltpu.VMEM((spans * rows, q_cols), F32),
         ],
-        20 * tokens * spans * rows * q_cols,
-    )
-    dkv_own, ffn_out, out_proj_grad = call(
+        10 * pairs,
+    )
+    dkv_own, block_output, out_proj_grad = call(
         back_kernel,
         "back",
-        7,
-        [((tokens, 2 * k_cols), F32), ((rows, width), F32), ((w_rows, width), F32)],
+        5,
+        [((plane, rows, q_cols), BF16), ((rows, width), BF16), ((w_rows, width), F32)],
         (
-            dkv.reshape(outer, tokens, 2 * k_cols),
+            dkv.reshape(outer, plane, rows, q_cols),
             out_parts,
             out_proj.astype(BF16).reshape(outer // INNER, INNER, w_rows, width),
+            middle,
         ),
         n_line + PlaneScatter.COPIES + outer,
         [
-            pltpu.VMEM((n_line, tokens, 2 * k_cols), BF16),
+            pltpu.VMEM((rows, width), F32),
+            pltpu.VMEM((n_line, plane, rows, q_cols), BF16),
             pltpu.VMEM((outer, w_rows, width), BF16),
         ]
         + PlaneScatter.scratch(rows, width),
     )
-    block_output = (middle + ffn_out).astype(BF16)
-    dkv_own = dkv_own.astype(BF16)
-    dqueries = dqueries.reshape(tokens, q_cols)
-    _, query_back = jax.vjp(query_map, q_raw, qk_gain[0])
-    dq_raw, qgain_grad = query_back(dqueries.astype(F32))
-    _, key_back = jax.vjp(query_map, k_raw, qk_gain[1])
-    dk_raw, kgain_grad = key_back(dkv_own[:, :k_cols].astype(F32))
-    dqkv = jnp.concatenate(
-        [dq_raw.astype(BF16), dk_raw.astype(BF16), dkv_own[:, k_cols:]], axis=-1
-    )
-    wqkv_grad = dot(normed.T, dqkv).astype(BF16)
-    dnormed, wqkv_own, gu_own = call(
+    input_grad, w_own, gu_own, down_out, small = call(
         last_kernel,
         "last",
-        8,
+        6,
         [
-            ((rows, width), F32),
+            ((rows, width), BF16),
             ((plane, w_rows, a_cols), F32),
             ((plane, w_rows, 2 * ff), BF16),
+            ((f_rows, width), F32),
+            ((8, width), F32),
         ],
         (
-            dot(dqkv, wqkv.T).astype(BF16).reshape(plane, rows, width),
-            wqkv_grad.reshape(heads, outer, INNER, w_rows, a_cols),
-            gu_grad.astype(BF16),
+            dqueries,
+            dkv_own,
+            raw,
+            normed,
+            wqkv,
+            qk_rows,
+            cosine,
+            sine,
+            block_input,
+            dmiddle,
+            gains,
+            norm2_grad,
+            down_grad,
+            *gu_sums,
         ),
-        n_line + 7 + PlaneScatter.COPIES + PlaneSwap.COPIES,
+        3 * n_line + 14 + PlaneScatter.COPIES + PlaneSwap.COPIES,
         [
+            pltpu.VMEM((plane, rows, a_cols), BF16),
+            pltpu.VMEM((plane, rows, width), BF16),
+            pltpu.VMEM((rows, width), F32),
+            pltpu.VMEM((outer, heads, INNER, w_rows, a_cols), BF16),
             pltpu.VMEM((n_line, heads, INNER, w_rows, a_cols), BF16),
             pltpu.VMEM((plane, w_rows, a_cols), F32),
+            pltpu.VMEM((plane, w_rows, 2 * ff), BF16),
+            pltpu.VMEM((n_line, f_rows, width), BF16),
+            pltpu.VMEM((8, width), F32),
+            pltpu.VMEM((plane, 8, width), F32),
+            pltpu.VMEM((outer, 8, width), F32),
         ]
         + PlaneScatter.scratch(rows, width),
     )
-    _, norm1_back = jax.vjp(rms_norm, in_flat, gain_one)
-    dinput_norm, norm1_grad = norm1_back(dnormed)
-    input_grad = (dmiddle + dinput_norm).astype(BF16)
-
-    small = jnp.concatenate([norm1_grad, norm2_grad, qgain_grad, kgain_grad])
-    small_rows = -(-small.shape[0] // 1024) * 8
-    small = jnp.pad(small, (0, small_rows * 128 - small.shape[0])).reshape(small_rows, 128)
-    summed = call(
-        small_kernel,
-        "small",
-        9,
-        [((small_rows, 128), F32)],
-        (small,),
-        7 + n_line,
-        [pltpu.VMEM((plane, small_rows, 128), F32), pltpu.VMEM((outer, small_rows, 128), F32)],
-    )[0].reshape(-1)
     own = (lax.axis_index("head") * blocks + lax.axis_index("blk")) * w_rows
-    norm1_out = lax.dynamic_slice_in_dim(summed, own, w_rows)
-    norm2_out = lax.dynamic_slice_in_dim(summed, width + own, w_rows)
-    qk_gain_grad = summed[2 * width : 2 * width + 2 * head_size].reshape(2, head_size)
-
-    def columns(blocks_in):
-        return blocks_in.transpose(1, 0, 2).reshape(w_rows, -1)
-
-    query_grad = columns(wqkv_own[:, :, :q_cols])
-    key_grad = columns(wqkv_own[:, :, q_cols : q_cols + k_cols])
-    value_grad = columns(wqkv_own[:, :, q_cols + k_cols :])
-
-    def uncut(blocks_in):
-        shaped = blocks_in.astype(F32).reshape(heads, INNER, w_rows, outer, f_rows)
-        return shaped.transpose(2, 0, 3, 1, 4).reshape(w_rows, -1)
-
-    gate_grad = uncut(gu_own[:, :, :ff])
-    up_grad = uncut(gu_own[:, :, ff:])
+    outs = local_call(
+        finish_kernel,
+        "finish",
+        (jnp.reshape(own, (1,)).astype(jnp.int32),),
+        (w_own, gu_own, small, block_output, input_grad, out_proj_grad, down_out),
+        [
+            ((rows, width), BF16),
+            ((rows, width), BF16),
+            ((w_rows, width), F32),
+            ((f_rows, width), F32),
+            ((1, w_rows), F32),
+            ((1, w_rows), F32),
+            (w_query.shape, F32),
+            (key_weight.shape, F32),
+            (value_weight.shape, F32),
+            ((2, size), F32),
+            (w_gate.shape, F32),
+            (w_up.shape, F32),
+        ],
+        [],
+        1 << 20,
+    )
+    (block_output, input_grad, out_proj_grad, down_grad, norm1_grad, norm2_grad,
+     query_grad, key_grad, value_grad, qk_gain_grad, gate_grad, up_grad) = outs
     return (
         block_output,
         input_grad,
-        norm1_out,
+        norm1_grad.reshape(w_rows),
         query_grad,
         key_grad,
         value_grad,
         qk_gain_grad,
         out_proj_grad,
-        norm2_out,
+        norm2_grad.reshape(w_rows),
         gate_grad,
         up_grad,
         down_grad,

time: 453 us -> 371 us (0.82); the launches traced: 447 us -> 370 us
  Pallas kernels: 281 us -> 339 us
  local copies, waits for them, and re-layouts: 52.7 us -> 7.48 us
  other arithmetic: 38 us -> 2.58 us
  matrix products: 32 us -> 4.33 us
  waiting for transfers between devices: 14.8 us -> 0.02 us
  starting transfers between devices: 26.1 us -> 15.3 us
    pallas_call x2 -> x4, Pallas kernels: 43.1 us -> 74.1 us  [local_call(): pl.pallas_call(body, name=name, out_shape=tuple((jax.ShapeDtypeStruct(sha...]
    dot_general x12 -> x2, matrix products: 32 us -> 4.33 us  [the longest x1 2.92 us: local(): lax.dot_general(attended.reshape(plane * rows, q_cols), dmid_rows, TN, pr...]
    pallas_call x9 -> x6, Pallas kernels: 238 us -> 265 us  [call(): pl.pallas_call(body, name=name, out_shape=tuple((jax.ShapeDtypeStruct(sha...]
    ppermute x12 -> x6, waiting for transfers between devices: 14.8 us -> 0.02 us  [the longest x3 0.01 us: local(): lax.ppermute(gu_piece, 'blk', shifts(outer, step))]
    reshape x16 -> x0, local copies, waits for them, and re-layouts: 12.9 us -> none  [the longest x6 8.38 us: uncut(): return shaped.transpose(2, 0, 3, 1, 4).reshape(w_rows, -1)]
    convert_element_type x11 -> x1, other arithmetic: 12.7 us -> 0.07 us  [local(): angles = where_at.astype(F32)[:, None, :] * frequency[None, :, None]]
    ppermute x12 -> x6, starting transfers between devices: 26.1 us -> 15.3 us  [the longest x3 9.25 us: local(): lax.ppermute(gu_piece, 'blk', shifts(outer, step))]
    dynamic_update_slice x8 -> x0, local copies, waits for them, and re-layouts: 9.64 us -> none  [the longest x6 7.79 us: line_gather(): lax.dynamic_update_slice_in_dim(full, jnp.expand_dims(got, axis), (z + ou...]
  transfers between devices with their start and end apart: 12 -> 6, of which waited for: 2 -> 0; matrix products, arithmetic and copies ran while one was open for 17% -> 1% of each run, Pallas kernels for 47% -> 55%
where the time goes in v3:
time: 371 us; the launch traced here: 370 us
  Pallas kernels  339 us (91%)
  starting transfers between devices  15.3 us (4%)
  local copies, waits for them, and re-layouts  7.48 us (2%)
  matrix products  4.33 us (1%)
    pallas_call x6, Pallas kernels, call(): pl.pallas_call(body, name=name, out_shape=tuple((jax.ShapeDtypeStruct(sha...  265 us
    pallas_call x4, Pallas kernels, local_call(): pl.pallas_call(body, name=name, out_shape=tuple((jax.ShapeDtypeStruct(sha...  74.1 us
    ppermute x3, starting transfers between devices, local(): lax.ppermute(gu_piece, 'blk', shifts(outer, step))  9.25 us
  transfers between devices with their start and end apart: 6, of which 0 were waited for; matrix products, arithmetic and copies ran while one was open for 1% of the time, Pallas kernels for 55%

profile of v3, /device:TPU:0, one launch (start us, length us, event | category | flops | bytes accessed | tf_op | source)
XLA Modules:
  0.0 370.0 jit_solution(16723440196018263993)
XLA Ops:
  0.7 1.9 reshape.126
  2.5 0.2 copy.41
  2.7 0.3 reshape.127
  3.1 0.9 reshape.128
  4.0 0.2 copy.40
  4.2 0.0 copy-start.7
  4.2 0.0 copy-start.8
  4.2 0.3 reshape.129
  4.6 1.0 concatenate.9.gu_ref
  5.6 30.4 %start.1 = (bf16[8,128,1024]{2,1,0:T(8,128)(2,1)}, bf16[4,4,2,32,256]{4,3,2,1,0:T(8,128)(2,1)}, f32[8,1024]{1,0:T(8,128)}, bf16[8,32,1152]{2,1,0:T(8,128)(2,1)}, bf16[2,2,32,1024]{3,2,1,0:T(8,128)(2,1)}) custom-call(bf16[128,1024]{1,0:T(8,128)(2,1)} %x_ref.5, bf16[32,1024]{1,0:T(8,128)(2,1)} %q_ref.1, bf16[32,512]{1,0:T(8,128)(2,1)} %k_ref.1, ...), custom_call_target="tpu_custom_call" | custom-call | tf_op jit(solution)/shard_map/start/pallas_call | solution.py:405
  36.0 8.6 %collective-permute-start.2 = (bf16[4,64,1152]{2,1,0:T(8,128)(2,1)}, bf16[4,64,1152]{2,1,0:T(8,128)(2,1)S(1)}, u32[]{:S(2)}, u32[]{:S(2)}) collective-permute-start(bf16[4,64,1152]{2,1,0:T(8,128)(2,1)} %bitcast.54), channel_id=1, source_target_pairs={{0,6},{1,7},{2,0},{3,1},{4,2},{5,3},{6,4},{7,5},{8,14},{9,15},{10,... | collective-permute-start | bytes 1769480 | tf_op jit(solution)/shard_map/ppermute | solution.py:1120
  44.6 0.0 collective-permute-start.1
  44.6 0.6 collective-permute-start
  45.3 0.1 reshape.122
  45.4 0.1 reshape.123.own_ref
  45.5 0.1 add_convert_fusion
  45.6 0.1 maximum_bitcast_fusion
  45.6 0.6 pad_maximum_fusion.qk_ref
  46.2 0.1 eq.15
  46.3 1.2 multiply_sine_fusion
  47.6 70.1 %line.1 = (bf16[8,128,128]{2,1,0:T(8,128)(2,1)}, bf16[4,8,128,128]{3,2,1,0:T(8,128)(2,1)}, f32[8,128,256]{2,1,0:T(8,128)}, bf16[8,128,1024]{2,1,0:T(8,128)(2,1)}, bf16[8,128,1024]{2,1,0:T(8,128)(2,1)}) custom-call(bf16[8,128,1024]{2,1,0:T(8,128)(2,1)} %get-tuple-element.59.x_ref, bf16[1024,256]{1,0:T(8,128)(2,1)} %bitcast.39, ...), custom_call_target="tpu_custom_call" | custom-call | tf_op jit(solution)/shard_map/line/pallas_call | solution.py:405
  117.7 0.6 select_reduce_fusion.at_ref
  118.3 20.6 %attend.1 = (bf16[8,128,128]{2,1,0:T(8,128)(2,1)}, f32[8,8,256]{2,1,0:T(8,128)}) custom-call(s32[8]{0:T(128)} %copy-done.9, s32[32]{0:T(128)} %select_reduce_fusion.at_ref, bf16[8,128,128]{2,1,0:T(8,128)(2,1)} %get-tuple-element.62.q_ref, bf16[32,128,128]{2,1,0:T(8,128)(2,1)} %bitcast.52), custom_call_target="tpu_custom_call" | custom-call | flops 2147483648 | bytes 8388608 | tf_op jit(solution)/shard_map/attend/pallas_call | solution.py:1027
  138.9 32.4 %mix.1 = (f32[128,1024]{1,0:T(8,128)}, bf16[8,128,1024]{2,1,0:T(8,128)(2,1)}, bf16[4,144,1024]{2,1,0:T(8,128)(2,1)}) custom-call(bf16[8,128,128]{2,1,0:T(8,128)(2,1)} %get-tuple-element.64.att_ref.out_ref, bf16[128,1024]{1,0:T(8,128)(2,1)} %bitcast.43, bf16[128,1024]{1,0:T(8,128)(2,1)} %x_ref.5, f32[8,1024]{1,0:T(8,128)} %get-tuple-element.61.gain_ref, ...), custom_call_target="tpu_custom_call" | custom-call | tf_op jit(solution)/shard_map/mix/pallas_call | solution.py:405
  171.3 0.0 collective-permute-done.2.refs_3_
  171.3 0.0 copy-start.10
  171.3 0.0 copy-start.11
  171.4 0.0 copy-start.12
  171.4 0.8 copy-done.10
  172.1 0.2 copy-done.11
  172.3 0.2 copy-done.12
  172.5 19.6 %feed.1 = (bf16[8,128,1024]{2,1,0:T(8,128)(2,1)}, bf16[8,128,1024]{2,1,0:T(8,128)(2,1)}, bf16[4,144,1024]{2,1,0:T(8,128)(2,1)}, bf16[8,32,1152]{2,1,0:T(8,128)(2...) custom-call(s32[1]{0:T(128)} %bitcast.12.z_ref, ...), custom_call_target="tpu_custom_call" | custom-call | flops 10871635968 | bytes 8388608 | tf_op jit(solution)/shard_map/feed/pallas_call | solution.py:1027
  192.1 27.5 %narrow.1 = (f32[128,1024]{1,0:T(8,128)}, bf16[8,128,1024]{2,1,0:T(8,128)(2,1)}, f32[1,1024]{1,0:T(1,128)}) custom-call(bf16[8,128,1024]{2,1,0:T(8,128)(2,1)} %get-tuple-element.70.parts_ref, f32[128,1024]{1,0:T(8,128)} %get-tuple-element.71.mid_ref, bf16[128,1024]{1,0:T(8,128)(2,1)} %og_ref.3, f32[8,1024]{1,0:T(8,128)} %get-tuple-element.61.gain_ref), custom_call_target="tpu_custom_call" | custom-call | tf_op jit(solution)/shard_map/narrow/pallas_call | solution.py:405
  219.6 2.9 fusion
  222.6 3.6 collective-permute-start.3
  226.2 2.3 collective-permute-start.4
  228.5 0.1 collective-permute-start.5
  228.7 1.4 convolution_convert_fusion
  230.1 30.5 %attend_back.1 = (bf16[8,128,128]{2,1,0:T(8,128)(2,1)}, bf16[32,128,128]{2,1,0:T(8,128)(2,1)}) custom-call(s32[8]{0:T(128)} %copy-done.9, s32[32]{0:T(128)} %select_reduce_fusion.at_ref, bf16[8,128,128]{2,1,0:T(8,128)(2,1)} %get-tuple-element.62.q_ref, bf16[32,128,128]{2,1,0:T(8,128)(2,1)} %bitcast.53, ...), custom_call_target="tpu_custom_call" | custom-call | flops 5368709120 | bytes 8388608 | tf_op jit(solution)/shard_map/attend_back/pallas_call | solution.py:1027
  260.6 50.1 %back.1 = (bf16[8,128,128]{2,1,0:T(8,128)(2,1)}, bf16[128,1024]{1,0:T(8,128)(2,1)}, f32[32,1024]{1,0:T(8,128)}) custom-call(bf16[4,8,128,128]{3,2,1,0:T(8,128)(2,1)} %bitcast.45, bf16[8,128,1024]{2,1,0:T(8,128)(2,1)} %get-tuple-element.76.parts_ref, bf16[2,2,32,1024]{3,2,1,0:T(8,128)(2,1)} %bitcast.46, f32[128,1024]{1,0:T(8,128)} %get-tuple-element.71.mid_ref), custom_call_target="tpu_custom_call" | custom-call | tf_op jit(solution)/shard_map/back/pallas_call | solution.py:405
  310.7 0.0 copy-start.3
  310.7 0.0 copy-start.4
  310.8 0.0 copy-start.5
  310.8 0.8 copy-done.3
  311.5 0.2 copy-done.4
  311.7 0.2 copy-done.5
  311.9 54.6 %last.1 = (bf16[128,1024]{1,0:T(8,128)(2,1)}, f32[8,32,256]{2,1,0:T(8,128)}, bf16[8,32,1152]{2,1,0:T(8,128)(2,1)}, f32[144,1024]{1,0:T(8,128)}, f32[8,1024]{1,0:T(8,128)}) custom-call(bf16[8,128,128]{2,1,0:T(8,128)(2,1)} %get-tuple-element.74.dq_ref, bf16[8,128,128]{2,1,0:T(8,128)(2,1)} %get-tuple-element.77.dkv_ref, ...), custom_call_target="tpu_custom_call" | custom-call | tf_op jit(solution)/shard_map/last/pallas_call | solution.py:405
  366.6 3.4 finish.1
  (32 shorter events, 0.2 us)
Async XLA Ops:
  0.6 2.5 copy-start.6
  4.2 41.1 %copy-start.7 = (f32[2,64]{1,0:T(2,128)S(1)}, f32[2,64]{1,0:T(2,128)}, u32[]{:S(2)}) copy-start(f32[2,64]{1,0:T(2,128)} %param.19) | copy-start | bytes 1540
  4.2 41.0 %copy-start.8 = (s32[32]{0:T(128)S(1)}, s32[32]{0:T(128)}, u32[]{:S(2)}) copy-start(s32[32]{0:T(128)} %param.14) | copy-start | bytes 388
  36.0 135.3 %collective-permute-start.2 = (bf16[4,64,1152]{2,1,0:T(8,128)(2,1)}, bf16[4,64,1152]{2,1,0:T(8,128)(2,1)S(1)}, u32[]{:S(2)}, u32[]{:S(2)}) collective-permute-start(bf16[4,64,1152]{2,1,0:T(8,128)(2,1)} %bitcast.54), channel_id=1, source_target_pairs={{0,6},{1,7},{2,0},{3,1},{4,2},{5,3},{6,4},{7,5},{8,14},{9,15},{10,... | collective-permute-start | bytes 1769480 | tf_op jit(solution)/shard_map/ppermute | solution.py:1120
  44.6 126.7 %collective-permute-start.1 = (bf16[4,64,1152]{2,1,0:T(8,128)(2,1)}, bf16[4,64,1152]{2,1,0:T(8,128)(2,1)S(1)}, u32[]{:S(2)}, u32[]{:S(2)}) collective-permute-start(bf16[4,64,1152]{2,1,0:T(8,128)(2,1)} %bitcast.55), channel_id=1, source_target_pairs={{0,4},{1,5},{2,6},{3,7},{4,0},{5,1},{6,2},{7,3},{8,12},{9,13},{10,... | collective-permute-start | bytes 1769480 | tf_op jit(solution)/shard_map/ppermute | solution.py:1120
  44.6 126.7 %collective-permute-start = (bf16[4,64,1152]{2,1,0:T(8,128)(2,1)}, bf16[4,64,1152]{2,1,0:T(8,128)(2,1)S(1)}, u32[]{:S(2)}, u32[]{:S(2)}) collective-permute-start(bf16[4,64,1152]{2,1,0:T(8,128)(2,1)} %bitcast.56), channel_id=1, source_target_pairs={{0,2},{1,3},{2,4},{3,5},{4,6},{5,7},{6,0},{7,1},{8,10},{9,11},{10,... | collective-permute-start | bytes 1769480 | tf_op jit(solution)/shard_map/ppermute | solution.py:1120
  45.5 72.8 %copy-start.9 = (s32[8]{0:T(128)}, s32[8]{0:T(128)S(1)}, u32[]{:S(2)}) copy-start(s32[8]{0:T(128)S(1)} %reshape.123.own_ref) | copy-start | bytes 100
  171.3 0.8 copy-start.10
  171.3 1.0 copy-start.11
  171.4 1.2 copy-start.12
  192.1 27.6 %copy-start.2 = (bf16[8,128,128]{2,1,0:T(8,128)(2,1)S(1)}, bf16[8,128,128]{2,1,0:T(8,128)(2,1)}, u32[]{:S(2)}) copy-start(bf16[8,128,128]{2,1,0:T(8,128)(2,1)} %get-tuple-element.64.att_ref.out_ref) | copy-start | bytes 786436
  192.1 30.5 %copy-start.15 = (bf16[8,32,1152]{2,1,0:T(8,128)(2,1)S(1)}, bf16[8,32,1152]{2,1,0:T(8,128)(2,1)}, u32[]{:S(2)}) copy-start(bf16[8,32,1152]{2,1,0:T(8,128)(2,1)} %get-tuple-element.84) | copy-start | bytes 1769476
  192.1 34.1 %copy-start.14 = (bf16[8,32,1152]{2,1,0:T(8,128)(2,1)S(1)}, bf16[8,32,1152]{2,1,0:T(8,128)(2,1)}, u32[]{:S(2)}) copy-start(bf16[8,32,1152]{2,1,0:T(8,128)(2,1)} %get-tuple-element.85) | copy-start | bytes 1769476
  192.1 36.4 %copy-start.13 = (bf16[8,32,1152]{2,1,0:T(8,128)(2,1)S(1)}, bf16[8,32,1152]{2,1,0:T(8,128)(2,1)}, u32[]{:S(2)}) copy-start(bf16[8,32,1152]{2,1,0:T(8,128)(2,1)} %get-tuple-element.86) | copy-start | bytes 1769476
  192.1 36.5 %copy-start.1 = (bf16[2,2,32,1024]{3,2,1,0:T(8,128)(2,1)S(1)}, bf16[2,2,32,1024]{3,2,1,0:T(8,128)(2,1)}, u32[]{:S(2)}) copy-start(bf16[2,2,32,1024]{3,2,1,0:T(8,128)(2,1)} %get-tuple-element.65) | copy-start | bytes 786436
  219.6 9.0 %copy-start = (bf16[8,128,1024]{2,1,0:T(8,128)(2,1)S(1)}, bf16[8,128,1024]{2,1,0:T(8,128)(2,1)}, u32[]{:S(2)}) copy-start(bf16[8,128,1024]{2,1,0:T(8,128)(2,1)} %get-tuple-element.72) | copy-start | bytes 6291460
  222.6 88.1 %collective-permute-start.3 = (bf16[8,32,1152]{2,1,0:T(8,128)(2,1)S(1)}, bf16[8,32,1152]{2,1,0:T(8,128)(2,1)S(1)}, u32[]{:S(2)}, u32[]{:S(2)}) collective-permute-start(bf16[8,32,1152]{2,1,0:T(8,128)(2,1)S(1)} %copy-done.15), channel_id=1, source_target_pairs={{0,2},{1,3},{2,4},{3,5},{4,6},{5,7},{6,0},{7,1},{8,10},{9,11},{10,... | collective-permute-start | bytes 1769480 | tf_op jit(solution)/shard_map/ppermute | solution.py:1199
  226.2 84.5 %collective-permute-start.4 = (bf16[8,32,1152]{2,1,0:T(8,128)(2,1)S(1)}, bf16[8,32,1152]{2,1,0:T(8,128)(2,1)S(1)}, u32[]{:S(2)}, u32[]{:S(2)}) collective-permute-start(bf16[8,32,1152]{2,1,0:T(8,128)(2,1)S(1)} %copy-done.14), channel_id=1, source_target_pairs={{0,4},{1,5},{2,6},{3,7},{4,0},{5,1},{6,2},{7,3},{8,12},{9,13},{10,... | collective-permute-start | bytes 1769480 | tf_op jit(solution)/shard_map/ppermute | solution.py:1199
  228.5 82.2 %collective-permute-start.5 = (bf16[8,32,1152]{2,1,0:T(8,128)(2,1)S(1)}, bf16[8,32,1152]{2,1,0:T(8,128)(2,1)S(1)}, u32[]{:S(2)}, u32[]{:S(2)}) collective-permute-start(bf16[8,32,1152]{2,1,0:T(8,128)(2,1)S(1)} %copy-done.13), channel_id=1, source_target_pairs={{0,6},{1,7},{2,0},{3,1},{4,2},{5,3},{6,4},{7,5},{8,14},{9,15},{10,... | collective-permute-start | bytes 1769480 | tf_op jit(solution)/shard_map/ppermute | solution.py:1199
  310.7 0.8 copy-start.3
  310.7 1.0 copy-start.4
  310.8 1.2 copy-start.5

commit v4 on v3

--- a/solution.py
+++ b/solution.py
@@ -1,4 +1,3 @@
-import functools
 import math
 
 import jax
@@ -7,6 +6,7 @@
 from jax.experimental import pallas as pl
 from jax.experimental.pallas import tpu as pltpu
 from jax.sharding import PartitionSpec as P
+
 
 EPS = 1e-05
 THETA = 1000000.0
@@ -109,7 +109,7 @@
         self.top, self.bot = pl.ds(0, half), pl.ds(half, half)
 
     def begin(self):
-        y, c, z, x = self.place
+        y, c, _, x = self.place
         pair, xn, yn = near(self.place)
         me = rank(y, c, x)
         send, base, src, out = self.mail.send, self.base, self.src, self.out
@@ -122,7 +122,7 @@
         out[me] = src[...]
 
     def middle(self):
-        y, c, z, x = self.place
+        y, c, _, x = self.place
         pair, xn, yn = near(self.place)
         xr, yr = rank(y, c, 1 - x), rank(1 - y, c, x)
         send, arrive, base, out = self.mail.send, self.mail.arrive, self.base, self.out
@@ -137,7 +137,7 @@
         send(base + 8, out.at[yr], out.at[yr], pair)
 
     def end(self):
-        y, c, z, x = self.place
+        y, c, _, x = self.place
         pair, xn, yn = near(self.place)
         dr = rank(1 - y, c, 1 - x)
         send, arrive, base, out = self.mail.send, self.mail.arrive, self.base, self.out
@@ -177,8 +177,8 @@
         ]
 
     def begin(self):
-        y, c, z, x = self.place
-        pair, xn, yn = near(self.place)
+        y, c, _, x = self.place
+        pair, _, _ = near(self.place)
         for slot, (py, px) in enumerate(((1 - y, 1 - x), (y, 1 - x), (1 - y, x), (y, x))):
             self.make(rank(py, 1 - c, px))
             self.mail.send(
@@ -189,15 +189,15 @@
             )
 
     def joined(self, slot, py, px):
-        y, c, z, x = self.place
-        pair, xn, yn = near(self.place)
+        _, c, _, _ = self.place
+        pair, _, _ = near(self.place)
         self.make(rank(py, c, px))
         self.mail.arrive(self.base + slot, self.first.at[py, px], pair)
         return self.parts[rank(py, c, px)].astype(F32) + self.first[py, px].astype(F32)
 
     def middle(self):
-        y, c, z, x = self.place
-        pair, xn, yn = near(self.place)
+        y, _, _, x = self.place
+        _, xn, yn = near(self.place)
         send, base, held = self.mail.send, self.base, self.held
         top, bot = self.top, self.bot
         held[1 - y, 1 - x] = self.joined(0, 1 - y, 1 - x).astype(BF16)
@@ -210,8 +210,8 @@
         self.out[...] = self.joined(3, y, x)
 
     def end(self):
-        y, c, z, x = self.place
-        pair, xn, yn = near(self.place)
+        y, _, _, x = self.place
+        _, xn, yn = near(self.place)
         send, arrive, base, held = self.mail.send, self.mail.arrive, self.base, self.held
         top, bot, last, out = self.top, self.bot, self.last, self.out
         arrive(base + 4, self.via_x.at[1 - y], xn)
@@ -230,23 +230,6 @@
         out[bot] = out[bot] + last[3].astype(F32)
 
 
-class LineGather:
-    def __init__(self, mail, place, src, out):
-        self.mail, self.place, self.src, self.out = mail, place, src, out
-        self.line = line_peers(place)
-        self.base = mail.take(len(self.line))
-
-    def begin(self):
-        z = self.place[2]
-        for slot, (dev, _, _) in enumerate(self.line):
-            self.mail.send(self.base + slot, self.src, self.out.at[z], dev)
-        self.out[z] = self.src[...]
-
-    def end(self):
-        for slot, (dev, _, back) in enumerate(self.line):
-            self.mail.arrive(self.base + slot, self.out.at[back], dev)
-
-
 class LineScatter:
     def __init__(self, mail, place, parts, got):
         self.mail, self.place, self.parts, self.got = mail, place, parts, got
@@ -273,7 +256,7 @@
         self.base = mail.take(self.COPIES)
 
     def begin(self):
-        y, c, z, x = self.place
+        y, c, _, x = self.place
         me = rank(y, c, x)
         for slot, (dev, other, _) in enumerate(plane_peers(self.place)):
             self.mail.send(self.base + slot, self.src.at[other], self.out.at[me], dev)
@@ -368,7 +351,7 @@
                 yield j, ox, own, copy
 
     def begin(self):
-        y, c, z, x = self.place
+        _, _, z, _ = self.place
         for j, ox, own, copy in self.copies():
 
             @pl.when(own)
@@ -400,11 +383,14 @@
         self.out[...] = total
 
 
-def call(body, name, ident, outs, args, copies, scratch=()):
+def call(body, ident, outs, args, copies, scratch=()):
     spec = pl.BlockSpec(memory_space=pltpu.VMEM)
+    return remote_call(body, ident, outs, args, copies, scratch, spec)
+
+
+def remote_call(body, ident, outs, args, copies, scratch, spec):
     return pl.pallas_call(
         body,
-        name=name,
         out_shape=tuple(jax.ShapeDtypeStruct(shape, dtype) for shape, dtype in outs),
         in_specs=[spec] * len(args),
         out_specs=tuple([spec] * len(outs)),
@@ -475,83 +461,116 @@
     return inverse * shaped - raw * (inverse * inverse * inverse * mean), dgain
 
 
+def all_peers(place):
+    y, c, z, x = place
+    outer = lax.axis_size("blk") // INNER
+    peers = []
+    for k in range(outer):
+        forth, back = lax.rem(z + k, outer), lax.rem(z + outer - k, outer)
+        for bits in range(0 if k else 1, 8):
+            py = 1 - y if bits & 4 else y
+            pc = 1 - c if bits & 2 else c
+            px = 1 - x if bits & 1 else x
+            peers.append((device(py, pc, forth, px), device(py, pc, back, px), py, pc, back, px))
+    return peers
+
+
 def start_kernel(
-    x_ref, q_ref, k_ref, v_ref, g1_ref, g2_ref, gu_ref, wo_ref,
-    xp_ref, wq_ref, gain_ref, gus_ref, wos_ref,
+    x_ref, q_ref, k_ref, v_ref, g1_ref, g2_ref, gate_ref, up_ref, wo_ref,
+    xp_ref, wq_ref, gain_ref, gu_ref, wos_ref,
     ss, rs, w_ref, g_ref, gs_ref,
 ):
     place = y, c, z, x = here()
     me = rank(y, c, x)
     head = y * CORES + c
     mail = Mail((ss, rs))
-    peers, line = plane_peers(place), line_peers(place)
-    plane, w_rows, cols = w_ref.shape
+    peers = all_peers(place)
+    plane, w_rows, _ = w_ref.shape
+    heads, outer = wq_ref.shape[:2]
     q_cols = q_ref.shape[1] // plane
     k_cols = k_ref.shape[1] // plane
     g_ref[...] = jnp.zeros_like(g_ref)
-    g_ref[0:1, :w_rows] = g1_ref[...]
-    g_ref[1:2, :w_rows] = g2_ref[...]
+    g_ref[0:1, :w_rows] = g1_ref[...].astype(F32)
+    g_ref[0:1, LANES // 2 : LANES // 2 + w_rows] = g2_ref[...].astype(F32)
     keys, values = k_ref[...].astype(F32), v_ref[...].astype(F32)
     for p in range(plane):
         at = slice(p * k_cols, (p + 1) * k_cols)
         pair = jnp.concatenate([keys[:, at], values[:, at]], axis=1)
         w_ref[p, :, :q_cols] = q_ref[:, p * q_cols : (p + 1) * q_cols]
         w_ref[p, :, q_cols:] = pair.astype(BF16)
-    greet([p[0] for p in peers] + blk_peers(place))
-    w_base, g_base = mail.take(7), mail.take(7)
-    zw_base, zg_base = mail.take(len(line)), mail.take(len(line))
-    for slot, (dev, other, _) in enumerate(peers):
+    greet([p[0] for p in peers])
+    w_base, g_base = mail.take(len(peers)), mail.take(len(peers))
+    rows = PlaneGather(mail, place, x_ref, xp_ref)
+    block = RowsOut(mail, place, wo_ref, wos_ref)
+    for slot, (dev, _, py, pc, _, px) in reversed(list(enumerate(peers))):
         mail.send(g_base + slot, g_ref, gs_ref.at[z, me], dev)
-        mail.send(w_base + slot, w_ref.at[other], wq_ref.at[head, z, x], dev)
+        mail.send(w_base + slot, w_ref.at[rank(py, pc, px)], wq_ref.at[head, z, x], dev)
+    rows.begin()
     gs_ref[z, me] = g_ref[...]
     wq_ref[head, z, x] = w_ref[me]
-    rows = PlaneGather(mail, place, x_ref, xp_ref)
-    swap = PlaneSwap(mail, place, gu_ref, gus_ref)
-    block = RowsOut(mail, place, wo_ref, wos_ref)
-    rows.begin()
-    for slot, (dev, other, (oh, ox)) in enumerate(peers):
-        mail.arrive(g_base + slot, gs_ref.at[z, other], dev)
-        mail.arrive(w_base + slot, wq_ref.at[oh, z, ox], dev)
-    for slot, (dev, _, _) in enumerate(line):
-        mail.send(zg_base + slot, gs_ref.at[z], gs_ref.at[z], dev)
-        mail.send(zw_base + slot, wq_ref.at[:, z], wq_ref.at[:, z], dev)
     block.begin()
+    f_cols = gate_ref.shape[1] // (heads * outer * INNER)
+    main = outer * f_cols // LANES * LANES
+    for oh in range(heads):
+        span = outer * INNER * f_cols
+        cut = []
+        for ref in (gate_ref, up_ref):
+            wide = ref[:, oh * span : (oh + 1) * span].astype(F32)
+            cut.append(
+                [
+                    jnp.concatenate(
+                        [
+                            wide[:, (oz * INNER + ox) * f_cols : (oz * INNER + ox + 1) * f_cols]
+                            for oz in range(outer)
+                        ],
+                        axis=1,
+                    )
+                    for ox in range(INNER)
+                ]
+            )
+        for ox in range(INNER):
+            gate, up = cut[0][ox], cut[1][ox]
+            p = oh * INNER + ox
+            gu_ref[p, :, :main] = gate[:, :main].astype(BF16)
+            gu_ref[p, :, main : 2 * main] = up[:, :main].astype(BF16)
+            tails = jnp.concatenate([gate[:, main:], up[:, main:]], axis=1)
+            gu_ref[p, :, 2 * main :] = tails.astype(BF16)
     rows.middle()
-    swap.begin()
     rows.end()
-    for slot, (dev, _, back) in enumerate(line):
-        mail.arrive(zg_base + slot, gs_ref.at[back], dev)
-        mail.arrive(zw_base + slot, wq_ref.at[:, back], dev)
-    heads, outer = wq_ref.shape[:2]
+    for slot, (_, dev, py, pc, oz, px) in enumerate(peers):
+        mail.arrive(g_base + slot, gs_ref.at[oz, rank(py, pc, px)], dev)
     gain_ref[...] = jnp.zeros_like(gain_ref)
     for row in range(2):
+        first = row * LANES // 2
         gain_ref[row : row + 1] = jnp.concatenate(
             [
-                gs_ref[oz, oh * INNER + ox].astype(F32)[row : row + 1, :w_rows]
+                gs_ref[oz, oh * INNER + ox][:, first : first + w_rows]
                 for oh in range(heads)
                 for oz in range(outer)
                 for ox in range(INNER)
             ],
             axis=1,
         )
+    for slot, (_, dev, py, pc, oz, px) in enumerate(peers):
+        mail.arrive(w_base + slot, wq_ref.at[py * CORES + pc, oz, px], dev)
     block.end()
-    swap.end()
     mail.close()
 
 
 def line_kernel(
-    x_ref, w_ref, gain_ref, qk_ref, cos_ref, sin_ref, og_ref,
-    q_ref, kvs_ref, raw_ref, norm_ref, ogs_ref,
+    x_ref, w_ref, gain_ref, qk_ref, cos_ref, sin_ref, og_ref, gu_ref,
+    q_ref, kvs_ref, raw_ref, norm_ref, ogs_ref, gus_ref,
     ss, rs, kv_ref,
 ):
     place = y, c, z, x = here()
     mail = Mail((ss, rs))
     line = line_peers(place)
-    greet([p[0] for p in line] + list(near(place)))
+    greet([p[0] for p in line] + [p[0] for p in plane_peers(place)])
     rows = PlaneGather(mail, place, og_ref, ogs_ref)
+    swap = PlaneSwap(mail, place, gu_ref, gus_ref)
     base = mail.take(2 * len(line))
     rows.begin()
-    count, tok, _ = x_ref.shape
+    count, _, _ = x_ref.shape
     q_cols = q_ref.shape[2]
     size = q_cols // 2
     gain_one = gain_ref[0:1]
@@ -578,7 +597,9 @@
             mail.send(base + 2 * slot + part, kv_ref.at[at], kvs_ref.at[z, at], dev)
     kvs_ref[z] = kv_ref[...]
     rows.middle()
+    swap.begin()
     rows.end()
+    swap.end()
     for part in range(2):
         at = pl.ds(part * half, half)
         for slot, (dev, _, back) in enumerate(line):
@@ -587,14 +608,13 @@
 
 
 def mix_kernel(
-    att_ref, wo_ref, x_ref, gain_ref, wd_ref,
-    mid_ref, n2_ref, wds_ref,
+    att_ref, wo_ref, x_ref, gain_ref,
+    mid_ref, n2_ref,
     ss, rs, parts, own, *bufs,
 ):
     place = here()
     mail = Mail((ss, rs))
-    greet([p[0] for p in line_peers(place)] + list(near(place)))
-    down = LineGather(mail, place, wd_ref, wds_ref)
+    greet(list(near(place)))
 
     def make(block):
         parts[block] = jnp.dot(
@@ -604,7 +624,6 @@
     summed = PlaneScatter(mail, place, parts, mid_ref, bufs, make)
     rows = PlaneGather(mail, place, own, n2_ref)
     summed.begin()
-    down.begin()
     summed.middle()
     summed.end()
     middle = x_ref[...].astype(F32) + mid_ref[...]
@@ -613,7 +632,6 @@
     rows.begin()
     rows.middle()
     rows.end()
-    down.end()
     mail.close()
 
 
@@ -812,12 +830,24 @@
             )
 
 
-def feed_kernel(z_ref, n2_ref, og_ref, wd_ref, *refs):
+def down_rows(ref, oz, f_rows, piece):
+    pack = math.gcd(f_rows, 16)
+    if pack == 16:
+        ref[pl.ds(pl.multiple_of(oz * f_rows, pack), f_rows)] = piece[...]
+        return
+    for at in range(ref.shape[0] // f_rows):
+
+        @pl.when(oz == at)
+        def _():
+            ref[at * f_rows : (at + 1) * f_rows] = piece[...]
+
+
+def feed_kernel(z_ref, n2_ref, og_ref, *refs):
     outer = lax.axis_size("blk") // INNER
-    pieces, refs = refs[:outer], refs[outer:]
+    pieces, downs, refs = refs[:outer], refs[outer : 2 * outer], refs[2 * outer :]
     out_ref, dn_ref, dg_ref = refs[:3]
     chunks = refs[3 : 3 + outer]
-    wgu, hid, dgu, gg = refs[3 + outer :]
+    wgu, wd_ref, hid, dgu, gg = refs[3 + outer :]
     z = z_ref[0]
     heads, stride, _ = pieces[0].shape
     ff = wd_ref.shape[0]
@@ -828,6 +858,9 @@
         for oh in range(heads):
             at = pl.multiple_of((oh * outer + oz) * stride, stride)
             wgu[pl.ds(at, stride)] = piece[oh]
+    f_rows = ff // outer
+    for k, piece in enumerate(downs):
+        down_rows(wd_ref, lax.rem(z + outer - k, outer), f_rows, piece)
     plane, rows, width = n2_ref.shape
 
     def both(gate, up, dhid):
@@ -882,7 +915,6 @@
     for k, chunk in enumerate(chunks):
         chunk[...] = gg[lax.rem(z + k, outer)]
     grads = og_ref[...].reshape(plane * rows, width)
-    f_rows = ff // outer
     down = lax.dot_general(hid[...], grads, TN, preferred_element_type=F32)
     for oz in range(outer):
         dg_ref[oz] = down[oz * f_rows : (oz + 1) * f_rows].astype(BF16)
@@ -1021,12 +1053,11 @@
     lax.fori_loop(0, spans, give_rows, 0)
 
 
-def local_call(body, name, scalars, args, outs, scratch, flops):
+def local_call(body, scalars, args, outs, scratch, flops):
     vmem = pl.BlockSpec(memory_space=pltpu.VMEM)
     smem = pl.BlockSpec(memory_space=pltpu.SMEM)
     return pl.pallas_call(
         body,
-        name=name,
         out_shape=tuple(jax.ShapeDtypeStruct(shape, dtype) for shape, dtype in outs),
         in_specs=[smem] * len(scalars) + [vmem] * len(args),
         out_specs=tuple([vmem] * len(outs)),
@@ -1075,19 +1106,15 @@
     n_line = outer - 1
     stride = INNER * w_rows
 
-    def cut(weight):
-        shaped = weight.reshape(w_rows, heads, outer, INNER, f_rows)
-        return shaped.transpose(1, 3, 0, 2, 4).reshape(plane, w_rows, ff)
-
-    main = ff // LANES * LANES
-    gate8, up8 = cut(w_gate), cut(w_up)
-    gu8 = jnp.concatenate(
-        [gate8[..., :main], up8[..., :main], gate8[..., main:], up8[..., main:]], axis=-1
-    )
-
-    x_all, wqkv, gains, gu_piece, out_mine = call(
+    def along(piece):
+        moved = [
+            lax.ppermute(piece, "blk", shifts(outer, step)) for step in range(1, outer)
+        ]
+        return [piece] + moved
+
+    down_pieces = along(w_down)
+    x_all, wqkv, gains, gu8, out_mine = call(
         start_kernel,
-        "start",
         1,
         [
             ((plane, rows, width), BF16),
@@ -1103,22 +1130,19 @@
             value_weight,
             norm1_gain.reshape(1, w_rows),
             norm2_gain.reshape(1, w_rows),
-            gu8,
+            w_gate,
+            w_up,
             w_out,
         ),
-        14 + 2 * n_line + PlaneGather.COPIES + PlaneSwap.COPIES + outer,
+        2 * (outer * plane - 1) + PlaneGather.COPIES + outer,
         [
             pltpu.VMEM((plane, w_rows, a_cols), BF16),
-            pltpu.VMEM((16, LANES), BF16),
-            pltpu.VMEM((outer, plane, 16, LANES), BF16),
+            pltpu.VMEM((1, LANES), F32),
+            pltpu.VMEM((outer, plane, 1, LANES), F32),
         ],
     )
     wqkv = wqkv.reshape(width, a_cols)
     out_mine = out_mine.reshape(q_cols, width)
-    gu_piece = gu_piece.reshape(heads, stride, 2 * ff)
-    gu_pieces = [gu_piece] + [
-        lax.ppermute(gu_piece, "blk", shifts(outer, step)) for step in range(1, outer)
-    ]
 
     by_place = span_order.reshape(heads, outer, INNER)
     own_spans = lax.dynamic_index_in_dim(by_place, z, 1, keepdims=False).reshape(plane)
@@ -1138,9 +1162,8 @@
         ]
     )
 
-    queries, kv_all, raw, normed, og_all = call(
+    queries, kv_all, raw, normed, og_all, gu_piece = call(
         line_kernel,
-        "line",
         2,
         [
             ((plane, rows, q_cols), BF16),
@@ -1148,39 +1171,37 @@
             ((plane, rows, a_cols), F32),
             ((plane, rows, width), BF16),
             ((plane, rows, width), BF16),
+            ((plane, w_rows, 2 * ff), BF16),
         ],
-        (x_all, wqkv, gains, qk_rows, cosine, sine, out_grad),
-        2 * n_line + PlaneGather.COPIES,
+        (x_all, wqkv, gains, qk_rows, cosine, sine, out_grad, gu8),
+        2 * n_line + PlaneGather.COPIES + PlaneSwap.COPIES,
         [pltpu.VMEM((plane, rows, q_cols), BF16)],
     )
+    gu_pieces = along(gu_piece.reshape(heads, stride, 2 * ff))
     kv_blocks = kv_all.reshape(spans, rows, q_cols)
     pairs = plane * rows * spans * rows * q_cols
     attended, log_total = local_call(
         forward_kernel,
-        "attend",
         (own_spans, span_at),
         (queries, kv_blocks),
         [((plane, rows, q_cols), BF16), ((plane, 8, 2 * rows), F32)],
         [pltpu.VMEM((spans * rows, q_cols), BF16), pltpu.VMEM((spans * rows, q_cols), BF16)],
         4 * pairs,
     )
-    middle, normed2, down_full = call(
+    middle, normed2 = call(
         mix_kernel,
-        "mix",
         3,
-        [((rows, width), F32), ((plane, rows, width), BF16), ((outer, f_rows, width), BF16)],
-        (attended, out_mine, block_input, gains, w_down),
-        n_line + PlaneScatter.COPIES + PlaneGather.COPIES,
+        [((rows, width), F32), ((plane, rows, width), BF16)],
+        (attended, out_mine, block_input, gains),
+        PlaneScatter.COPIES + PlaneGather.COPIES,
         [pltpu.VMEM((plane, rows, width), BF16), pltpu.VMEM((rows, width), BF16)]
         + PlaneScatter.scratch(rows, width),
     )
-    down_full = down_full.reshape(ff, width)
 
     out_parts, dn_parts, down_grad, *gu_grads = local_call(
         feed_kernel,
-        "feed",
         (jnp.reshape(z, (1,)).astype(jnp.int32),),
-        (normed2, og_all, down_full, *gu_pieces),
+        (normed2, og_all, *gu_pieces, *down_pieces),
         [
             ((plane, rows, width), BF16),
             ((plane, rows, width), BF16),
@@ -1189,6 +1210,7 @@
         + [((plane, w_rows, 2 * ff), BF16)] * outer,
         [
             pltpu.VMEM((width, 2 * ff), BF16),
+            pltpu.VMEM((ff, width), BF16),
             pltpu.VMEM((plane * rows, ff), BF16),
             pltpu.VMEM((plane * rows, 2 * ff), BF16),
             pltpu.VMEM((outer, plane, w_rows, 2 * ff), BF16),
@@ -1200,7 +1222,6 @@
     ]
     dmiddle, dmid_all, norm2_grad = call(
         narrow_kernel,
-        "narrow",
         4,
         [((rows, width), F32), ((plane, rows, width), BF16), ((1, width), F32)],
         (dn_parts, middle, out_grad, gains),
@@ -1215,7 +1236,6 @@
     dattended = lax.dot_general(dmid_rows, out_mine, NT, preferred_element_type=F32).astype(BF16)
     dqueries, dkv = local_call(
         backward_kernel,
-        "attend_back",
         (own_spans, span_at),
         (queries, kv_blocks, attended, dattended.reshape(plane, rows, q_cols), log_total),
         [((plane, rows, q_cols), BF16), ((spans, rows, q_cols), BF16)],
@@ -1228,7 +1248,6 @@
     )
     dkv_own, block_output, out_proj_grad = call(
         back_kernel,
-        "back",
         5,
         [((plane, rows, q_cols), BF16), ((rows, width), BF16), ((w_rows, width), F32)],
         (
@@ -1247,7 +1266,6 @@
     )
     input_grad, w_own, gu_own, down_out, small = call(
         last_kernel,
-        "last",
         6,
         [
             ((rows, width), BF16),
@@ -1291,7 +1309,6 @@
     own = (lax.axis_index("head") * blocks + lax.axis_index("blk")) * w_rows
     outs = local_call(
         finish_kernel,
-        "finish",
         (jnp.reshape(own, (1,)).astype(jnp.int32),),
         (w_own, gu_own, small, block_output, input_grad, out_proj_grad, down_out),
         [

time: 371 us -> 338 us (0.911)
  Pallas kernels: 339 us -> 296 us
  starting transfers between devices: 15.3 us -> 23.3 us
  waiting for transfers between devices: 0.02 us -> 6.47 us
    pallas_call x10, Pallas kernels: 339 us -> 296 us  [the longest x6 228 us: remote_call(): pl.pallas_call(body, out_shape=tuple((jax.ShapeDtypeStruct(shape, dtype)...]
    ppermute x3 -> x6, waiting for transfers between devices: 0.01 us -> 6.46 us  [along(): lax.ppermute(piece, 'blk', shifts(outer, step))]
    ppermute x3, starting transfers between devices: 6.08 us -> 10.3 us  [local(): lax.ppermute(gu_grads[step], 'blk', shifts(outer, step))]
    ppermute x3 -> x6, starting transfers between devices: 9.25 us -> 13.1 us  [along(): lax.ppermute(piece, 'blk', shifts(outer, step))]
    reshape x6 -> x0, local copies, waits for them, and re-layouts: 3.78 us -> none  [the longest x4 3.13 us: cut(): shaped = weight.reshape(w_rows, heads, outer, INNER, f_rows)]
  transfers between devices with their start and end apart: 6 -> 9, of which waited for: 0 -> 1; matrix products, arithmetic and copies ran while one was open for 1% -> 2% of each run, Pallas kernels for 55% -> 55%
where the time goes in v4:
time: 338 us
  Pallas kernels  296 us (88%)
  starting transfers between devices  23.3 us (7%)
  waiting for transfers between devices  6.47 us (2%)
  matrix products  4.33 us (1%)
  local copies, waits for them, and re-layouts  3.9 us (1%)
    pallas_call x6, Pallas kernels, remote_call(): pl.pallas_call(body, out_shape=tuple((jax.ShapeDtypeStruct(shape, dtype)...  228 us
    pallas_call x4, Pallas kernels, local_call(): pl.pallas_call(body, out_shape=tuple((jax.ShapeDtypeStruct(shape, dtype)...  67.8 us
    ppermute x6, starting transfers between devices, along(): lax.ppermute(piece, 'blk', shifts(outer, step))  13.1 us
    ppermute x3, starting transfers between devices, local(): lax.ppermute(gu_grads[step], 'blk', shifts(outer, step))  10.3 us
  transfers between devices with their start and end apart: 9, of which 1 were waited for; matrix products, arithmetic and copies ran while one was open for 2% of the time, Pallas kernels for 55%

profile of v4, /device:TPU:0, one launch (start us, length us, event | category | flops | bytes accessed | tf_op | source)
XLA Modules:
  0.0 337.6 jit_solution(14037439382125627838)
XLA Ops:
  0.6 4.1 %collective-permute-start.4 = (bf16[144,1024]{1,0:T(8,128)(2,1)}, bf16[144,1024]{1,0:T(8,128)(2,1)S(1)}, u32[]{:S(2)}, u32[]{:S(2)}) collective-permute-start(bf16[144,1024]{1,0:T(8,128)(2,1)} %refs_4_.1), channel_id=1, source_target_pairs={{0,4},{1,5},{2,6},{3,7},{4,0},{5,1},{6,2},{7,3},{8,12},{9,13},{10,... | collective-permute-start | bytes 884744 | tf_op jit(solution)/shard_map/ppermute | solution.py:1111
  4.8 0.8 slice_bitcast_fusion.1
  5.5 0.7 reshape.107
  6.3 0.1 reshape.108.own_ref
  6.4 0.1 add_convert_fusion
  6.5 0.1 maximum_bitcast_fusion
  6.6 1.2 multiply_sine_fusion
  7.8 0.6 pad_maximum_fusion.qk_ref
  8.4 29.4 %shard_map.220 = (bf16[8,128,1024]{2,1,0:T(8,128)(2,1)}, bf16[4,4,2,32,256]{4,3,2,1,0:T(8,128)(2,1)}, f32[8,1024]{1,0:T(8,128)}, bf16[8,32,1152]{2,1,0:T(8,128)(2,1)}, bf16[2,2,32,1024]{3,2,1,0:T(8,128)(2,1)}) custom-call(bf16[128,1024]{1,0:T(8,128)(2,1)} %x_ref.5, bf16[32,1024]{1,0:T(8,128)(2,1)} %q_ref.1, bf16[32,512]{1,0:T(8,128)(2,1)} %k_ref.1, ...), custom_call_target="tpu_custom_call" | custom-call | tf_op jit(solution)/shard_map/pallas_call | solution.py:392
  37.8 0.0 copy-start.13
  37.8 34.9 %shard_map.221 = (bf16[8,128,128]{2,1,0:T(8,128)(2,1)}, bf16[4,8,128,128]{3,2,1,0:T(8,128)(2,1)}, f32[8,128,256]{2,1,0:T(8,128)}, bf16[8,128,1024]{2,1,0:T(8,128...) custom-call(bf16[8,128,1024]{2,1,0:T(8,128)(2,1)} %get-tuple-element.59.x_ref, ...), custom_call_target="tpu_custom_call" | custom-call | tf_op jit(solution)/shard_map/pallas_call | solution.py:392
  72.8 4.2 %collective-permute-start.2 = (bf16[4,64,1152]{2,1,0:T(8,128)(2,1)}, bf16[4,64,1152]{2,1,0:T(8,128)(2,1)S(1)}, u32[]{:S(2)}, u32[]{:S(2)}) collective-permute-start(bf16[4,64,1152]{2,1,0:T(8,128)(2,1)} %bitcast.44), channel_id=1, source_target_pairs={{0,6},{1,7},{2,0},{3,1},{4,2},{5,3},{6,4},{7,5},{8,14},{9,15},{10,... | collective-permute-start | bytes 1769480 | tf_op jit(solution)/shard_map/ppermute | solution.py:1111
  77.0 0.0 collective-permute-start.1
  77.0 0.6 collective-permute-start
  77.7 2.8 collective-permute-start.3
  80.5 0.1 eq.15
  80.6 0.0 collective-permute-done.4.refs_6_
  80.6 1.2 collective-permute-start.5
  81.9 0.6 select_reduce_fusion.at_ref
  82.5 18.0 %shard_map.222 = (bf16[8,128,128]{2,1,0:T(8,128)(2,1)}, f32[8,8,256]{2,1,0:T(8,128)}) custom-call(s32[8]{0:T(128)} %copy-done.6, s32[32]{0:T(128)} %select_reduce_fusion.at_ref, bf16[8,128,128]{2,1,0:T(8,128)(2,1)} %get-tuple-element.63.q_ref, bf16[32,128,128]{2,1,0:T(8,128)(2,1)} %bitcast.42), custom_call_target="tpu_custom_call" | custom-call | flops 2147483648 | bytes 8388608 | tf_op jit(solution)/shard_map/pallas_call | solution.py:1059
  100.4 28.4 %shard_map.223 = (f32[128,1024]{1,0:T(8,128)}, bf16[8,128,1024]{2,1,0:T(8,128)(2,1)}) custom-call(bf16[8,128,128]{2,1,0:T(8,128)(2,1)} %get-tuple-element.65.att_ref.out_ref, bf16[128,1024]{1,0:T(8,128)(2,1)} %bitcast.34, bf16[128,1024]{1,0:T(8,128)(2,1)} %x_ref.5, f32[8,1024]{1,0:T(8,128)} %get-tuple-element.61.gain_ref), custom_call_target="tpu_custom_call" | custom-call | tf_op jit(solution)/shard_map/pallas_call | solution.py:392
  128.8 0.0 collective-permute-done.3.refs_5_
  128.9 0.0 collective-permute-done.5.refs_7_
  128.9 0.0 collective-permute-done.2.refs_3_
  128.9 0.0 copy-start.7
  128.9 6.4 %collective-permute-done.1.refs_2_ = bf16[4,64,1152]{2,1,0:T(8,128)(2,1)S(1)} collective-permute-done((bf16[4,64,1152]{2,1,0:T(8,128)(2,1)}, bf16[4,64,1152]{2,1,0:T(8,128)(2,1)S(1)}, u32[]{:S(2)}, u32[]{:S(2)}) %collective-permute-start.1) | collective-permute-done | bytes 589856 | tf_op jit(solution)/shard_map/ppermute | solution.py:1111
  135.4 0.0 collective-permute-done.refs_1_
  135.4 0.8 copy-done.8
  136.2 0.2 copy-done.9
  136.4 19.6 %shard_map.224 = (bf16[8,128,1024]{2,1,0:T(8,128)(2,1)}, bf16[8,128,1024]{2,1,0:T(8,128)(2,1)}, bf16[4,144,1024]{2,1,0:T(8,128)(2,1)}, bf16[8,32,1152]{2,1,0:T(8...) custom-call(s32[1]{0:T(128)} %bitcast.10.z_ref, ...), custom_call_target="tpu_custom_call" | custom-call | flops 10871635968 | bytes 8388608 | tf_op jit(solution)/shard_map/pallas_call | solution.py:1059
  156.0 28.3 %shard_map.225 = (f32[128,1024]{1,0:T(8,128)}, bf16[8,128,1024]{2,1,0:T(8,128)(2,1)}, f32[1,1024]{1,0:T(1,128)}) custom-call(bf16[8,128,1024]{2,1,0:T(8,128)(2,1)} %get-tuple-element.70.parts_ref, f32[128,1024]{1,0:T(8,128)} %get-tuple-element.71.mid_ref, bf16[128,1024]{1,0:T(8,128)(2,1)} %og_ref.3, f32[8,1024]{1,0:T(8,128)} %get-tuple-element.61.gain_ref), custom_call_target="tpu_custom_call" | custom-call | tf_op jit(solution)/shard_map/pallas_call | solution.py:392
  184.3 2.9 fusion
  187.2 5.9 %collective-permute-start.6 = (bf16[8,32,1152]{2,1,0:T(8,128)(2,1)S(1)}, bf16[8,32,1152]{2,1,0:T(8,128)(2,1)S(1)}, u32[]{:S(2)}, u32[]{:S(2)}) collective-permute-start(bf16[8,32,1152]{2,1,0:T(8,128)(2,1)S(1)} %copy-done.12), channel_id=1, source_target_pairs={{0,2},{1,3},{2,4},{3,5},{4,6},{5,7},{6,0},{7,1},{8,10},{9,11},{10,... | collective-permute-start | bytes 1769480 | tf_op jit(solution)/shard_map/ppermute | solution.py:1221
  193.1 1.5 collective-permute-start.7
  194.6 2.9 collective-permute-start.8
  197.5 1.4 convolution_convert_fusion
  198.9 26.9 %shard_map.226 = (bf16[8,128,128]{2,1,0:T(8,128)(2,1)}, bf16[32,128,128]{2,1,0:T(8,128)(2,1)}) custom-call(s32[8]{0:T(128)} %copy-done.6, s32[32]{0:T(128)} %select_reduce_fusion.at_ref, bf16[8,128,128]{2,1,0:T(8,128)(2,1)} %get-tuple-element.63.q_ref, bf16[32,128,128]{2,1,0:T(8,128)(2,1)} %bitcast.43, ...), custom_call_target="tpu_custom_call" | custom-call | flops 5368709120 | bytes 8388608 | tf_op jit(solution)/shard_map/pallas_call | solution.py:1059
  225.8 47.6 %shard_map.227 = (bf16[8,128,128]{2,1,0:T(8,128)(2,1)}, bf16[128,1024]{1,0:T(8,128)(2,1)}, f32[32,1024]{1,0:T(8,128)}) custom-call(bf16[4,8,128,128]{3,2,1,0:T(8,128)(2,1)} %bitcast.36, bf16[8,128,1024]{2,1,0:T(8,128)(2,1)} %get-tuple-element.76.parts_ref, bf16[2,2,32,1024]{3,2,1,0:T(8,128)(2,1)} %bitcast.37, f32[128,1024]{1,0:T(8,128)} %get-tuple-element.71.mid_ref), custom_call_target="tpu_custom_call" | custom-call | tf_op jit(solution)/shard_map/pallas_call | solution.py:392
  273.4 0.0 collective-permute-done.6.refs_1_
  273.4 0.0 copy-start.3
  273.4 0.0 copy-start.4
  273.4 0.0 collective-permute-done.8.refs_3_
  273.4 0.0 copy-start.5
  273.4 0.8 copy-done.3
  274.2 0.2 copy-done.4
  274.4 0.2 copy-done.5
  274.6 59.6 %shard_map.228 = (bf16[128,1024]{1,0:T(8,128)(2,1)}, f32[8,32,256]{2,1,0:T(8,128)}, bf16[8,32,1152]{2,1,0:T(8,128)(2,1)}, f32[144,1024]{1,0:T(8,128)}, f32[8,1024]{1,0:T(8,128)}) custom-call(bf16[8,128,128]{2,1,0:T(8,128)(2,1)} %get-tuple-element.74.dq_ref, bf16[8,128,128]{2,1,0:T(8,128)(2,1)} %get-tuple-element.77.dkv_ref, ...), custom_call_target="tpu_custom_call" | custom-call | tf_op jit(solution)/shard_map/pallas_call | solution.py:392
  334.2 3.4 %shard_map.229 = (bf16[128,1024]{1,0:T(8,128)(2,1)}, bf16[128,1024]{1,0:T(8,128)(2,1)}, f32[32,1024]{1,0:T(8,128)}, f32[144,1024]{1,0:T(8,128)}, f32[1,32]{1,0:T...) custom-call(s32[1]{0:T(128)} %bitcast.own_ref, ...), custom_call_target="tpu_custom_call" | custom-call | flops 1048576 | bytes 8388608 | tf_op jit(solution)/shard_map/pallas_call | solution.py:1059
  (29 shorter events, 0.1 us)
Async XLA Ops:
  0.6 80.0 %collective-permute-start.4 = (bf16[144,1024]{1,0:T(8,128)(2,1)}, bf16[144,1024]{1,0:T(8,128)(2,1)S(1)}, u32[]{:S(2)}, u32[]{:S(2)}) collective-permute-start(bf16[144,1024]{1,0:T(8,128)(2,1)} %refs_4_.1), channel_id=1, source_target_pairs={{0,4},{1,5},{2,6},{3,7},{4,0},{5,1},{6,2},{7,3},{8,12},{9,13},{10,... | collective-permute-start | bytes 884744 | tf_op jit(solution)/shard_map/ppermute | solution.py:1111
  6.4 66.4 %copy-start.6 = (s32[8]{0:T(128)}, s32[8]{0:T(128)S(1)}, u32[]{:S(2)}) copy-start(s32[8]{0:T(128)S(1)} %reshape.108.own_ref) | copy-start | bytes 100
  37.8 39.8 %copy-start.13 = (bf16[144,1024]{1,0:T(8,128)(2,1)S(1)}, bf16[144,1024]{1,0:T(8,128)(2,1)}, u32[]{:S(2)}) copy-start(bf16[144,1024]{1,0:T(8,128)(2,1)} %refs_4_.1) | copy-start | bytes 884740
  72.8 56.1 %collective-permute-start.2 = (bf16[4,64,1152]{2,1,0:T(8,128)(2,1)}, bf16[4,64,1152]{2,1,0:T(8,128)(2,1)S(1)}, u32[]{:S(2)}, u32[]{:S(2)}) collective-permute-start(bf16[4,64,1152]{2,1,0:T(8,128)(2,1)} %bitcast.44), channel_id=1, source_target_pairs={{0,6},{1,7},{2,0},{3,1},{4,2},{5,3},{6,4},{7,5},{8,14},{9,15},{10,... | collective-permute-start | bytes 1769480 | tf_op jit(solution)/shard_map/ppermute | solution.py:1111
  77.0 58.3 %collective-permute-start.1 = (bf16[4,64,1152]{2,1,0:T(8,128)(2,1)}, bf16[4,64,1152]{2,1,0:T(8,128)(2,1)S(1)}, u32[]{:S(2)}, u32[]{:S(2)}) collective-permute-start(bf16[4,64,1152]{2,1,0:T(8,128)(2,1)} %bitcast.45), channel_id=1, source_target_pairs={{0,4},{1,5},{2,6},{3,7},{4,0},{5,1},{6,2},{7,3},{8,12},{9,13},{10,... | collective-permute-start | bytes 1769480 | tf_op jit(solution)/shard_map/ppermute | solution.py:1111
  77.0 58.3 %collective-permute-start = (bf16[4,64,1152]{2,1,0:T(8,128)(2,1)}, bf16[4,64,1152]{2,1,0:T(8,128)(2,1)S(1)}, u32[]{:S(2)}, u32[]{:S(2)}) collective-permute-start(bf16[4,64,1152]{2,1,0:T(8,128)(2,1)} %bitcast.46), channel_id=1, source_target_pairs={{0,2},{1,3},{2,4},{3,5},{4,6},{5,7},{6,0},{7,1},{8,10},{9,11},{10,... | collective-permute-start | bytes 1769480 | tf_op jit(solution)/shard_map/ppermute | solution.py:1111
  77.7 51.2 %collective-permute-start.3 = (bf16[144,1024]{1,0:T(8,128)(2,1)S(1)}, bf16[144,1024]{1,0:T(8,128)(2,1)S(1)}, u32[]{:S(2)}, u32[]{:S(2)}) collective-permute-start(bf16[144,1024]{1,0:T(8,128)(2,1)S(1)} %copy-done.13), channel_id=1, source_target_pairs={{0,2},{1,3},{2,4},{3,5},{4,6},{5,7},{6,0},{7,1},{8,10},{9,11},{10,... | collective-permute-start | bytes 884744 | tf_op jit(solution)/shard_map/ppermute | solution.py:1111
  80.6 19.8 %copy-start.14 = (bf16[144,1024]{1,0:T(8,128)(2,1)}, bf16[144,1024]{1,0:T(8,128)(2,1)S(1)}, u32[]{:S(2)}) copy-start(bf16[144,1024]{1,0:T(8,128)(2,1)S(1)} %collective-permute-done.4.refs_6_) | copy-start | bytes 884740
  80.6 48.2 %collective-permute-start.5 = (bf16[144,1024]{1,0:T(8,128)(2,1)S(1)}, bf16[144,1024]{1,0:T(8,128)(2,1)S(1)}, u32[]{:S(2)}, u32[]{:S(2)}) collective-permute-start(bf16[144,1024]{1,0:T(8,128)(2,1)S(1)} %copy-done.13), channel_id=1, source_target_pairs={{0,6},{1,7},{2,0},{3,1},{4,2},{5,3},{6,4},{7,5},{8,14},{9,15},{10,... | collective-permute-start | bytes 884744 | tf_op jit(solution)/shard_map/ppermute | solution.py:1111
  128.9 6.5 %copy-start.15 = (bf16[144,1024]{1,0:T(8,128)(2,1)}, bf16[144,1024]{1,0:T(8,128)(2,1)S(1)}, u32[]{:S(2)}) copy-start(bf16[144,1024]{1,0:T(8,128)(2,1)S(1)} %collective-permute-done.3.refs_5_) | copy-start | bytes 884740
  128.9 6.5 %copy-start.16 = (bf16[144,1024]{1,0:T(8,128)(2,1)}, bf16[144,1024]{1,0:T(8,128)(2,1)S(1)}, u32[]{:S(2)}) copy-start(bf16[144,1024]{1,0:T(8,128)(2,1)S(1)} %collective-permute-done.5.refs_7_) | copy-start | bytes 884740
  128.9 6.5 %copy-start.7 = (bf16[4,64,1152]{2,1,0:T(8,128)(2,1)}, bf16[4,64,1152]{2,1,0:T(8,128)(2,1)S(1)}, u32[]{:S(2)}) copy-start(bf16[4,64,1152]{2,1,0:T(8,128)(2,1)S(1)} %collective-permute-done.2.refs_3_) | copy-start | bytes 1769476
  135.4 0.8 copy-start.8
  135.4 1.0 copy-start.9
  155.9 28.3 %copy-start.2 = (bf16[8,128,128]{2,1,0:T(8,128)(2,1)S(1)}, bf16[8,128,128]{2,1,0:T(8,128)(2,1)}, u32[]{:S(2)}) copy-start(bf16[8,128,128]{2,1,0:T(8,128)(2,1)} %get-tuple-element.65.att_ref.out_ref) | copy-start | bytes 786436
  155.9 31.3 %copy-start.12 = (bf16[8,32,1152]{2,1,0:T(8,128)(2,1)S(1)}, bf16[8,32,1152]{2,1,0:T(8,128)(2,1)}, u32[]{:S(2)}) copy-start(bf16[8,32,1152]{2,1,0:T(8,128)(2,1)} %get-tuple-element.84) | copy-start | bytes 1769476
  155.9 37.2 %copy-start.11 = (bf16[8,32,1152]{2,1,0:T(8,128)(2,1)S(1)}, bf16[8,32,1152]{2,1,0:T(8,128)(2,1)}, u32[]{:S(2)}) copy-start(bf16[8,32,1152]{2,1,0:T(8,128)(2,1)} %get-tuple-element.85) | copy-start | bytes 1769476
  156.0 38.7 %copy-start.10 = (bf16[8,32,1152]{2,1,0:T(8,128)(2,1)S(1)}, bf16[8,32,1152]{2,1,0:T(8,128)(2,1)}, u32[]{:S(2)}) copy-start(bf16[8,32,1152]{2,1,0:T(8,128)(2,1)} %get-tuple-element.86) | copy-start | bytes 1769476
  156.0 41.5 %copy-start.1 = (bf16[2,2,32,1024]{3,2,1,0:T(8,128)(2,1)S(1)}, bf16[2,2,32,1024]{3,2,1,0:T(8,128)(2,1)}, u32[]{:S(2)}) copy-start(bf16[2,2,32,1024]{3,2,1,0:T(8,128)(2,1)} %get-tuple-element.66) | copy-start | bytes 786436
  184.3 13.2 %copy-start = (bf16[8,128,1024]{2,1,0:T(8,128)(2,1)S(1)}, bf16[8,128,1024]{2,1,0:T(8,128)(2,1)}, u32[]{:S(2)}) copy-start(bf16[8,128,1024]{2,1,0:T(8,128)(2,1)} %get-tuple-element.72) | copy-start | bytes 6291460
  187.2 86.2 %collective-permute-start.6 = (bf16[8,32,1152]{2,1,0:T(8,128)(2,1)S(1)}, bf16[8,32,1152]{2,1,0:T(8,128)(2,1)S(1)}, u32[]{:S(2)}, u32[]{:S(2)}) collective-permute-start(bf16[8,32,1152]{2,1,0:T(8,128)(2,1)S(1)} %copy-done.12), channel_id=1, source_target_pairs={{0,2},{1,3},{2,4},{3,5},{4,6},{5,7},{6,0},{7,1},{8,10},{9,11},{10,... | collective-permute-start | bytes 1769480 | tf_op jit(solution)/shard_map/ppermute | solution.py:1221
  193.1 80.3 %collective-permute-start.7 = (bf16[8,32,1152]{2,1,0:T(8,128)(2,1)S(1)}, bf16[8,32,1152]{2,1,0:T(8,128)(2,1)S(1)}, u32[]{:S(2)}, u32[]{:S(2)}) collective-permute-start(bf16[8,32,1152]{2,1,0:T(8,128)(2,1)S(1)} %copy-done.11), channel_id=1, source_target_pairs={{0,4},{1,5},{2,6},{3,7},{4,0},{5,1},{6,2},{7,3},{8,12},{9,13},{10,... | collective-permute-start | bytes 1769480 | tf_op jit(solution)/shard_map/ppermute | solution.py:1221
  194.6 78.8 %collective-permute-start.8 = (bf16[8,32,1152]{2,1,0:T(8,128)(2,1)S(1)}, bf16[8,32,1152]{2,1,0:T(8,128)(2,1)S(1)}, u32[]{:S(2)}, u32[]{:S(2)}) collective-permute-start(bf16[8,32,1152]{2,1,0:T(8,128)(2,1)S(1)} %copy-done.10), channel_id=1, source_target_pairs={{0,6},{1,7},{2,0},{3,1},{4,2},{5,3},{6,4},{7,5},{8,14},{9,15},{10,... | collective-permute-start | bytes 1769480 | tf_op jit(solution)/shard_map/ppermute | solution.py:1221
  273.4 0.8 copy-start.3
  273.4 1.0 copy-start.4
  273.4 1.2 copy-start.5

commit v5 on v4

--- a/solution.py
+++ b/solution.py
@@ -65,6 +65,7 @@
         self.sends, self.recvs = sems
         self.used = 0
         self.open = []
+        self.guarded = []
 
     def take(self, count):
         first = self.used
@@ -89,9 +90,19 @@
     def arrive(self, slot, dst, dev):
         self.copy(slot, dst, dst, dev).wait_recv()
 
+    def send_if(self, when, slot, src, dst, dev):
+        copy = self.copy(slot, src, dst, dev)
+        pl.when(when)(copy.start)
+        self.guarded.append((when, copy))
+
+    def arrive_if(self, when, slot, dst, dev):
+        pl.when(when)(self.copy(slot, dst, dst, dev).wait_recv)
+
     def close(self):
         for copy in self.open:
             copy.wait_send()
+        for when, copy in self.guarded:
+            pl.when(when)(copy.wait_send)
 
 
 def near(place):
@@ -230,21 +241,117 @@
         out[bot] = out[bot] + last[3].astype(F32)
 
 
+class LineGather:
+    def __init__(self, mail, place, src, view):
+        self.mail, self.place, self.src, self.view = mail, place, src, view
+        self.outer = lax.axis_size("blk") // INNER
+        self.base = mail.take(self.copies(self.outer))
+
+    @staticmethod
+    def copies(outer):
+        return 2 * (outer - 1)
+
+    def sides(self):
+        _, _, z, _ = self.place
+        outer = self.outer
+
+        def along(sign):
+            def at(k):
+                there = z + sign * k
+                exists = (there >= 0) & (there < outer)
+                return lax.rem(there + 2 * outer, outer), exists
+
+            return at
+
+        return ((self.base, along(1)), (self.base + outer - 1, along(-1)))
+
+    def begin(self):
+        y, c, z, x = self.place
+        for base, at in self.sides():
+            to, exists = at(1)
+            self.mail.send_if(exists, base, self.src, self.view(z), device(y, c, to, x))
+
+    def relay(self):
+        y, c, _, x = self.place
+        for base, at in self.sides():
+            back, has = at(-1)
+            self.mail.arrive_if(has, base, self.view(back), device(y, c, back, x))
+            for k in range(1, self.outer - 1):
+                to, exists = at(k)
+                self.mail.send_if(
+                    has & exists,
+                    base + k,
+                    self.view(back),
+                    self.view(back),
+                    device(y, c, to, x),
+                )
+
+    def end(self):
+        y, c, _, x = self.place
+        for base, at in self.sides():
+            for k in range(1, self.outer - 1):
+                sender, _ = at(-k)
+                owner, has = at(-k - 1)
+                self.mail.arrive_if(has, base + k, self.view(owner), device(y, c, sender, x))
+
+
 class LineScatter:
-    def __init__(self, mail, place, parts, got):
-        self.mail, self.place, self.parts, self.got = mail, place, parts, got
-        self.line = line_peers(place)
-        self.base = mail.take(len(self.line))
+    def __init__(self, mail, place, parts, bufs):
+        self.mail, self.place, self.parts = mail, place, parts
+        self.far, self.staged, self.final = bufs
+        self.outer = lax.axis_size("blk") // INNER
+        self.base = mail.take(LineGather.copies(self.outer))
+        self.far[...] = jnp.zeros_like(self.far)
+        self.final[...] = jnp.zeros_like(self.final)
+
+    sides = LineGather.sides
+
+    @staticmethod
+    def scratch(outer, shape):
+        return [
+            pltpu.VMEM((2, outer - 2, *shape), BF16),
+            pltpu.VMEM((2, *shape), BF16),
+            pltpu.VMEM((2, *shape), BF16),
+        ]
 
     def begin(self):
-        for slot, (dev, forth, _) in enumerate(self.line):
-            self.mail.send(self.base + slot, self.parts.at[forth], self.got.at[slot], dev)
+        y, c, _, x = self.place
+        for side, (base, at) in enumerate(self.sides()):
+            for k in range(1, self.outer - 1):
+                to, _ = at(k)
+                owner, exists = at(k + 1)
+                self.mail.send_if(
+                    exists,
+                    base + k,
+                    self.parts.at[owner],
+                    self.far.at[side, k - 1],
+                    device(y, c, to, x),
+                )
+
+    def relay(self):
+        y, c, _, x = self.place
+        for side, (base, at) in enumerate(self.sides()):
+            owner, exists = at(1)
+            for k in range(1, self.outer - 1):
+                sender, has = at(-k)
+                self.mail.arrive_if(
+                    exists & has, base + k, self.far.at[side, k - 1], device(y, c, sender, x)
+                )
+            total = self.parts[owner].astype(F32)
+            for k in range(self.outer - 2):
+                total = total + self.far[side, k].astype(F32)
+            self.staged[side] = total.astype(BF16)
+            self.mail.send_if(
+                exists, base, self.staged.at[side], self.final.at[side], device(y, c, owner, x)
+            )
 
     def end(self):
-        total = self.parts[self.place[2]].astype(F32)
-        for slot, (dev, _, _) in enumerate(self.line):
-            self.mail.arrive(self.base + slot, self.got.at[slot], dev)
-            total = total + self.got[slot].astype(F32)
+        y, c, z, x = self.place
+        total = self.parts[z].astype(F32)
+        for side, (base, at) in enumerate(self.sides()):
+            sender, has = at(-1)
+            self.mail.arrive_if(has, base, self.final.at[side], device(y, c, sender, x))
+            total = total + self.final[side].astype(F32)
         return total
 
 
@@ -383,16 +490,16 @@
         self.out[...] = total
 
 
-def call(body, ident, outs, args, copies, scratch=()):
+def call(body, ident, outs, args, copies, scratch=(), scalars=()):
     spec = pl.BlockSpec(memory_space=pltpu.VMEM)
-    return remote_call(body, ident, outs, args, copies, scratch, spec)
-
-
-def remote_call(body, ident, outs, args, copies, scratch, spec):
+    return remote_call(body, ident, outs, args, copies, scratch, scalars, spec)
+
+
+def remote_call(body, ident, outs, args, copies, scratch, scalars, spec):
     return pl.pallas_call(
         body,
         out_shape=tuple(jax.ShapeDtypeStruct(shape, dtype) for shape, dtype in outs),
-        in_specs=[spec] * len(args),
+        in_specs=[pl.BlockSpec(memory_space=pltpu.SMEM)] * len(scalars) + [spec] * len(args),
         out_specs=tuple([spec] * len(outs)),
         scratch_shapes=[
             pltpu.SemaphoreType.DMA((copies,)),
@@ -402,7 +509,7 @@
         compiler_params=pltpu.CompilerParams(
             collective_id=ident, has_side_effects=True, vmem_limit_bytes=60 * 1024 * 1024
         ),
-    )(*args)
+    )(*scalars, *args)
 
 
 def lanes(shape):
@@ -445,6 +552,18 @@
         jnp.concatenate([cos, cos, cos, cos], axis=0).T,
         jnp.concatenate([-sin, sin, -sin, sin], axis=0).T,
     )
+
+
+def place_of(span_ref, oz, r):
+    blocks = lax.axis_size("blk")
+    return span_ref[r // INNER * blocks + oz * INNER + r % INNER]
+
+
+def qk_rows(qk_ref):
+    gains = qk_ref[...]
+    one = jnp.ones((1, gains.shape[1]), F32)
+    query = jnp.concatenate([gains[0:1], gains[0:1]], axis=1)
+    return query, jnp.concatenate([gains[1:2], one], axis=1)
 
 
 def head_forward(raw, gain_vec, cos, sin, size):
@@ -475,17 +594,19 @@
     return peers
 
 
-def start_kernel(
-    x_ref, q_ref, k_ref, v_ref, g1_ref, g2_ref, gate_ref, up_ref, wo_ref,
-    xp_ref, wq_ref, gain_ref, gu_ref, wos_ref,
-    ss, rs, w_ref, g_ref, gs_ref,
+def open_kernel(
+    span_ref, x_ref, q_ref, k_ref, v_ref, g1_ref, g2_ref, gate_ref, up_ref, wo_ref, wd_ref, og_ref,
+    qk_ref, freq_ref,
+    qs_ref, kvs_ref, raw_ref, norm_ref, ogs_ref, gus_ref, wq_ref, gain_ref, wos_ref, wds_ref,
+    cos_ref, sin_ref,
+    ss, rs, w_ref, g_ref, gs_ref, xp_ref, gu_ref, kv_ref,
 ):
     place = y, c, z, x = here()
     me = rank(y, c, x)
     head = y * CORES + c
     mail = Mail((ss, rs))
     peers = all_peers(place)
-    plane, w_rows, _ = w_ref.shape
+    plane, w_rows, cols = w_ref.shape
     heads, outer = wq_ref.shape[:2]
     q_cols = q_ref.shape[1] // plane
     k_cols = k_ref.shape[1] // plane
@@ -501,14 +622,24 @@
     greet([p[0] for p in peers])
     w_base, g_base = mail.take(len(peers)), mail.take(len(peers))
     rows = PlaneGather(mail, place, x_ref, xp_ref)
+    grads = PlaneGather(mail, place, og_ref, ogs_ref)
+    swap = PlaneSwap(mail, place, gu_ref, gus_ref)
     block = RowsOut(mail, place, wo_ref, wos_ref)
+    down = LineGather(mail, place, wd_ref, lambda oz: wds_ref.at[oz])
+    half = plane // 2
+    pairs = []
+    for part in range(2):
+        at = pl.ds(part * half, half)
+        pairs.append(
+            LineGather(mail, place, kv_ref.at[at], lambda oz, at=at: kvs_ref.at[oz, at])
+        )
     for slot, (dev, _, py, pc, _, px) in reversed(list(enumerate(peers))):
         mail.send(g_base + slot, g_ref, gs_ref.at[z, me], dev)
         mail.send(w_base + slot, w_ref.at[rank(py, pc, px)], wq_ref.at[head, z, x], dev)
     rows.begin()
     gs_ref[z, me] = g_ref[...]
     wq_ref[head, z, x] = w_ref[me]
-    block.begin()
+    wds_ref[z] = wd_ref[...]
     f_cols = gate_ref.shape[1] // (heads * outer * INNER)
     main = outer * f_cols // LANES * LANES
     for oh in range(heads):
@@ -536,6 +667,13 @@
             tails = jnp.concatenate([gate[:, main:], up[:, main:]], axis=1)
             gu_ref[p, :, 2 * main :] = tails.astype(BF16)
     rows.middle()
+    tok = x_ref.shape[0]
+    for r in range(plane):
+        first = place_of(span_ref, z, r) * tok
+        where_at = (first + lanes((1, tok))).astype(F32)
+        angles = where_at * freq_ref[...]
+        cos_ref[r] = jnp.cos(angles)
+        sin_ref[r] = jnp.sin(angles)
     rows.end()
     for slot, (_, dev, py, pc, oz, px) in enumerate(peers):
         mail.arrive(g_base + slot, gs_ref.at[oz, rank(py, pc, px)], dev)
@@ -551,59 +689,48 @@
             ],
             axis=1,
         )
+    gain_one = gain_ref[0:1]
+
+    def one_norm(r, carry):
+        rows_in = xp_ref[r].astype(F32)
+        norm_ref[r] = (rows_in * rms_of(rows_in) * gain_one).astype(BF16)
+        return carry
+
+    lax.fori_loop(0, plane, one_norm, 0)
     for slot, (_, dev, py, pc, oz, px) in enumerate(peers):
         mail.arrive(w_base + slot, wq_ref.at[py * CORES + pc, oz, px], dev)
-    block.end()
-    mail.close()
-
-
-def line_kernel(
-    x_ref, w_ref, gain_ref, qk_ref, cos_ref, sin_ref, og_ref, gu_ref,
-    q_ref, kvs_ref, raw_ref, norm_ref, ogs_ref, gus_ref,
-    ss, rs, kv_ref,
-):
-    place = y, c, z, x = here()
-    mail = Mail((ss, rs))
-    line = line_peers(place)
-    greet([p[0] for p in line] + [p[0] for p in plane_peers(place)])
-    rows = PlaneGather(mail, place, og_ref, ogs_ref)
-    swap = PlaneSwap(mail, place, gu_ref, gus_ref)
-    base = mail.take(2 * len(line))
-    rows.begin()
-    count, _, _ = x_ref.shape
-    q_cols = q_ref.shape[2]
+    block.begin()
+    grads.begin()
+    down.begin()
     size = q_cols // 2
-    gain_one = gain_ref[0:1]
-    gain_q, gain_k = qk_ref[0:1], qk_ref[1:2]
+    gain_q, gain_k = qk_rows(qk_ref)
+    weights = wq_ref[...].reshape(heads * outer * INNER * w_rows, cols)
 
     def one_block(r, carry):
-        block = x_ref[r].astype(F32)
-        normed = (block * rms_of(block) * gain_one).astype(BF16)
-        norm_ref[r] = normed
-        raw = jnp.dot(normed, w_ref[...], preferred_element_type=F32)
+        raw = jnp.dot(norm_ref[r], weights, preferred_element_type=F32)
         raw_ref[r] = raw
         cos, sin = turn(cos_ref, sin_ref, r)
-        q_ref[r] = head_forward(raw[:, :q_cols], gain_q, cos, sin, size).astype(BF16)
+        qs_ref[r] = head_forward(raw[:, :q_cols], gain_q, cos, sin, size).astype(BF16)
         pair = raw[:, q_cols:]
         turned = head_forward(pair, gain_k, cos, sin, size)
         kv_ref[r] = jnp.where(lanes(pair.shape) < size, turned, pair).astype(BF16)
         return carry
 
-    half = count // 2
     for part in range(2):
         lax.fori_loop(part * half, (part + 1) * half, one_block, 0)
-        at = pl.ds(part * half, half)
-        for slot, (dev, _, _) in enumerate(line):
-            mail.send(base + 2 * slot + part, kv_ref.at[at], kvs_ref.at[z, at], dev)
+        pairs[part].begin()
     kvs_ref[z] = kv_ref[...]
-    rows.middle()
+    grads.middle()
     swap.begin()
-    rows.end()
+    pairs[0].relay()
+    pairs[1].relay()
+    down.relay()
+    grads.end()
     swap.end()
-    for part in range(2):
-        at = pl.ds(part * half, half)
-        for slot, (dev, _, back) in enumerate(line):
-            mail.arrive(base + 2 * slot + part, kvs_ref.at[back, at], dev)
+    block.end()
+    pairs[0].end()
+    pairs[1].end()
+    down.end()
     mail.close()
 
 
@@ -659,73 +786,74 @@
     mail.close()
 
 
-def back_kernel(
-    dkv_ref, parts_ref, op_ref, mid_ref,
-    kv_ref, out_ref, ops_ref,
-    ss, rs, acc, got, op_got, *bufs,
-):
-    place = here()
-    mail = Mail((ss, rs))
-    greet(blk_peers(place) + list(near(place)))
-    line = LineScatter(mail, place, dkv_ref, got)
-    rows = PlaneScatter(mail, place, parts_ref, acc, bufs)
-    block = RowsBack(mail, place, op_ref, op_got, ops_ref)
-    line.begin()
-    rows.begin()
-    block.begin()
-    rows.middle()
-    rows.end()
-    out_ref[...] = (mid_ref[...] + acc[...]).astype(BF16)
-    kv_ref[...] = line.end().astype(BF16)
-    block.end()
-    mail.close()
-
-
-def last_kernel(
-    dq_ref, dkv_ref, raw_ref, norm_ref, w_ref, qk_ref, cos_ref, sin_ref,
+def close_kernel(
+    dq_ref, dkv_ref, outp_ref, op_ref, mid_ref, raw_ref, norm_ref, w_ref, qk_ref, cos_ref, sin_ref,
     x_ref, dmid_ref, gain_ref, g2_ref, dg_ref, *refs,
 ):
     outer = lax.axis_size("blk") // INNER
     gu_refs, refs = refs[:outer], refs[outer:]
-    (in_ref, ws_ref, gus_ref, down_ref, small_ref,
-     ss, rs, dqkv, parts, acc, grads, got, held, gu_own, dg_got, small, p_got, z_got, *bufs) = refs
+    (out_ref, ops_ref, in_ref, ws_ref, gus_ref, down_ref, small_ref,
+     ss, rs, dqkv, parts, acc, grads, held, gu_own, small, p_got, z_got, op_got, *bufs) = refs
     place = y, c, z, x = here()
     me = rank(y, c, x)
     mail = Mail((ss, rs))
     peers, line = plane_peers(place), line_peers(place)
-    greet([p[0] for p in line] + [p[0] for p in peers])
     swap = PlaneSwap(mail, place, gu_own, gus_ref)
-    weights = LineScatter(mail, place, grads, got)
-    down = LineScatter(mail, place, dg_ref, dg_got)
+    pairs = LineScatter(mail, place, dkv_ref, bufs[0:3])
+    weights = LineScatter(mail, place, grads, bufs[3:6])
+    down = LineScatter(mail, place, dg_ref, bufs[6:9])
+    block = RowsBack(mail, place, op_ref, op_got, ops_ref)
+
+    def make(oblock):
+        parts[oblock] = lax.dot_general(
+            dqkv[oblock], w_ref[...], NT, preferred_element_type=F32
+        ).astype(BF16)
+
+    outs = PlaneScatter(mail, place, outp_ref, acc, bufs[9:14])
+    rows = PlaneScatter(mail, place, parts, acc, bufs[14:19], make)
+    greet([p[0] for p in peers] + blk_peers(place))
+    pairs.begin()
+    outs.begin()
+    block.begin()
+
+    count, tok, q_cols = dq_ref.shape
+    size = q_cols // 2
+    gain_q, gain_k = qk_rows(qk_ref)
+
+    def one_query(r, total):
+        cos, sin = turn(cos_ref, sin_ref, r)
+        raw = raw_ref[r, :, :q_cols]
+        dq, part = head_back(raw, gain_q, cos, sin, size, dq_ref[r].astype(F32))
+        dqkv[r, :, :q_cols] = dq.astype(BF16)
+        return total + part
+
+    zero = jnp.zeros((1, q_cols), F32)
+    q_sum = lax.fori_loop(0, count, one_query, zero)
+    pairs.relay()
+    down.begin()
+    outs.middle()
     total = gu_refs[0][...].astype(F32)
     for ref in gu_refs[1:]:
         total = total + ref[...].astype(F32)
     gu_own[...] = total.astype(BF16).reshape(gu_own.shape)
+    outs.end()
     swap.begin()
-
-    count, tok, q_cols = dq_ref.shape
-    size = q_cols // 2
-    gain_q, gain_k = qk_ref[0:1], qk_ref[1:2]
-
-    def one_block(r, sums):
+    out_ref[...] = (mid_ref[...] + acc[...]).astype(BF16)
+    dqkv[:, :, q_cols:] = pairs.end().astype(BF16)
+
+    def one_key(r, total):
         cos, sin = turn(cos_ref, sin_ref, r)
-        raw_q, raw_k = raw_ref[r, :, :q_cols], raw_ref[r, :, q_cols:]
-        dq, q_sum = head_back(raw_q, gain_q, cos, sin, size, dq_ref[r].astype(F32))
-        dkv = dkv_ref[r].astype(F32)
-        dk, k_sum = head_back(raw_k, gain_k, cos, sin, size, dkv)
-        dqkv[r, :, :q_cols] = dq.astype(BF16)
+        dkv = dqkv[r, :, q_cols:].astype(F32)
+        dk, part = head_back(raw_ref[r, :, q_cols:], gain_k, cos, sin, size, dkv)
         dqkv[r, :, q_cols:] = jnp.where(lanes(dk.shape) < size, dk, dkv).astype(BF16)
-        return sums[0] + q_sum, sums[1] + k_sum
-
-    zero = jnp.zeros((1, q_cols), F32)
-    q_sum, k_sum = lax.fori_loop(0, count, one_block, (zero, zero))
-
+        return total + part
+
+    k_sum = lax.fori_loop(0, count, one_key, zero)
     width = norm_ref.shape[2]
-    flat = dqkv[...].reshape(count * tok, -1)
     w_grad = lax.dot_general(
         norm_ref[...].reshape(count * tok, width),
-        flat,
-        (((0,), (0,)), ((), ())),
+        dqkv[...].reshape(count * tok, -1),
+        TN,
         preferred_element_type=F32,
     ).astype(BF16)
     heads, w_rows = grads.shape[1], grads.shape[3]
@@ -735,16 +863,9 @@
             first = (oh * outer + oz) * stride
             grads[oz, oh] = w_grad[first : first + stride].reshape(INNER, w_rows, -1)
     weights.begin()
-
-    def make(block):
-        parts[block] = lax.dot_general(
-            dqkv[block], w_ref[...], NT, preferred_element_type=F32
-        ).astype(BF16)
-
-    rows = PlaneScatter(mail, place, parts, acc, bufs, make)
     rows.begin()
     rows.middle()
-    down.begin()
+    weights.relay()
     rows.end()
     back, dgain = rms_back(x_ref[...].astype(F32), gain_ref[0:1], acc[...])
     in_ref[...] = (dmid_ref[...] + back).astype(BF16)
@@ -757,6 +878,7 @@
     for slot, (dev, other, _) in enumerate(peers):
         mail.send(p_base + slot, small, p_got.at[me], dev)
     p_got[me] = small[...]
+    down.relay()
     held[...] = weights.end().reshape(held.shape)
     for slot, (dev, other, _) in enumerate(peers):
         mail.send(w_base + slot, held.at[other], ws_ref.at[me], dev)
@@ -767,6 +889,7 @@
     for slot, (dev, _, _) in enumerate(line):
         mail.send(z_base + slot, z_got.at[z], z_got.at[z], dev)
     swap.end()
+    block.end()
     down_ref[...] = down.end()
     for slot, (dev, other, _) in enumerate(peers):
         mail.arrive(w_base + slot, ws_ref.at[other], dev)
@@ -776,7 +899,7 @@
     mail.close()
 
 
-def finish_kernel(own_ref, ws_ref, gus_ref, small_ref, *refs):
+def finish_kernel(ws_ref, gus_ref, small_ref, *refs):
     n1_ref, n2_ref, q_ref, k_ref, v_ref, qk_ref, gate_ref, up_ref = refs[-8:]
     passed = refs[:-8]
     for src, dst in zip(passed[: len(passed) // 2], passed[len(passed) // 2 :]):
@@ -794,7 +917,8 @@
         k_ref[:, at] = jnp.where(left, one, pltpu.roll(two, k_cols, 1))
         v_ref[:, at] = jnp.where(left, pltpu.roll(one, k_cols, 1), two)
     width = small_ref.shape[1]
-    move = lax.rem(width - own_ref[0], width)
+    own = (lax.axis_index("head") * lax.axis_size("blk") + lax.axis_index("blk")) * w_rows
+    move = lax.rem(width - own, width)
     totals = pltpu.roll(small_ref[...], move, 1)
     n1_ref[...] = totals[0:1, :w_rows]
     n2_ref[...] = totals[1:2, :w_rows]
@@ -830,25 +954,13 @@
             )
 
 
-def down_rows(ref, oz, f_rows, piece):
-    pack = math.gcd(f_rows, 16)
-    if pack == 16:
-        ref[pl.ds(pl.multiple_of(oz * f_rows, pack), f_rows)] = piece[...]
-        return
-    for at in range(ref.shape[0] // f_rows):
-
-        @pl.when(oz == at)
-        def _():
-            ref[at * f_rows : (at + 1) * f_rows] = piece[...]
-
-
-def feed_kernel(z_ref, n2_ref, og_ref, *refs):
+def feed_kernel(n2_ref, og_ref, wd_ref, *refs):
     outer = lax.axis_size("blk") // INNER
-    pieces, downs, refs = refs[:outer], refs[outer : 2 * outer], refs[2 * outer :]
+    pieces, refs = refs[:outer], refs[outer:]
     out_ref, dn_ref, dg_ref = refs[:3]
     chunks = refs[3 : 3 + outer]
-    wgu, wd_ref, hid, dgu, gg = refs[3 + outer :]
-    z = z_ref[0]
+    wgu, hid, dgu, gg = refs[3 + outer :]
+    z = here()[2]
     heads, stride, _ = pieces[0].shape
     ff = wd_ref.shape[0]
     main = ff // LANES * LANES
@@ -859,8 +971,6 @@
             at = pl.multiple_of((oh * outer + oz) * stride, stride)
             wgu[pl.ds(at, stride)] = piece[oh]
     f_rows = ff // outer
-    for k, piece in enumerate(downs):
-        down_rows(wd_ref, lax.rem(z + outer - k, outer), f_rows, piece)
     plane, rows, width = n2_ref.shape
 
     def both(gate, up, dhid):
@@ -940,11 +1050,21 @@
     return jnp.concatenate([first, second], axis=0).astype(BF16)
 
 
-def forward_kernel(own_ref, at_ref, q_ref, kv_ref, out_ref, lse_ref, keys, ones):
+def span_table(span_ref, at_ref, plane):
+    def one(block, carry):
+        at_ref[place_of(span_ref, block // plane, block % plane)] = block
+        return carry
+
+    lax.fori_loop(0, at_ref.shape[0], one, 0)
+
+
+def forward_kernel(span_ref, q_ref, kv_ref, out_ref, lse_ref, at_ref, keys, ones):
     count, rows, size2 = q_ref.shape
     size = size2 // 2
     scale = float(size) ** (-0.5) * LOG2E
     step = SPANS * rows
+    z = here()[2]
+    span_table(span_ref, at_ref, count)
 
     def place_rows(p, carry):
         block = kv_ref[at_ref[p]]
@@ -955,7 +1075,7 @@
     lax.fori_loop(0, kv_ref.shape[0], place_rows, 0)
 
     def one_block(r, carry):
-        place = own_ref[r]
+        place = place_of(span_ref, z, r)
         queries = stack_left(q_ref[r], size)
 
         def weights(c):
@@ -989,13 +1109,29 @@
 
 
 def backward_kernel(
-    own_ref, at_ref, q_ref, kv_ref, out_ref, do_ref, lse_ref, dq_ref, dkv_ref, keys, turned, sums
+    span_ref, q_ref, kv_ref, out_ref, dmid_ref, wo_ref, lse_ref,
+    dq_ref, dkv_ref, op_ref,
+    at_ref, keys, turned, sums,
 ):
     count, rows, size2 = q_ref.shape
     size = size2 // 2
     scale = float(size) ** (-0.5)
     step = SPANS * rows
     spans = kv_ref.shape[0]
+    z = here()[2]
+    span_table(span_ref, at_ref, count)
+    width = dmid_ref.shape[2]
+    op = lax.dot_general(
+        out_ref[...].reshape(count * rows, size2),
+        dmid_ref[...].reshape(count * rows, width),
+        TN,
+        preferred_element_type=F32,
+    )
+    per, inner, w_rows, _ = op_ref.shape
+    for j in range(per):
+        for ox in range(inner):
+            first = (j * inner + ox) * w_rows
+            op_ref[j, ox] = op[first : first + w_rows].astype(BF16)
 
     def place_rows(p, carry):
         block = kv_ref[at_ref[p]]
@@ -1007,10 +1143,12 @@
     sums[...] = jnp.zeros_like(sums)
 
     def one_block(r, carry):
-        place = own_ref[r]
+        place = place_of(span_ref, z, r)
         queries = stack_left(q_ref[r], size)
-        grads = stack_right(do_ref[r], size)
-        both = (do_ref[r].astype(F32) * out_ref[r].astype(F32)).T
+        grad = lax.dot_general(dmid_ref[r], wo_ref[...], NT, preferred_element_type=F32)
+        grad = grad.astype(BF16)
+        grads = stack_right(grad, size)
+        both = (grad.astype(F32) * out_ref[r].astype(F32)).T
         delta = jnp.concatenate(
             [jnp.sum(both[:size], axis=0)[None], jnp.sum(both[size:], axis=0)[None]], axis=1
         )
@@ -1094,7 +1232,6 @@
     blocks = lax.axis_size("blk")
     outer = blocks // INNER
     plane = heads * INNER
-    z = lax.axis_index("blk") // INNER
     rows, width = block_input.shape
     size = qk_gain.shape[1]
     w_rows = w_query.shape[0]
@@ -1112,16 +1249,26 @@
         ]
         return [piece] + moved
 
-    down_pieces = along(w_down)
-    x_all, wqkv, gains, gu8, out_mine = call(
-        start_kernel,
+    half = size // 2
+    frequency = jnp.exp(jnp.arange(half, dtype=F32) * F32(-2.0 * math.log(THETA) / size))
+    frequency = jnp.broadcast_to(frequency[:, None], (half, rows))
+    (queries, kv_all, raw, normed, og_all, gu_piece, wqkv, gains, out_mine, down_full,
+     cosine, sine) = call(
+        open_kernel,
         1,
         [
+            ((plane, rows, q_cols), BF16),
+            ((outer, plane, rows, q_cols), BF16),
+            ((plane, rows, a_cols), F32),
             ((plane, rows, width), BF16),
+            ((plane, rows, width), BF16),
+            ((plane, w_rows, 2 * ff), BF16),
             ((heads, outer, INNER, w_rows, a_cols), BF16),
             ((8, width), F32),
-            ((plane, w_rows, 2 * ff), BF16),
             ((outer // INNER, INNER, w_rows, width), BF16),
+            ((outer, f_rows, width), BF16),
+            ((plane, half, rows), F32),
+            ((plane, half, rows), F32),
         ],
         (
             block_input,
@@ -1133,59 +1280,42 @@
             w_gate,
             w_up,
             w_out,
+            w_down,
+            out_grad,
+            qk_gain,
+            frequency,
         ),
-        2 * (outer * plane - 1) + PlaneGather.COPIES + outer,
+        2 * (outer * plane - 1)
+        + 2 * PlaneGather.COPIES
+        + PlaneSwap.COPIES
+        + outer
+        + 3 * LineGather.copies(outer),
         [
             pltpu.VMEM((plane, w_rows, a_cols), BF16),
             pltpu.VMEM((1, LANES), F32),
             pltpu.VMEM((outer, plane, 1, LANES), F32),
+            pltpu.VMEM((plane, rows, width), BF16),
+            pltpu.VMEM((plane, w_rows, 2 * ff), BF16),
+            pltpu.VMEM((plane, rows, q_cols), BF16),
         ],
+        (span_order,),
     )
     wqkv = wqkv.reshape(width, a_cols)
     out_mine = out_mine.reshape(q_cols, width)
-
-    by_place = span_order.reshape(heads, outer, INNER)
-    own_spans = lax.dynamic_index_in_dim(by_place, z, 1, keepdims=False).reshape(plane)
-    all_spans = by_place.transpose(1, 0, 2).reshape(spans)
-    every = jnp.arange(spans, dtype=jnp.int32)
-    span_at = jnp.sum(jnp.where(all_spans[:, None] == every[None, :], every[:, None], 0), axis=0)
-    where_at = own_spans[:, None] * rows + jnp.arange(rows, dtype=jnp.int32)[None, :]
-    half = size // 2
-    frequency = jnp.exp(jnp.arange(half, dtype=F32) * F32(-2.0 * math.log(THETA) / size))
-    angles = where_at.astype(F32)[:, None, :] * frequency[None, :, None]
-    cosine, sine = jnp.cos(angles), jnp.sin(angles)
-    ones = jnp.ones((size,), F32)
-    qk_rows = jnp.stack(
-        [
-            jnp.concatenate([qk_gain[0], qk_gain[0]]),
-            jnp.concatenate([qk_gain[1], ones]),
-        ]
-    )
-
-    queries, kv_all, raw, normed, og_all, gu_piece = call(
-        line_kernel,
-        2,
-        [
-            ((plane, rows, q_cols), BF16),
-            ((outer, plane, rows, q_cols), BF16),
-            ((plane, rows, a_cols), F32),
-            ((plane, rows, width), BF16),
-            ((plane, rows, width), BF16),
-            ((plane, w_rows, 2 * ff), BF16),
-        ],
-        (x_all, wqkv, gains, qk_rows, cosine, sine, out_grad, gu8),
-        2 * n_line + PlaneGather.COPIES + PlaneSwap.COPIES,
-        [pltpu.VMEM((plane, rows, q_cols), BF16)],
-    )
+    down_full = down_full.reshape(ff, width)
     gu_pieces = along(gu_piece.reshape(heads, stride, 2 * ff))
     kv_blocks = kv_all.reshape(spans, rows, q_cols)
     pairs = plane * rows * spans * rows * q_cols
     attended, log_total = local_call(
         forward_kernel,
-        (own_spans, span_at),
+        (span_order,),
         (queries, kv_blocks),
         [((plane, rows, q_cols), BF16), ((plane, 8, 2 * rows), F32)],
-        [pltpu.VMEM((spans * rows, q_cols), BF16), pltpu.VMEM((spans * rows, q_cols), BF16)],
+        [
+            pltpu.SMEM((spans,), jnp.int32),
+            pltpu.VMEM((spans * rows, q_cols), BF16),
+            pltpu.VMEM((spans * rows, q_cols), BF16),
+        ],
         4 * pairs,
     )
     middle, normed2 = call(
@@ -1200,8 +1330,8 @@
 
     out_parts, dn_parts, down_grad, *gu_grads = local_call(
         feed_kernel,
-        (jnp.reshape(z, (1,)).astype(jnp.int32),),
-        (normed2, og_all, *gu_pieces, *down_pieces),
+        (),
+        (normed2, og_all, down_full, *gu_pieces),
         [
             ((plane, rows, width), BF16),
             ((plane, rows, width), BF16),
@@ -1210,7 +1340,6 @@
         + [((plane, w_rows, 2 * ff), BF16)] * outer,
         [
             pltpu.VMEM((width, 2 * ff), BF16),
-            pltpu.VMEM((ff, width), BF16),
             pltpu.VMEM((plane * rows, ff), BF16),
             pltpu.VMEM((plane * rows, 2 * ff), BF16),
             pltpu.VMEM((outer, plane, w_rows, 2 * ff), BF16),
@@ -1229,45 +1358,29 @@
         [pltpu.VMEM((rows, width), BF16)] + PlaneScatter.scratch(rows, width),
     )
 
-    dmid_rows = dmid_all.reshape(plane * rows, width)
-    out_proj = lax.dot_general(
-        attended.reshape(plane * rows, q_cols), dmid_rows, TN, preferred_element_type=F32
-    )
-    dattended = lax.dot_general(dmid_rows, out_mine, NT, preferred_element_type=F32).astype(BF16)
-    dqueries, dkv = local_call(
+    dqueries, dkv, out_proj = local_call(
         backward_kernel,
-        (own_spans, span_at),
-        (queries, kv_blocks, attended, dattended.reshape(plane, rows, q_cols), log_total),
-        [((plane, rows, q_cols), BF16), ((spans, rows, q_cols), BF16)],
+        (span_order,),
+        (queries, kv_blocks, attended, dmid_all, out_mine, log_total),
         [
+            ((plane, rows, q_cols), BF16),
+            ((spans, rows, q_cols), BF16),
+            ((outer // INNER, INNER, w_rows, width), BF16),
+        ],
+        [
+            pltpu.SMEM((spans,), jnp.int32),
             pltpu.VMEM((spans * rows, q_cols), BF16),
             pltpu.VMEM((q_cols, spans * rows), BF16),
             pltpu.VMEM((spans * rows, q_cols), F32),
         ],
         10 * pairs,
     )
-    dkv_own, block_output, out_proj_grad = call(
-        back_kernel,
+    block_output, out_proj_grad, input_grad, w_own, gu_own, down_out, small = call(
+        close_kernel,
         5,
-        [((plane, rows, q_cols), BF16), ((rows, width), BF16), ((w_rows, width), F32)],
-        (
-            dkv.reshape(outer, plane, rows, q_cols),
-            out_parts,
-            out_proj.astype(BF16).reshape(outer // INNER, INNER, w_rows, width),
-            middle,
-        ),
-        n_line + PlaneScatter.COPIES + outer,
         [
-            pltpu.VMEM((rows, width), F32),
-            pltpu.VMEM((n_line, plane, rows, q_cols), BF16),
-            pltpu.VMEM((outer, w_rows, width), BF16),
-        ]
-        + PlaneScatter.scratch(rows, width),
-    )
-    input_grad, w_own, gu_own, down_out, small = call(
-        last_kernel,
-        6,
-        [
+            ((rows, width), BF16),
+            ((w_rows, width), F32),
             ((rows, width), BF16),
             ((plane, w_rows, a_cols), F32),
             ((plane, w_rows, 2 * ff), BF16),
@@ -1276,11 +1389,14 @@
         ],
         (
             dqueries,
-            dkv_own,
+            dkv.reshape(outer, plane, rows, q_cols),
+            out_parts,
+            out_proj,
+            middle,
             raw,
             normed,
             wqkv,
-            qk_rows,
+            qk_gain,
             cosine,
             sine,
             block_input,
@@ -1290,26 +1406,33 @@
             down_grad,
             *gu_sums,
         ),
-        3 * n_line + 14 + PlaneScatter.COPIES + PlaneSwap.COPIES,
+        3 * LineGather.copies(outer)
+        + n_line
+        + 14
+        + outer
+        + 2 * PlaneScatter.COPIES
+        + PlaneSwap.COPIES,
         [
             pltpu.VMEM((plane, rows, a_cols), BF16),
             pltpu.VMEM((plane, rows, width), BF16),
             pltpu.VMEM((rows, width), F32),
             pltpu.VMEM((outer, heads, INNER, w_rows, a_cols), BF16),
-            pltpu.VMEM((n_line, heads, INNER, w_rows, a_cols), BF16),
             pltpu.VMEM((plane, w_rows, a_cols), F32),
             pltpu.VMEM((plane, w_rows, 2 * ff), BF16),
-            pltpu.VMEM((n_line, f_rows, width), BF16),
             pltpu.VMEM((8, width), F32),
             pltpu.VMEM((plane, 8, width), F32),
             pltpu.VMEM((outer, 8, width), F32),
+            pltpu.VMEM((outer, w_rows, width), BF16),
         ]
+        + LineScatter.scratch(outer, (plane, rows, q_cols))
+        + LineScatter.scratch(outer, (heads, INNER, w_rows, a_cols))
+        + LineScatter.scratch(outer, (f_rows, width))
+        + PlaneScatter.scratch(rows, width)
         + PlaneScatter.scratch(rows, width),
     )
-    own = (lax.axis_index("head") * blocks + lax.axis_index("blk")) * w_rows
     outs = local_call(
         finish_kernel,
-        (jnp.reshape(own, (1,)).astype(jnp.int32),),
+        (),
         (w_own, gu_own, small, block_output, input_grad, out_proj_grad, down_out),
         [
             ((rows, width), BF16),

time: 338 us -> 292 us (0.86)
  Pallas kernels: 296 us -> 277 us
  starting transfers between devices: 23.3 us -> 9.59 us
  waiting for transfers between devices: 6.47 us -> 1.89 us
  matrix products: 4.33 us -> 0 us
    pallas_call x6 -> x4, Pallas kernels: 228 us -> 205 us  [remote_call(): pl.pallas_call(body, out_shape=tuple((jax.ShapeDtypeStruct(shape, dtype)...]
    ppermute x6 -> x3, starting transfers between devices: 13.1 us -> 3.21 us  [along(): lax.ppermute(piece, 'blk', shifts(outer, step))]
    ppermute x6 -> x3, waiting for transfers between devices: 6.46 us -> 1.88 us  [along(): lax.ppermute(piece, 'blk', shifts(outer, step))]
    dot_general x2 -> x0, matrix products: 4.33 us -> none  [the longest x1 2.91 us: local(): lax.dot_general(attended.reshape(plane * rows, q_cols), dmid_rows, TN, pr...]
    pallas_call x4, Pallas kernels: 67.8 us -> 71.9 us  [local_call(): pl.pallas_call(body, out_shape=tuple((jax.ShapeDtypeStruct(shape, dtype)...]
    ppermute x3, starting transfers between devices: 10.3 us -> 6.38 us  [local(): lax.ppermute(gu_grads[step], 'blk', shifts(outer, step))]
  transfers between devices with their start and end apart: 9 -> 6, of which waited for: 1 -> 1; matrix products, arithmetic and copies ran while one was open for 2% -> 0% of each run, Pallas kernels for 55% -> 36%
where the time goes in v5:
time: 292 us
  Pallas kernels  277 us (95%)
  starting transfers between devices  9.59 us (3%)
    pallas_call x4, Pallas kernels, remote_call(): pl.pallas_call(body, out_shape=tuple((jax.ShapeDtypeStruct(shape, dtype)...  205 us
    pallas_call x4, Pallas kernels, local_call(): pl.pallas_call(body, out_shape=tuple((jax.ShapeDtypeStruct(shape, dtype)...  71.9 us
    ppermute x3, starting transfers between devices, local(): lax.ppermute(gu_grads[step], 'blk', shifts(outer, step))  6.38 us
  transfers between devices with their start and end apart: 6, of which 1 were waited for; matrix products, arithmetic and copies ran while one was open for 0% of the time, Pallas kernels for 36%

profile of v5, /device:TPU:0, one launch (start us, length us, event | category | flops | bytes accessed | tf_op | source)
XLA Modules:
  0.0 291.8 jit_solution(12620237175148731422)
XLA Ops:
  0.7 0.7 broadcast_in_dim.2.freq_ref
  1.3 76.0 %shard_map.220 = (bf16[8,128,128]{2,1,0:T(8,128)(2,1)}, bf16[4,8,128,128]{3,2,1,0:T(8,128)(2,1)}, f32[8,128,256]{2,1,0:T(8,128)}, bf16[8,128,1024]{2,1,0:T(8,128...) custom-call(s32[32]{0:T(128)} %span_ref.5, ...), custom_call_target="tpu_custom_call" | custom-call | tf_op jit(solution)/shard_map/pallas_call | solution.py:499
  77.3 2.6 collective-permute-start.2
  79.9 0.0 collective-permute-start.1
  79.9 0.6 collective-permute-start
  80.5 18.7 %shard_map.221 = (bf16[8,128,128]{2,1,0:T(8,128)(2,1)}, f32[8,8,256]{2,1,0:T(8,128)}) custom-call(s32[32]{0:T(128)} %span_ref.5, bf16[8,128,128]{2,1,0:T(8,128)(2,1)} %get-tuple-element.60.q_ref, bf16[32,128,128]{2,1,0:T(8,128)(2,1)} %bitcast.17), custom_call_target="tpu_custom_call" | custom-call | flops 2147483648 | bytes 8388608 | tf_op jit(solution)/shard_map/pallas_call | solution.py:1197
  99.2 28.4 %shard_map.222 = (f32[128,1024]{1,0:T(8,128)}, bf16[8,128,1024]{2,1,0:T(8,128)(2,1)}) custom-call(bf16[8,128,128]{2,1,0:T(8,128)(2,1)} %get-tuple-element.62.att_ref.out_ref, bf16[128,1024]{1,0:T(8,128)(2,1)} %bitcast.12, bf16[128,1024]{1,0:T(8,128)(2,1)} %x_ref.5, f32[8,1024]{1,0:T(8,128)} %get-tuple-element.64.gain_ref), custom_call_target="tpu_custom_call" | custom-call | tf_op jit(solution)/shard_map/pallas_call | solution.py:499
  127.7 0.0 collective-permute-done.2.refs_3_
  127.7 0.0 copy-start.3
  127.7 1.9 collective-permute-done.1.refs_2_
  129.6 0.0 copy-start.4
  129.6 0.0 collective-permute-done.refs_1_
  129.6 0.0 copy-start.5
  129.6 0.0 copy-done.3
  129.6 0.8 copy-done.4
  130.4 0.2 copy-done.5
  130.6 19.6 %shard_map.223 = (bf16[8,128,1024]{2,1,0:T(8,128)(2,1)}, bf16[8,128,1024]{2,1,0:T(8,128)(2,1)}, bf16[4,144,1024]{2,1,0:T(8,128)(2,1)}, bf16[8,32,1152]{2,1,0:T(8...) custom-call(bf16[8,128,1024]{2,1,0:T(8,128)(2,1)} %get-tuple-element.65.n2_ref,, ...), custom_call_target="tpu_custom_call" | custom-call | flops 10871635968 | bytes 8388608 | tf_op jit(solution)/shard_map/pallas_call | solution.py:1197
  150.2 2.7 collective-permute-start.3
  152.9 0.8 collective-permute-start.4
  153.7 2.9 %collective-permute-start.5 = (bf16[8,32,1152]{2,1,0:T(8,128)(2,1)}, bf16[8,32,1152]{2,1,0:T(8,128)(2,1)S(1)}, u32[]{:S(2)}, u32[]{:S(2)}) collective-permute-start(bf16[8,32,1152]{2,1,0:T(8,128)(2,1)} %get-tuple-element.88), channel_id=1, source_target_pairs={{0,6},{1,7},{2,0},{3,1},{4,2},{5,3},{6,4},{7,5},{8,14},{9,15},{10,... | collective-permute-start | bytes 1769480 | tf_op jit(solution)/shard_map/ppermute | solution.py:1350
  156.6 28.6 %shard_map.224 = (f32[128,1024]{1,0:T(8,128)}, bf16[8,128,1024]{2,1,0:T(8,128)(2,1)}, f32[1,1024]{1,0:T(1,128)}) custom-call(bf16[8,128,1024]{2,1,0:T(8,128)(2,1)} %get-tuple-element.69.parts_ref, f32[128,1024]{1,0:T(8,128)} %get-tuple-element.70.mid_ref, bf16[128,1024]{1,0:T(8,128)(2,1)} %og_ref.3, f32[8,1024]{1,0:T(8,128)} %get-tuple-element.64.gain_ref), custom_call_target="tpu_custom_call" | custom-call | tf_op jit(solution)/shard_map/pallas_call | solution.py:499
  185.2 30.2 %shard_map.225 = (bf16[8,128,128]{2,1,0:T(8,128)(2,1)}, bf16[32,128,128]{2,1,0:T(8,128)(2,1)}, bf16[2,2,32,1024]{3,2,1,0:T(8,128)(2,1)}) custom-call(s32[32]{0:T(128)} %span_ref.5, bf16[8,128,128]{2,1,0:T(8,128)(2,1)} %get-tuple-element.60.q_ref, bf16[32,128,128]{2,1,0:T(8,128)(2,1)} %bitcast.18, bf16[8,128,128]{2,1,0:T(8,128)(2,1)} %get-tuple-element.62.att_ref.out_ref, ...), custom_call_target="tpu_custom_call" | custom-call | flops 5368709120 | bytes 8388608 | tf_op jit(solution)/shard_map/pallas_call | solution.py:1197
  215.4 0.0 collective-permute-done.3.refs_1_
  215.4 0.0 copy-start
  215.4 0.0 collective-permute-done.4.refs_2_
  215.4 0.0 copy-start.1
  215.4 0.0 collective-permute-done.5.refs_3_
  215.4 0.0 copy-start.2
  215.4 0.8 copy-done
  216.2 0.2 copy-done.1
  216.4 0.2 copy-done.2
  216.6 71.8 %shard_map.226 = (bf16[128,1024]{1,0:T(8,128)(2,1)}, f32[32,1024]{1,0:T(8,128)}, bf16[128,1024]{1,0:T(8,128)(2,1)}, f32[8,32,256]{2,1,0:T(8,128)}, bf16[8,32,115...) custom-call(bf16[8,128,128]{2,1,0:T(8,128)(2,1)} %get-tuple-element.73.dq_ref, ...), custom_call_target="tpu_custom_call" | custom-call | tf_op jit(solution)/shard_map/pallas_call | solution.py:499
  288.4 3.4 %shard_map.227 = (bf16[128,1024]{1,0:T(8,128)(2,1)}, bf16[128,1024]{1,0:T(8,128)(2,1)}, f32[32,1024]{1,0:T(8,128)}, f32[144,1024]{1,0:T(8,128)}, f32[1,32]{1,0:T...) custom-call(f32[8,32,256]{2,1,0:T(8,128)} %get-tuple-element.89.ws_r, ...), custom_call_target="tpu_custom_call" | custom-call | flops 1048576 | bytes 8388608 | tf_op jit(solution)/shard_map/pallas_call | solution.py:1197
  (1 shorter events, 0.0 us)
Async XLA Ops:
  77.3 50.4 %collective-permute-start.2 = (bf16[4,64,1152]{2,1,0:T(8,128)(2,1)}, bf16[4,64,1152]{2,1,0:T(8,128)(2,1)S(1)}, u32[]{:S(2)}, u32[]{:S(2)}) collective-permute-start(bf16[4,64,1152]{2,1,0:T(8,128)(2,1)} %bitcast.19), channel_id=1, source_target_pairs={{0,6},{1,7},{2,0},{3,1},{4,2},{5,3},{6,4},{7,5},{8,14},{9,15},{10,... | collective-permute-start | bytes 1769480 | tf_op jit(solution)/shard_map/ppermute | solution.py:1248
  79.9 49.7 %collective-permute-start.1 = (bf16[4,64,1152]{2,1,0:T(8,128)(2,1)}, bf16[4,64,1152]{2,1,0:T(8,128)(2,1)S(1)}, u32[]{:S(2)}, u32[]{:S(2)}) collective-permute-start(bf16[4,64,1152]{2,1,0:T(8,128)(2,1)} %bitcast.20), channel_id=1, source_target_pairs={{0,4},{1,5},{2,6},{3,7},{4,0},{5,1},{6,2},{7,3},{8,12},{9,13},{10,... | collective-permute-start | bytes 1769480 | tf_op jit(solution)/shard_map/ppermute | solution.py:1248
  79.9 49.7 %collective-permute-start = (bf16[4,64,1152]{2,1,0:T(8,128)(2,1)}, bf16[4,64,1152]{2,1,0:T(8,128)(2,1)S(1)}, u32[]{:S(2)}, u32[]{:S(2)}) collective-permute-start(bf16[4,64,1152]{2,1,0:T(8,128)(2,1)} %bitcast.21), channel_id=1, source_target_pairs={{0,2},{1,3},{2,4},{3,5},{4,6},{5,7},{6,0},{7,1},{8,10},{9,11},{10,... | collective-permute-start | bytes 1769480 | tf_op jit(solution)/shard_map/ppermute | solution.py:1248
  127.7 1.9 copy-start.3
  129.6 0.8 copy-start.4
  129.6 1.0 copy-start.5
  150.2 65.1 %collective-permute-start.3 = (bf16[8,32,1152]{2,1,0:T(8,128)(2,1)}, bf16[8,32,1152]{2,1,0:T(8,128)(2,1)S(1)}, u32[]{:S(2)}, u32[]{:S(2)}) collective-permute-start(bf16[8,32,1152]{2,1,0:T(8,128)(2,1)} %get-tuple-element.86), channel_id=1, source_target_pairs={{0,2},{1,3},{2,4},{3,5},{4,6},{5,7},{6,0},{7,1},{8,10},{9,11},{10,... | collective-permute-start | bytes 1769480 | tf_op jit(solution)/shard_map/ppermute | solution.py:1350
  152.9 62.5 %collective-permute-start.4 = (bf16[8,32,1152]{2,1,0:T(8,128)(2,1)}, bf16[8,32,1152]{2,1,0:T(8,128)(2,1)S(1)}, u32[]{:S(2)}, u32[]{:S(2)}) collective-permute-start(bf16[8,32,1152]{2,1,0:T(8,128)(2,1)} %get-tuple-element.87), channel_id=1, source_target_pairs={{0,4},{1,5},{2,6},{3,7},{4,0},{5,1},{6,2},{7,3},{8,12},{9,13},{10,... | collective-permute-start | bytes 1769480 | tf_op jit(solution)/shard_map/ppermute | solution.py:1350
  153.7 61.7 %collective-permute-start.5 = (bf16[8,32,1152]{2,1,0:T(8,128)(2,1)}, bf16[8,32,1152]{2,1,0:T(8,128)(2,1)S(1)}, u32[]{:S(2)}, u32[]{:S(2)}) collective-permute-start(bf16[8,32,1152]{2,1,0:T(8,128)(2,1)} %get-tuple-element.88), channel_id=1, source_target_pairs={{0,6},{1,7},{2,0},{3,1},{4,2},{5,3},{6,4},{7,5},{8,14},{9,15},{10,... | collective-permute-start | bytes 1769480 | tf_op jit(solution)/shard_map/ppermute | solution.py:1350
  215.4 0.8 copy-start
  215.4 1.0 copy-start.1
  215.4 1.2 copy-start.2
